TPU v7x, 32 devices: a whole 2x2x4 slice. The times are simulated.
32 devices in a mesh: gx: 8 (over y, x, core), gy: 4 (over z).
Axes of the slice: x: 2, y: 2, z: 4, core: 2. Of those that a mesh axis runs over, the one named last changes fastest.
Arguments:
- products: bfloat16 [1536, 3, 2048], P('gy', None, 'gx'), may hold values from -6 to 6
- operator: bfloat16 [1536, 1536], P(None, 'gy'), may hold values from -0.21875 to 0.21875
Outputs:
- derivative: bfloat16 [1536, 3, 2048], P(('gy', 'gx'))
All inputs are finite; a program needn't handle non-finite values.
Results may differ from a plain program's by a relative error of at most 0.002.
Values may be sent and summed in bfloat16 or wider, within the bound.
No kernel may reach another device: no remote copies, remote signals or barrier semaphores. Data moves between devices by JAX's collectives and lax.ppermute only.
A program may use at most 64 MiB of HBM per device.

v0:
```python
import jax
import jax.numpy as jnp
from jax import lax
from jax.sharding import PartitionSpec as P


def body(products, operator):
    y_local, three, m_local = products.shape
    flat = products.reshape(y_local, three * m_local)
    summed = lax.psum_scatter(
        jnp.dot(operator, flat, preferred_element_type=jnp.float32),
        "gy",
        scatter_dimension=0,
        tiled=True,
    )
    result = summed.astype(jnp.bfloat16).reshape(y_local, three, m_local)
    return lax.all_to_all(result, "gx", split_axis=0, concat_axis=2, tiled=True)


def solution(mesh):
    return jax.shard_map(
        body,
        mesh=mesh,
        in_specs=(P("gy", None, "gx"), P(None, "gy")),
        out_specs=P(("gy", "gx"), None, None),
        check_vma=False,
    )
```

profile of v0, /device:TPU:0, one launch (start us, length us, event | category | flops | bytes accessed | tf_op | source)
XLA Modules:
  0.0 125.9 jit_solution(14700882482431408080)
XLA Ops:
  6.5 0.0 copy-start
  6.5 0.0 reduce-scatter.2.cloned.1.call-start
  6.5 1.5 %copy.14 = bf16[384,3,256]{0,2,1:T(8,128)(2,1)S(1)} copy(bf16[384,3,256]{2,0,1:T(8,128)(2,1)} %param.2) | data formatting | bytes 1179648 | tf_op args[0]
  8.0 0.0 copy-done
  8.0 3.5 %fusion = f32[1536,768]{1,0:T(8,128)} fusion(bf16[1536,384]{1,0:T(8,128)(2,1)S(1)} %copy-done, bf16[384,768]{0,1:T(8,128)(2,1)S(1)} %bitcast.9), kind=kOutput, calls=%fused_computation | convolution fusion | flops 905969664 | bytes 6488064 | tf_op jit(solution)/shard_map/dot_general | solution.py:11
  11.5 0.0 reduce-scatter.2.cloned.1.call-update
  11.6 88.2 %reduce-scatter.2.cloned.1.call-done = f32[384,768]{1,0:T(8,128)} async-done(((f32[1536,768]{1,0:T(8,128)}), f32[384,768]{1,0:T(8,128)}) %reduce-scatter.2.cloned.1.call-update) | async-done | bytes 1179664 | tf_op jit(solution)/shard_map/reduce_scatter | solution.py:10
  99.7 1.3 %convert_element_type.3 = bf16[384,768]{1,0:T(8,128)(2,1)S(1)} convert(f32[384,768]{1,0:T(8,128)} %reduce-scatter.2.cloned.1.call-done) | non-fusion elementwise | flops 294912 | bytes 1769472 | tf_op jit(solution)/shard_map/convert_element_type | solution.py:16
  101.1 0.3 copy.15
  101.4 0.8 copy.16
  102.2 16.0 %all_to_all.18 = bf16[384,3,256]{2,1,0:T(4,128)(2,1)S(1)} all-to-all(bf16[384,3,256]{2,1,0:T(4,128)(2,1)S(1)} %copy.16), channel_id=1, replica_groups=mesh['gx'=8,'gy'=4] {'gx'}, dimensions={0} | all-to-all | bytes 1179648 | tf_op jit(solution)/shard_map/all_to_all | solution.py:17
  118.1 0.1 copy.17
  118.2 0.9 copy.19
Async XLA Ops:
  6.5 1.5 %copy-start = (bf16[1536,384]{1,0:T(8,128)(2,1)S(1)}, bf16[1536,384]{1,0:T(8,128)(2,1)}, u32[]{:S(2)}) copy-start(bf16[1536,384]{1,0:T(8,128)(2,1)} %param.3) | copy-start | bytes 3538948
  6.5 93.2 %reduce-scatter.2.cloned.1.call-start = ((), (), s32[]{:S(2)}) async-start(), calls=%async_computation.2 | async-start | bytes 5898240 | tf_op jit(solution)/shard_map/reduce_scatter | solution.py:10
Sparse Core Ops, SparseCore 0:
  11.7 88.0 reduce-scatter.1
where the time goes:
time: 126 us
  waiting for transfers between devices  88.2 us (70%)
  blocking collectives  16 us (13%)
  between operations  13.4 us (11%)
  matrix products  3.53 us (3%)
  local copies, waits for them, and re-layouts  3.49 us (3%)
  other arithmetic  1.33 us (1%)
    reduce_scatter x1, waiting for transfers between devices, body(): lax.psum_scatter(jnp.dot(operator, flat, preferred_element_type=jnp.float...  88.2 us
    all_to_all x1, blocking collectives, body(): return lax.all_to_all(result, 'gx', split_axis=0, concat_axis=2, tiled=True)  16 us
    dot_general x1, matrix products, body(): jnp.dot(operator, flat, preferred_element_type=jnp.float32)  3.53 us
  transfers between devices with their start and end apart: 1, of which 1 were waited for; matrix products, arithmetic and copies ran while one was open for 0% of the time, Pallas kernels for 0%

commit v1 on v0

v1 whole, which is shorter than its diff:
```python
import jax
import jax.numpy as jnp
from jax import lax
from jax.experimental import pallas as pl
from jax.experimental.pallas import tpu as pltpu
from jax.sharding import PartitionSpec as P


def hop(index, step, size):
    return index ^ step if size & (size - 1) == 0 else (index + step) % size


def back(index, step, size):
    return index ^ step if size & (size - 1) == 0 else (index - step + size) % size


def assemble(first, place, *refs):
    *parts, _, out, whole, sem = refs
    comps, _, width = whole.shape
    half = width // (2 * len(parts))
    for number, part in enumerate(parts):
        for other in range(2):
            start = pl.multiple_of(place[2 * number + other] * half, half)
            for comp in range(comps):
                column = (other * comps + comp) * half
                whole[comp, :, pl.ds(start, half)] = part[:, column : column + half]
    copy = pltpu.make_async_copy(whole, out.at[pl.ds(first, comps)], sem)
    copy.start()
    copy.wait()


def assemble_first(first, place, *refs):
    assemble(first, place, *refs[:-3], None, *refs[-3:])


def write_out(spots, parts, first, comps, shape, earlier):
    rows = parts[0].shape[0]
    smem, vmem, anywhere = (pl.BlockSpec(memory_space=m) for m in (pltpu.SMEM, pltpu.VMEM, pl.ANY))
    given = [] if earlier is None else [earlier]
    kernel = assemble if given else assemble_first
    return pl.pallas_call(
        lambda *refs: kernel(first, *refs),
        out_shape=jax.ShapeDtypeStruct(shape, jnp.bfloat16),
        in_specs=[smem] + [vmem] * len(parts) + [anywhere] * len(given),
        out_specs=anywhere,
        scratch_shapes=[pltpu.VMEM((comps, rows, shape[2]), jnp.bfloat16), pltpu.SemaphoreType.DMA],
        input_output_aliases={1 + len(parts): 0} if given else {},
        compiler_params=pltpu.CompilerParams(vmem_limit_bytes=8 << 20),
    )(spots, *parts, *given)


def direct(products, operator):
    points, comps, modes = products.shape
    flat = products.reshape(points, comps * modes)
    partial = jnp.dot(operator, flat, preferred_element_type=jnp.float32)
    summed = lax.psum_scatter(partial, "gy", scatter_dimension=0, tiled=True)
    result = summed.astype(jnp.bfloat16).reshape(points, comps, modes)
    return lax.all_to_all(result, "gx", split_axis=0, concat_axis=2, tiled=True)


def arrival_order(deep):
    return [0] + [k for k in list(range(deep - 1, 2, -1)) + [1, 2] if k < deep]


def paired(wide, deep, products, operator):
    points, comps, modes = products.shape
    chips, half = wide // 2, modes // 2
    piece = points // chips
    rows = piece // 2
    x, z = lax.axis_index("gx"), lax.axis_index("gy")
    chip, core, q = x // 2, x % 2, z % 2
    swap = [(i, i ^ 1) for i in range(wide)]
    order = arrival_order(deep)
    groups = [(0, half // 2), (half // 2, comps * half)]
    chunks = [(0, comps, [0, 1])]

    pieces = {
        k: lax.dynamic_slice_in_dim(operator, ((z ^ k) ^ core) * points + chip * piece, piece, 0) for k in order[1:]
    }
    products, pieces = lax.optimization_barrier((products, pieces))

    halves = [
        lax.dynamic_slice_in_dim(products, (q ^ odd) * half, half, 2).reshape(points, -1).T for odd in range(2)
    ]
    mine = []
    shares = {}
    for g, (a, b) in enumerate(groups):
        mine.append({0: halves[0][a:b]})
        for k in order[1:]:
            message = halves[k % 2][a:b]
            if g == 0:
                message = jnp.concatenate([pieces[k], message])
            message = lax.ppermute(message, "gy", [(i, i ^ k) for i in range(deep)])
            if g == 0:
                shares[k], message = message[:piece], message[piece:]
            mine[g][k] = message

    arrived = jnp.concatenate([shares[k] for k in range(1, deep)])
    gathered = [arrived]
    for j in range(1, chips):
        pairs = [(i, 2 * hop(i // 2, j, chips) + i % 2) for i in range(wide)]
        gathered.append(lax.ppermute(arrived, "gx", pairs))
    block = lax.dynamic_slice_in_dim(operator, (z ^ core) * points, points, 0)
    block = lax.optimization_barrier((block, arrived))[0]
    own = [lax.dynamic_slice_in_dim(block, back(chip, j, chips) * piece, piece, 0) for j in range(chips)]
    weights = [jnp.concatenate(own)]
    for k in range(deep - 1):
        weights.append(jnp.concatenate([g[k * piece : k * piece + piece] for g in gathered]))

    out = None
    for first, end, members in chunks:
        total = None
        for k in order:
            ours = jnp.concatenate([mine[g][k] for g in members])
            theirs = lax.ppermute(ours, "gx", swap)
            both = jnp.concatenate([ours, theirs])
            term = lax.dot_general(
                weights[k], both, (((1,), (1,)), ((), ())), preferred_element_type=jnp.float32
            )
            total = term if total is None else lax.optimization_barrier(total) + term
        result = total.astype(jnp.bfloat16).reshape(chips, piece, -1)

        kept, passed, places = [], [], []
        for j in list(range(1, chips)) + [0]:
            pairs = []
            for i in range(wide):
                for y in range(deep):
                    pairs.append((i * deep + y, (2 * back(i // 2, j, chips) + i % 2) * deep + (y ^ (i % 2))))
            landed = lax.ppermute(result[j], ("gx", "gy"), pairs)
            kept.append(lax.dynamic_slice_in_dim(landed, core * rows, rows, 0))
            passed.append(lax.dynamic_slice_in_dim(landed, (1 - core) * rows, rows, 0))
            places.append(hop(chip, j, chips))
        fetched = lax.ppermute(jnp.stack(passed), "gx", swap)
        spots = [
            (place * 2 + (core ^ via ^ e)) * 2 + (q ^ core ^ via)
            for via in range(2)
            for place in places
            for e in range(2)
        ]
        parts = kept + [fetched[i] for i in range(chips)]
        out = write_out(jnp.stack(spots).astype(jnp.int32), parts, first, end - first, (comps, rows, wide * modes), out)
    return out.transpose(1, 0, 2)


def solution(mesh):
    wide, deep = mesh.shape["gx"], mesh.shape["gy"]
    even = wide % 2 == 0 and deep > 1 and deep & (deep - 1) == 0

    def body(products, operator):
        if not even:
            return direct(products, operator)
        return paired(wide, deep, products, operator)

    return jax.shard_map(
        body,
        mesh=mesh,
        in_specs=(P("gy", None, "gx"), P(None, "gy")),
        out_specs=P(("gy", "gx"), None, None),
        check_vma=False,
    )
```

time: 126 us -> 57.5 us (0.46)
  waiting for transfers between devices: 88.2 us -> 25.5 us
  starting transfers between devices: 0.01 us -> 23.4 us
  blocking collectives: 16 us -> 0 us
  between operations: 13.4 us -> 0.42 us
  matrix products: 3.53 us -> 1.97 us
  Pallas kernels: 0 us -> 1.52 us
    reduce_scatter x1 -> x0, waiting for transfers between devices: 88.2 us -> none  [body(): lax.psum_scatter(jnp.dot(operator, flat, preferred_element_type=jnp.float...]
    ppermute x0 -> x18, waiting for transfers between devices: none -> 25.5 us  [the longest x6 16.5 us: paired(): message = lax.ppermute(message, 'gy', [(i, i ^ k) for i in range(deep)])]
    ppermute x0 -> x18, starting transfers between devices: none -> 23.4 us  [the longest x6 13.9 us: paired(): message = lax.ppermute(message, 'gy', [(i, i ^ k) for i in range(deep)])]
    all_to_all x1 -> x0, blocking collectives: 16 us -> none  [body(): return lax.all_to_all(result, 'gx', split_axis=0, concat_axis=2, tiled=True)]
    dynamic_slice x0 -> x6, local copies, waits for them, and re-layouts: none -> 3.54 us  [the longest x3 1.53 us: paired(): lax.dynamic_slice_in_dim(products, (q ^ odd) * half, half, 2)]
    dot_general x1 -> x4, matrix products: 3.53 us -> 1.97 us  [paired(): lax.dot_general(weights[k], both, (((1,), (1,)), ((), ())), preferred_ele...]
    pallas_call x0 -> x1, Pallas kernels: none -> 1.52 us  [write_out(): pl.pallas_call(lambda *refs: kernel(first, *refs), out_shape=jax.ShapeDty...]
    unnamed x3 -> x0, local copies, waits for them, and re-layouts: 1.47 us -> none
  transfers between devices with their start and end apart: 1 -> 18, of which waited for: 1 -> 7; matrix products, arithmetic and copies ran while one was open for 0% -> 6% of each run, Pallas kernels for 0% -> 0%
where the time goes in v1:
time: 57.5 us; the launch traced here: 57.3 us
  waiting for transfers between devices  25.5 us (44%)
  starting transfers between devices  23.4 us (41%)
  local copies, waits for them, and re-layouts  3.94 us (7%)
  matrix products  1.97 us (3%)
  Pallas kernels  1.52 us (3%)
  other arithmetic  0.63 us (1%)
    ppermute x6, waiting for transfers between devices, paired(): message = lax.ppermute(message, 'gy', [(i, i ^ k) for i in range(deep)])  16.5 us
    ppermute x6, starting transfers between devices, paired(): message = lax.ppermute(message, 'gy', [(i, i ^ k) for i in range(deep)])  13.9 us
    ppermute x4, waiting for transfers between devices, paired(): landed = lax.ppermute(result[j], ('gx', 'gy'), pairs)  7.21 us
    ppermute x3, starting transfers between devices, paired(): gathered.append(lax.ppermute(arrived, 'gx', pairs))  4.54 us
    ppermute x4, starting transfers between devices, paired(): landed = lax.ppermute(result[j], ('gx', 'gy'), pairs)  4.21 us
    dot_general x4, matrix products, paired(): lax.dot_general(weights[k], both, (((1,), (1,)), ((), ())), preferred_ele...  1.97 us
    dynamic_slice x3, local copies, waits for them, and re-layouts, paired(): lax.dynamic_slice_in_dim(products, (q ^ odd) * half, half, 2)  1.53 us
    pallas_call x1, Pallas kernels, write_out(): pl.pallas_call(lambda *refs: kernel(first, *refs), out_shape=jax.ShapeDty...  1.52 us
  transfers between devices with their start and end apart: 18, of which 7 were waited for; matrix products, arithmetic and copies ran while one was open for 6% of the time, Pallas kernels for 0%

profile of v1, /device:TPU:0, one launch (start us, length us, event | category | flops | bytes accessed | tf_op | source)
XLA Modules:
  0.0 57.3 jit_solution(1716863446436807650)
XLA Ops:
  0.0 1.0 %constant_dynamic-slice_fusion.10 = (bf16[96,384]{1,0:T(8,128)(2,1)S(1)}, bf16[96,384]{1,0:T(8,128)(2,1)S(1)}, bf16[96,384]{1,0:T(8,128)(2,1)S(1)}) fusion(bf16[1536,384]{1,0:T(8,128)(2,1)} %param.3, s32[]{:T(128)S(6)} %select_n.63, s32[]{:T(128)S(6)} %select_n.61, s32[]{:T(128)S(6)} %select_n.62), kind=kLoop, calls=%fused_computation.77 | loop fusion | bytes 442380 | tf_op jit(solution)/shard_map/dynamic_slice | solution.py:78
  1.0 1.1 %constant_dynamic-slice_fusion.9 = (bf16[384,3,128]{2,0,1:T(8,128)(2,1)S(1)}, bf16[384,3,128]{2,0,1:T(8,128)(2,1)S(1)}) fusion(bf16[384,3,256]{2,0,1:T(8,128)(2,1)} %param.2, s32[]{:T(128)S(6)} %select_n.64, s32[]{:T(128)S(6)} %select_n.65), kind=kLoop, calls=%fused_computation.76 | loop fusion | bytes 1179656 | tf_op jit(solution)/shard_map/dynamic_slice | solution.py:83
  2.1 0.2 copy.3
  2.4 5.1 %collective-permute-start.2 = (bf16[160,384]{1,0:T(8,128)(2,1)S(1)}, bf16[160,384]{1,0:T(8,128)(2,1)S(1)}, u32[]{:S(2)}, u32[]{:S(2)}) collective-permute-start(bf16[160,384]{1,0:T(8,128)(2,1)S(1)} %get-tuple-element.50), channel_id=1, source_target_pairs={{0,3},{1,2},{2,1},{3,0},{4,7},{5,6},{6,5},{7,4},{8,11},{9,10},{10,... | collective-permute-start | bytes 368648 | tf_op jit(solution)/shard_map/ppermute | solution.py:93
  7.5 0.2 copy.4
  7.8 0.1 collective-permute-start.1
  7.8 0.6 collective-permute-start
  8.4 0.0 collective-permute-start.3
  8.4 3.9 %collective-permute-start.7 = (bf16[320,384]{1,0:T(8,128)(2,1)S(1)}, bf16[320,384]{1,0:T(8,128)(2,1)S(1)}, u32[]{:S(2)}, u32[]{:S(2)}) collective-permute-start(bf16[320,384]{1,0:T(8,128)(2,1)S(1)} %slice.127), channel_id=1, source_target_pairs={{0,3},{1,2},{2,1},{3,0},{4,7},{5,6},{6,5},{7,4},{8,11},{9,10},{10,... | collective-permute-start | bytes 737288 | tf_op jit(solution)/shard_map/ppermute | solution.py:93
  12.3 1.0 %constant_dynamic-slice_fusion.13 = bf16[384,384]{1,0:T(8,128)(2,1)S(1)} fusion(bf16[1536,384]{1,0:T(8,128)(2,1)} %param.3, s32[]{:T(128)S(6)} %select_n.60), kind=kLoop, calls=%fused_computation.80 | loop fusion | bytes 589828 | tf_op jit(solution)/shard_map/dynamic_slice | solution.py:103
  13.4 0.0 collective-permute-done.2
  13.4 4.2 %collective-permute-start.9 = (bf16[320,384]{1,0:T(8,128)(2,1)S(1)}, bf16[320,384]{1,0:T(8,128)(2,1)S(1)}, u32[]{:S(2)}, u32[]{:S(2)}) collective-permute-start(bf16[320,384]{1,0:T(8,128)(2,1)S(1)} %slice.127), channel_id=1, source_target_pairs={{0,1},{1,0},{2,3},{3,2},{4,5},{5,4},{6,7},{7,6},{8,9},{9,8},{10,11... | collective-permute-start | bytes 737288 | tf_op jit(solution)/shard_map/ppermute | solution.py:93
  17.6 6.5 %collective-permute-done.1 = bf16[160,384]{1,0:T(8,128)(2,1)S(1)} collective-permute-done((bf16[160,384]{1,0:T(8,128)(2,1)S(1)}, bf16[160,384]{1,0:T(8,128)(2,1)S(1)}, u32[]{:S(2)}, u32[]{:S(2)}) %collective-permute-start.1) | collective-permute-done | bytes 122912 | tf_op jit(solution)/shard_map/ppermute | solution.py:93
  24.1 0.0 collective-permute-start.11
  24.1 0.0 collective-permute-done
  24.2 2.5 %collective-permute-start.6 = (bf16[288,384]{1,0:T(8,128)(2,1)S(1)}, bf16[288,384]{1,0:T(8,128)(2,1)S(1)}, u32[]{:S(2)}, u32[]{:S(2)}) collective-permute-start(bf16[288,384]{1,0:T(8,128)(2,1)S(1)} %pad_maximum_fusion.4), channel_id=1, source_target_pairs={{0,24},{4,28},{8,16},{12,20},{16,8},{20,12},{24,0},{28,4},{1,25},{... | collective-permute-start | bytes 663560 | tf_op jit(solution)/shard_map/ppermute | solution.py:102
  26.8 0.0 collective-permute-done.7
  26.8 0.6 collective-permute-start.5
  27.4 0.8 %collective-permute-done.9 = bf16[320,384]{1,0:T(8,128)(2,1)S(1)} collective-permute-done((bf16[320,384]{1,0:T(8,128)(2,1)S(1)}, bf16[320,384]{1,0:T(8,128)(2,1)S(1)}, u32[]{:S(2)}, u32[]{:S(2)}) %collective-permute-start.9) | collective-permute-done | bytes 245792 | tf_op jit(solution)/shard_map/ppermute | solution.py:93
  28.2 1.5 %collective-permute-start.4 = (bf16[288,384]{1,0:T(8,128)(2,1)S(1)}, bf16[288,384]{1,0:T(8,128)(2,1)S(1)}, u32[]{:S(2)}, u32[]{:S(2)}) collective-permute-start(bf16[288,384]{1,0:T(8,128)(2,1)S(1)} %pad_maximum_fusion.4), channel_id=1, source_target_pairs={{0,8},{4,12},{8,0},{12,4},{16,24},{20,28},{24,16},{28,20},{1,9},{5... | collective-permute-start | bytes 663560 | tf_op jit(solution)/shard_map/ppermute | solution.py:102
  29.7 9.3 %collective-permute-done.11 = bf16[320,384]{1,0:T(8,128)(2,1)S(1)} collective-permute-done((bf16[320,384]{1,0:T(8,128)(2,1)S(1)}, bf16[320,384]{1,0:T(8,128)(2,1)S(1)}, u32[]{:S(2)}, u32[]{:S(2)}) %collective-permute-start.11) | collective-permute-done | bytes 245792 | tf_op jit(solution)/shard_map/ppermute | solution.py:93
  38.9 0.0 collective-permute-start.8
  39.0 0.0 collective-permute-done.3
  39.0 0.6 collective-permute-start.10
  39.6 0.5 fusion
  40.1 0.0 collective-permute-done.6
  40.1 0.1 collective-permute-start.12
  40.2 0.0 collective-permute-done.4
  40.3 0.3 collective-permute-done.8
  40.5 0.5 fusion.4
  41.0 0.1 add.199
  41.2 0.0 collective-permute-done.10
  41.2 0.5 fusion.10
  41.7 0.1 add.200
  41.8 0.0 collective-permute-done.12
  41.8 0.5 fusion.16
  42.3 0.1 add_convert_fusion
  42.5 1.6 %collective-permute-start.13 = (bf16[96,768]{1,0:T(8,128)(2,1)S(1)}, bf16[96,768]{1,0:T(8,128)(2,1)S(1)}, u32[]{:S(2)}, u32[]{:S(2)}) collective-permute-start(bf16[96,768]{1,0:T(8,128)(2,1)S(1)} %get-tuple-element.21), channel_id=1, source_target_pairs={{0,8},{1,9},{2,10},{3,11},{4,13},{5,12},{6,15},{7,14},{8,0},{9,1},... | collective-permute-start | bytes 442376 | tf_op jit(solution)/shard_map/ppermute | solution.py:129
  44.1 1.5 %collective-permute-start.14 = (bf16[96,768]{1,0:T(8,128)(2,1)S(1)}, bf16[96,768]{1,0:T(8,128)(2,1)S(1)}, u32[]{:S(2)}, u32[]{:S(2)}) collective-permute-start(bf16[96,768]{1,0:T(8,128)(2,1)S(1)} %get-tuple-element.20), channel_id=1, source_target_pairs={{0,16},{1,17},{2,18},{3,19},{4,21},{5,20},{6,23},{7,22},{8,24},{9,... | collective-permute-start | bytes 442376 | tf_op jit(solution)/shard_map/ppermute | solution.py:129
  45.6 0.5 collective-permute-start.15
  46.1 0.7 %collective-permute-start.16 = (bf16[96,768]{1,0:T(8,128)(2,1)S(1)}, bf16[96,768]{1,0:T(8,128)(2,1)S(1)}, u32[]{:S(2)}, u32[]{:S(2)}) collective-permute-start(bf16[96,768]{1,0:T(8,128)(2,1)S(1)} %get-tuple-element.18), channel_id=1, source_target_pairs={{0,0},{1,1},{2,2},{3,3},{4,5},{5,4},{6,7},{7,6},{8,8},{9,9},{10,10... | collective-permute-start | bytes 442376 | tf_op jit(solution)/shard_map/ppermute | solution.py:129
  46.8 2.6 %collective-permute-done.13 = bf16[96,768]{1,0:T(8,128)(2,1)S(1)} collective-permute-done((bf16[96,768]{1,0:T(8,128)(2,1)S(1)}, bf16[96,768]{1,0:T(8,128)(2,1)S(1)}, u32[]{:S(2)}, u32[]{:S(2)}) %collective-permute-start.13) | collective-permute-done | bytes 147488 | tf_op jit(solution)/shard_map/ppermute | solution.py:129
  49.3 4.6 %collective-permute-done.14 = bf16[96,768]{1,0:T(8,128)(2,1)S(1)} collective-permute-done((bf16[96,768]{1,0:T(8,128)(2,1)S(1)}, bf16[96,768]{1,0:T(8,128)(2,1)S(1)}, u32[]{:S(2)}, u32[]{:S(2)}) %collective-permute-start.14) | collective-permute-done | bytes 147488 | tf_op jit(solution)/shard_map/ppermute | solution.py:129
  54.0 0.0 collective-permute-done.16
  54.1 0.1 collective-permute-start.17
  54.2 0.1 stack.82.refs_0_
  54.3 1.4 %collective-permute-done.17 = bf16[4,48,768]{2,1,0:T(8,128)(2,1)S(1)} collective-permute-done((bf16[4,48,768]{2,1,0:T(8,128)(2,1)S(1)}, bf16[4,48,768]{2,1,0:T(8,128)(2,1)S(1)}, u32[]{:S(2)}, u32[]{:S(2)}) %collective-permute-start.17) | collective-permute-done | bytes 294944 | tf_op jit(solution)/shard_map/ppermute | solution.py:133
  55.8 1.5 %shard_map.28 = bf16[3,48,2048]{2,1,0:T(8,128)(2,1)} custom-call(s32[16]{0:T(128)S(1)} %stack.82.refs_0_, bf16[48,768]{1,0:T(8,128)(2,1)S(1)} %get-tuple-element.42.refs_1_, bf16[48,768]{1,0:T(8,128)(2,1)S(1)} %get-tuple-element.44.refs_2_, bf16[48,768]{1,0:T(8,128)(2,1)S(1)} %get-tuple-element.46.refs_3_, bf16[48,768]{1,0:T(8,128)(2,1)S(1)} %get-tuple-element.48.refs_4_, ...), custom_call_target="tpu_custom_call" | custom-call | tf_op jit(solution)/shard_map/pallas_call | solution.py:41
  (29 shorter events, 0.6 us)
Async XLA Ops:
  2.4 11.0 %collective-permute-start.2 = (bf16[160,384]{1,0:T(8,128)(2,1)S(1)}, bf16[160,384]{1,0:T(8,128)(2,1)S(1)}, u32[]{:S(2)}, u32[]{:S(2)}) collective-permute-start(bf16[160,384]{1,0:T(8,128)(2,1)S(1)} %get-tuple-element.50), channel_id=1, source_target_pairs={{0,3},{1,2},{2,1},{3,0},{4,7},{5,6},{6,5},{7,4},{8,11},{9,10},{10,... | collective-permute-start | bytes 368648 | tf_op jit(solution)/shard_map/ppermute | solution.py:93
  7.8 16.3 %collective-permute-start.1 = (bf16[160,384]{1,0:T(8,128)(2,1)S(1)}, bf16[160,384]{1,0:T(8,128)(2,1)S(1)}, u32[]{:S(2)}, u32[]{:S(2)}) collective-permute-start(bf16[160,384]{1,0:T(8,128)(2,1)S(1)} %pad_maximum_fusion.7), channel_id=1, source_target_pairs={{0,2},{1,3},{2,0},{3,1},{4,6},{5,7},{6,4},{7,5},{8,10},{9,11},{10,... | collective-permute-start | bytes 368648 | tf_op jit(solution)/shard_map/ppermute | solution.py:93
  7.8 16.3 %collective-permute-start = (bf16[160,384]{1,0:T(8,128)(2,1)S(1)}, bf16[160,384]{1,0:T(8,128)(2,1)S(1)}, u32[]{:S(2)}, u32[]{:S(2)}) collective-permute-start(bf16[160,384]{1,0:T(8,128)(2,1)S(1)} %get-tuple-element.49), channel_id=1, source_target_pairs={{0,1},{1,0},{2,3},{3,2},{4,5},{5,4},{6,7},{7,6},{8,9},{9,8},{10,11... | collective-permute-start | bytes 368648 | tf_op jit(solution)/shard_map/ppermute | solution.py:93
  8.4 30.6 %collective-permute-start.3 = (bf16[384,384]{1,0:T(8,128)(2,1)S(1)}, bf16[384,384]{1,0:T(8,128)(2,1)S(1)}, u32[]{:S(2)}, u32[]{:S(2)}) collective-permute-start(bf16[384,384]{1,0:T(8,128)(2,1)S(1)} %bitcast.40), channel_id=1, source_target_pairs={{0,4},{4,0},{8,12},{12,8},{16,20},{20,16},{24,28},{28,24},{1,5},{5... | collective-permute-start | bytes 884744 | tf_op jit(solution)/shard_map/ppermute | solution.py:115
  8.4 18.3 %collective-permute-start.7 = (bf16[320,384]{1,0:T(8,128)(2,1)S(1)}, bf16[320,384]{1,0:T(8,128)(2,1)S(1)}, u32[]{:S(2)}, u32[]{:S(2)}) collective-permute-start(bf16[320,384]{1,0:T(8,128)(2,1)S(1)} %slice.127), channel_id=1, source_target_pairs={{0,3},{1,2},{2,1},{3,0},{4,7},{5,6},{6,5},{7,4},{8,11},{9,10},{10,... | collective-permute-start | bytes 737288 | tf_op jit(solution)/shard_map/ppermute | solution.py:93
  13.4 14.8 %collective-permute-start.9 = (bf16[320,384]{1,0:T(8,128)(2,1)S(1)}, bf16[320,384]{1,0:T(8,128)(2,1)S(1)}, u32[]{:S(2)}, u32[]{:S(2)}) collective-permute-start(bf16[320,384]{1,0:T(8,128)(2,1)S(1)} %slice.127), channel_id=1, source_target_pairs={{0,1},{1,0},{2,3},{3,2},{4,5},{5,4},{6,7},{7,6},{8,9},{9,8},{10,11... | collective-permute-start | bytes 737288 | tf_op jit(solution)/shard_map/ppermute | solution.py:93
  24.1 14.9 %collective-permute-start.11 = (bf16[320,384]{1,0:T(8,128)(2,1)S(1)}, bf16[320,384]{1,0:T(8,128)(2,1)S(1)}, u32[]{:S(2)}, u32[]{:S(2)}) collective-permute-start(bf16[320,384]{1,0:T(8,128)(2,1)S(1)} %slice.136), channel_id=1, source_target_pairs={{0,2},{1,3},{2,0},{3,1},{4,6},{5,7},{6,4},{7,5},{8,10},{9,11},{10,... | collective-permute-start | bytes 737288 | tf_op jit(solution)/shard_map/ppermute | solution.py:93
  24.2 15.9 %collective-permute-start.6 = (bf16[288,384]{1,0:T(8,128)(2,1)S(1)}, bf16[288,384]{1,0:T(8,128)(2,1)S(1)}, u32[]{:S(2)}, u32[]{:S(2)}) collective-permute-start(bf16[288,384]{1,0:T(8,128)(2,1)S(1)} %pad_maximum_fusion.4), channel_id=1, source_target_pairs={{0,24},{4,28},{8,16},{12,20},{16,8},{20,12},{24,0},{28,4},{1,25},{... | collective-permute-start | bytes 663560 | tf_op jit(solution)/shard_map/ppermute | solution.py:102
  26.8 13.4 %collective-permute-start.5 = (bf16[288,384]{1,0:T(8,128)(2,1)S(1)}, bf16[288,384]{1,0:T(8,128)(2,1)S(1)}, u32[]{:S(2)}, u32[]{:S(2)}) collective-permute-start(bf16[288,384]{1,0:T(8,128)(2,1)S(1)} %pad_maximum_fusion.4), channel_id=1, source_target_pairs={{0,16},{4,20},{8,24},{12,28},{16,0},{20,4},{24,8},{28,12},{1,17},{... | collective-permute-start | bytes 663560 | tf_op jit(solution)/shard_map/ppermute | solution.py:102
  28.2 12.0 %collective-permute-start.4 = (bf16[288,384]{1,0:T(8,128)(2,1)S(1)}, bf16[288,384]{1,0:T(8,128)(2,1)S(1)}, u32[]{:S(2)}, u32[]{:S(2)}) collective-permute-start(bf16[288,384]{1,0:T(8,128)(2,1)S(1)} %pad_maximum_fusion.4), channel_id=1, source_target_pairs={{0,8},{4,12},{8,0},{12,4},{16,24},{20,28},{24,16},{28,20},{1,9},{5... | collective-permute-start | bytes 663560 | tf_op jit(solution)/shard_map/ppermute | solution.py:102
  38.9 1.6 %collective-permute-start.8 = (bf16[384,384]{1,0:T(8,128)(2,1)S(1)}, bf16[384,384]{1,0:T(8,128)(2,1)S(1)}, u32[]{:S(2)}, u32[]{:S(2)}) collective-permute-start(bf16[384,384]{1,0:T(8,128)(2,1)S(1)} %pad_maximum_fusion), channel_id=1, source_target_pairs={{0,4},{4,0},{8,12},{12,8},{16,20},{20,16},{24,28},{28,24},{1,5},{5... | collective-permute-start | bytes 884744 | tf_op jit(solution)/shard_map/ppermute | solution.py:115
  39.0 2.2 %collective-permute-start.10 = (bf16[384,384]{1,0:T(8,128)(2,1)S(1)}, bf16[384,384]{1,0:T(8,128)(2,1)S(1)}, u32[]{:S(2)}, u32[]{:S(2)}) collective-permute-start(bf16[384,384]{1,0:T(8,128)(2,1)S(1)} %pad_maximum_fusion.1), channel_id=1, source_target_pairs={{0,4},{4,0},{8,12},{12,8},{16,20},{20,16},{24,28},{28,24},{1,5},{5... | collective-permute-start | bytes 884744 | tf_op jit(solution)/shard_map/ppermute | solution.py:115
  40.1 1.8 %collective-permute-start.12 = (bf16[384,384]{1,0:T(8,128)(2,1)S(1)}, bf16[384,384]{1,0:T(8,128)(2,1)S(1)}, u32[]{:S(2)}, u32[]{:S(2)}) collective-permute-start(bf16[384,384]{1,0:T(8,128)(2,1)S(1)} %pad_maximum_fusion.2), channel_id=1, source_target_pairs={{0,4},{4,0},{8,12},{12,8},{16,20},{20,16},{24,28},{28,24},{1,5},{5... | collective-permute-start | bytes 884744 | tf_op jit(solution)/shard_map/ppermute | solution.py:115
  42.5 6.8 %collective-permute-start.13 = (bf16[96,768]{1,0:T(8,128)(2,1)S(1)}, bf16[96,768]{1,0:T(8,128)(2,1)S(1)}, u32[]{:S(2)}, u32[]{:S(2)}) collective-permute-start(bf16[96,768]{1,0:T(8,128)(2,1)S(1)} %get-tuple-element.21), channel_id=1, source_target_pairs={{0,8},{1,9},{2,10},{3,11},{4,13},{5,12},{6,15},{7,14},{8,0},{9,1},... | collective-permute-start | bytes 442376 | tf_op jit(solution)/shard_map/ppermute | solution.py:129
  44.1 9.9 %collective-permute-start.14 = (bf16[96,768]{1,0:T(8,128)(2,1)S(1)}, bf16[96,768]{1,0:T(8,128)(2,1)S(1)}, u32[]{:S(2)}, u32[]{:S(2)}) collective-permute-start(bf16[96,768]{1,0:T(8,128)(2,1)S(1)} %get-tuple-element.20), channel_id=1, source_target_pairs={{0,16},{1,17},{2,18},{3,19},{4,21},{5,20},{6,23},{7,22},{8,24},{9,... | collective-permute-start | bytes 442376 | tf_op jit(solution)/shard_map/ppermute | solution.py:129
  45.6 8.4 %collective-permute-start.15 = (bf16[96,768]{1,0:T(8,128)(2,1)S(1)}, bf16[96,768]{1,0:T(8,128)(2,1)S(1)}, u32[]{:S(2)}, u32[]{:S(2)}) collective-permute-start(bf16[96,768]{1,0:T(8,128)(2,1)S(1)} %get-tuple-element.19), channel_id=1, source_target_pairs={{0,24},{1,25},{2,26},{3,27},{4,29},{5,28},{6,31},{7,30},{8,16},{9,... | collective-permute-start | bytes 442376 | tf_op jit(solution)/shard_map/ppermute | solution.py:129
  46.1 7.9 %collective-permute-start.16 = (bf16[96,768]{1,0:T(8,128)(2,1)S(1)}, bf16[96,768]{1,0:T(8,128)(2,1)S(1)}, u32[]{:S(2)}, u32[]{:S(2)}) collective-permute-start(bf16[96,768]{1,0:T(8,128)(2,1)S(1)} %get-tuple-element.18), channel_id=1, source_target_pairs={{0,0},{1,1},{2,2},{3,3},{4,5},{5,4},{6,7},{7,6},{8,8},{9,9},{10,10... | collective-permute-start | bytes 442376 | tf_op jit(solution)/shard_map/ppermute | solution.py:129
  54.1 1.6 %collective-permute-start.17 = (bf16[4,48,768]{2,1,0:T(8,128)(2,1)S(1)}, bf16[4,48,768]{2,1,0:T(8,128)(2,1)S(1)}, u32[]{:S(2)}, u32[]{:S(2)}) collective-permute-start(bf16[4,48,768]{2,1,0:T(8,128)(2,1)S(1)} %pad_maximum_fusion.3), channel_id=1, source_target_pairs={{0,4},{4,0},{8,12},{12,8},{16,20},{20,16},{24,28},{28,24},{1,5},{5... | collective-permute-start | bytes 884744 | tf_op jit(solution)/shard_map/ppermute | solution.py:133

commit v2 on v1

--- a/solution.py
+++ b/solution.py
@@ -71,29 +71,24 @@
     chip, core, q = x // 2, x % 2, z % 2
     swap = [(i, i ^ 1) for i in range(wide)]
     order = arrival_order(deep)
-    groups = [(0, half // 2), (half // 2, comps * half)]
-    chunks = [(0, comps, [0, 1])]
+    groups = [(0, half), (half, comps * half)]
+    chunks = [(0, 1, [0]), (1, comps, [1])]
 
     pieces = {
         k: lax.dynamic_slice_in_dim(operator, ((z ^ k) ^ core) * points + chip * piece, piece, 0) for k in order[1:]
     }
-    products, pieces = lax.optimization_barrier((products, pieces))
+    shares = {}
+    for k in order[1:]:
+        shares[k] = lax.ppermute(pieces[k], "gy", [(i, i ^ k) for i in range(deep)])
 
     halves = [
         lax.dynamic_slice_in_dim(products, (q ^ odd) * half, half, 2).reshape(points, -1).T for odd in range(2)
     ]
     mine = []
-    shares = {}
     for g, (a, b) in enumerate(groups):
         mine.append({0: halves[0][a:b]})
         for k in order[1:]:
-            message = halves[k % 2][a:b]
-            if g == 0:
-                message = jnp.concatenate([pieces[k], message])
-            message = lax.ppermute(message, "gy", [(i, i ^ k) for i in range(deep)])
-            if g == 0:
-                shares[k], message = message[:piece], message[piece:]
-            mine[g][k] = message
+            mine[g][k] = lax.ppermute(halves[k % 2][a:b], "gy", [(i, i ^ k) for i in range(deep)])
 
     arrived = jnp.concatenate([shares[k] for k in range(1, deep)])
     gathered = [arrived]
@@ -121,7 +116,7 @@
         result = total.astype(jnp.bfloat16).reshape(chips, piece, -1)
 
         kept, passed, places = [], [], []
-        for j in list(range(1, chips)) + [0]:
+        for j in range(chips):
             pairs = []
             for i in range(wide):
                 for y in range(deep):

time: 57.5 us -> 75.6 us (1.31)
  starting transfers between devices: 23.4 us -> 35.5 us
  waiting for transfers between devices: 25.5 us -> 29.6 us
  Pallas kernels: 1.52 us -> 2.66 us
  matrix products: 1.97 us -> 2.75 us
    ppermute x3, waiting for transfers between devices: 0.01 us -> 13.2 us  [paired(): gathered.append(lax.ppermute(arrived, 'gx', pairs))]
    ppermute x6 -> x9, waiting for transfers between devices: 16.5 us -> 7.04 us  [the longest x6 3.87 us: paired(): lax.ppermute(halves[k % 2][a:b], 'gy', [(i, i ^ k) for i in range(deep)])]
    ppermute x4 -> x8, starting transfers between devices: 4.21 us -> 8.94 us  [paired(): landed = lax.ppermute(result[j], ('gx', 'gy'), pairs)]
    ppermute x1 -> x2, starting transfers between devices: 0.07 us -> 4.74 us  [paired(): fetched = lax.ppermute(jnp.stack(passed), 'gx', swap)]
    ppermute x4 -> x8, waiting for transfers between devices: 0.27 us -> 2.4 us  [paired(): theirs = lax.ppermute(ours, 'gx', swap)]
    ppermute x4 -> x8, starting transfers between devices: 0.67 us -> 2.29 us  [paired(): theirs = lax.ppermute(ours, 'gx', swap)]
    ppermute x1 -> x2, waiting for transfers between devices: 1.44 us -> 0.01 us  [paired(): fetched = lax.ppermute(jnp.stack(passed), 'gx', swap)]
    pallas_call x1 -> x2, Pallas kernels: 1.52 us -> 2.66 us  [write_out(): pl.pallas_call(lambda *refs: kernel(first, *refs), out_shape=jax.ShapeDty...]
  transfers between devices with their start and end apart: 18 -> 30, of which waited for: 7 -> 13; matrix products, arithmetic and copies ran while one was open for 6% -> 7% of each run, Pallas kernels for 0% -> 2%
where the time goes in v2:
time: 75.6 us; the launch traced here: 75.3 us
  starting transfers between devices  35.5 us (47%)
  waiting for transfers between devices  29.6 us (39%)
  local copies, waits for them, and re-layouts  3.97 us (5%)
  matrix products  2.75 us (4%)
  Pallas kernels  2.66 us (4%)
    ppermute x3, waiting for transfers between devices, paired(): gathered.append(lax.ppermute(arrived, 'gx', pairs))  13.2 us
    ppermute x6, starting transfers between devices, paired(): lax.ppermute(halves[k % 2][a:b], 'gy', [(i, i ^ k) for i in range(deep)])  9.52 us
    ppermute x8, starting transfers between devices, paired(): landed = lax.ppermute(result[j], ('gx', 'gy'), pairs)  8.94 us
    ppermute x8, waiting for transfers between devices, paired(): landed = lax.ppermute(result[j], ('gx', 'gy'), pairs)  6.94 us
    ppermute x3, starting transfers between devices, paired(): gathered.append(lax.ppermute(arrived, 'gx', pairs))  5.52 us
    ppermute x2, starting transfers between devices, paired(): fetched = lax.ppermute(jnp.stack(passed), 'gx', swap)  4.74 us
    ppermute x3, starting transfers between devices, paired(): shares[k] = lax.ppermute(pieces[k], 'gy', [(i, i ^ k) for i in range(deep)])  4.45 us
    ppermute x6, waiting for transfers between devices, paired(): lax.ppermute(halves[k % 2][a:b], 'gy', [(i, i ^ k) for i in range(deep)])  3.87 us
  transfers between devices with their start and end apart: 30, of which 13 were waited for; matrix products, arithmetic and copies ran while one was open for 7% of the time, Pallas kernels for 2%

profile of v2, /device:TPU:0, one launch (start us, length us, event | category | flops | bytes accessed | tf_op | source)
XLA Modules:
  0.0 75.3 jit_solution(16189173253581443285)
XLA Ops:
  0.0 1.1 %constant_dynamic-slice_fusion.8 = (bf16[384,3,128]{2,0,1:T(8,128)(2,1)S(1)}, bf16[384,3,128]{2,0,1:T(8,128)(2,1)S(1)}) fusion(bf16[384,3,256]{2,0,1:T(8,128)(2,1)} %param.2, s32[]{:T(128)S(6)} %select_n.77, s32[]{:T(128)S(6)} %select_n.76), kind=kLoop, calls=%fused_computation.67 | loop fusion | bytes 1179656 | tf_op jit(solution)/shard_map/dynamic_slice | solution.py:85
  1.1 0.2 copy.7
  1.3 3.1 %collective-permute-start.21 = (bf16[128,384]{1,0:T(8,128)(2,1)S(1)}, bf16[128,384]{1,0:T(8,128)(2,1)S(1)}, u32[]{:S(2)}, u32[]{:S(2)}) collective-permute-start(bf16[128,384]{1,0:T(8,128)(2,1)S(1)} %slice.148), channel_id=1, source_target_pairs={{0,1},{1,0},{2,3},{3,2},{4,5},{5,4},{6,7},{7,6},{8,9},{9,8},{10,11... | collective-permute-start | bytes 294920 | tf_op jit(solution)/shard_map/ppermute | solution.py:91
  4.4 2.5 %collective-permute-start.19 = (bf16[128,384]{1,0:T(8,128)(2,1)S(1)}, bf16[128,384]{1,0:T(8,128)(2,1)S(1)}, u32[]{:S(2)}, u32[]{:S(2)}) collective-permute-start(bf16[128,384]{1,0:T(8,128)(2,1)S(1)} %slice.148), channel_id=1, source_target_pairs={{0,3},{1,2},{2,1},{3,0},{4,7},{5,6},{6,5},{7,4},{8,11},{9,10},{10,... | collective-permute-start | bytes 294920 | tf_op jit(solution)/shard_map/ppermute | solution.py:91
  6.9 1.0 %constant_dynamic-slice_fusion.14 = (bf16[96,384]{1,0:T(8,128)(2,1)S(1)}, bf16[96,384]{1,0:T(8,128)(2,1)S(1)}, bf16[96,384]{1,0:T(8,128)(2,1)S(1)}) fusion(bf16[1536,384]{1,0:T(8,128)(2,1)} %param.3, s32[]{:T(128)S(6)} %select_n.71, s32[]{:T(128)S(6)} %select_n.69, s32[]{:T(128)S(6)} %select_n.70), kind=kLoop, calls=%fused_computation.73 | loop fusion | bytes 442380 | tf_op jit(solution)/shard_map/dynamic_slice | solution.py:78
  7.9 1.4 %collective-permute-start.2 = (bf16[96,384]{1,0:T(8,128)(2,1)S(1)}, bf16[96,384]{1,0:T(8,128)(2,1)S(1)}, u32[]{:S(2)}, u32[]{:S(2)}) collective-permute-start(bf16[96,384]{1,0:T(8,128)(2,1)S(1)} %get-tuple-element.7), channel_id=1, source_target_pairs={{0,3},{1,2},{2,1},{3,0},{4,7},{5,6},{6,5},{7,4},{8,11},{9,10},{10,... | collective-permute-start | bytes 221192 | tf_op jit(solution)/shard_map/ppermute | solution.py:82
  9.3 3.0 %collective-permute-start.1 = (bf16[96,384]{1,0:T(8,128)(2,1)S(1)}, bf16[96,384]{1,0:T(8,128)(2,1)S(1)}, u32[]{:S(2)}, u32[]{:S(2)}) collective-permute-start(bf16[96,384]{1,0:T(8,128)(2,1)S(1)} %get-tuple-element.9), channel_id=1, source_target_pairs={{0,2},{1,3},{2,0},{3,1},{4,6},{5,7},{6,4},{7,5},{8,10},{9,11},{10,... | collective-permute-start | bytes 221192 | tf_op jit(solution)/shard_map/ppermute | solution.py:82
  12.8 1.0 %constant_dynamic-slice_fusion.17 = bf16[384,384]{1,0:T(8,128)(2,1)S(1)} fusion(bf16[1536,384]{1,0:T(8,128)(2,1)} %param.3, s32[]{:T(128)S(6)} %select_n.68), kind=kLoop, calls=%fused_computation.76 | loop fusion | bytes 589828 | tf_op jit(solution)/shard_map/dynamic_slice | solution.py:98
  13.8 0.6 collective-permute-done
  14.4 1.1 %collective-permute-start.9 = (bf16[256,384]{1,0:T(8,128)(2,1)S(1)}, bf16[256,384]{1,0:T(8,128)(2,1)S(1)}, u32[]{:S(2)}, u32[]{:S(2)}) collective-permute-start(bf16[256,384]{1,0:T(8,128)(2,1)S(1)} %slice.132), channel_id=1, source_target_pairs={{0,1},{1,0},{2,3},{3,2},{4,5},{5,4},{6,7},{7,6},{8,9},{9,8},{10,11... | collective-permute-start | bytes 589832 | tf_op jit(solution)/shard_map/ppermute | solution.py:91
  15.5 2.6 %collective-permute-done.1 = bf16[96,384]{1,0:T(8,128)(2,1)S(1)} collective-permute-done((bf16[96,384]{1,0:T(8,128)(2,1)S(1)}, bf16[96,384]{1,0:T(8,128)(2,1)S(1)}, u32[]{:S(2)}, u32[]{:S(2)}) %collective-permute-start.1) | collective-permute-done | bytes 73760 | tf_op jit(solution)/shard_map/ppermute | solution.py:82
  18.1 2.5 %collective-permute-start.6 = (bf16[288,384]{1,0:T(8,128)(2,1)S(1)}, bf16[288,384]{1,0:T(8,128)(2,1)S(1)}, u32[]{:S(2)}, u32[]{:S(2)}) collective-permute-start(bf16[288,384]{1,0:T(8,128)(2,1)S(1)} %constant_dynamic-update-slice_fusion), channel_id=1, source_target_pairs={{0,24},{4,28},{8,16},{12,20},{16,8},{20,12},{24,0},{28,4},{1,25},{... | collective-permute-start | bytes 663560 | tf_op jit(solution)/shard_map/ppermute | solution.py:97
  20.7 2.7 %collective-permute-start.7 = (bf16[256,384]{1,0:T(8,128)(2,1)S(1)}, bf16[256,384]{1,0:T(8,128)(2,1)S(1)}, u32[]{:S(2)}, u32[]{:S(2)}) collective-permute-start(bf16[256,384]{1,0:T(8,128)(2,1)S(1)} %slice.132), channel_id=1, source_target_pairs={{0,3},{1,2},{2,1},{3,0},{4,7},{5,6},{6,5},{7,4},{8,11},{9,10},{10,... | collective-permute-start | bytes 589832 | tf_op jit(solution)/shard_map/ppermute | solution.py:91
  23.4 0.3 fusion.15
  23.7 3.2 %collective-permute-done.6 = bf16[288,384]{1,0:T(8,128)(2,1)S(1)} collective-permute-done((bf16[288,384]{1,0:T(8,128)(2,1)S(1)}, bf16[288,384]{1,0:T(8,128)(2,1)S(1)}, u32[]{:S(2)}, u32[]{:S(2)}) %collective-permute-start.6) | collective-permute-done | bytes 221216 | tf_op jit(solution)/shard_map/ppermute | solution.py:97
  26.9 1.5 %collective-permute-start.5 = (bf16[288,384]{1,0:T(8,128)(2,1)S(1)}, bf16[288,384]{1,0:T(8,128)(2,1)S(1)}, u32[]{:S(2)}, u32[]{:S(2)}) collective-permute-start(bf16[288,384]{1,0:T(8,128)(2,1)S(1)} %constant_dynamic-update-slice_fusion), channel_id=1, source_target_pairs={{0,16},{4,20},{8,24},{12,28},{16,0},{20,4},{24,8},{28,12},{1,17},{... | collective-permute-start | bytes 663560 | tf_op jit(solution)/shard_map/ppermute | solution.py:97
  28.5 5.4 %collective-permute-done.5 = bf16[288,384]{1,0:T(8,128)(2,1)S(1)} collective-permute-done((bf16[288,384]{1,0:T(8,128)(2,1)S(1)}, bf16[288,384]{1,0:T(8,128)(2,1)S(1)}, u32[]{:S(2)}, u32[]{:S(2)}) %collective-permute-start.5) | collective-permute-done | bytes 221216 | tf_op jit(solution)/shard_map/ppermute | solution.py:97
  33.9 1.5 %collective-permute-start.4 = (bf16[288,384]{1,0:T(8,128)(2,1)S(1)}, bf16[288,384]{1,0:T(8,128)(2,1)S(1)}, u32[]{:S(2)}, u32[]{:S(2)}) collective-permute-start(bf16[288,384]{1,0:T(8,128)(2,1)S(1)} %constant_dynamic-update-slice_fusion), channel_id=1, source_target_pairs={{0,8},{4,12},{8,0},{12,4},{16,24},{20,28},{24,16},{28,20},{1,9},{5... | collective-permute-start | bytes 663560 | tf_op jit(solution)/shard_map/ppermute | solution.py:97
  35.5 4.5 %collective-permute-done.4 = bf16[288,384]{1,0:T(8,128)(2,1)S(1)} collective-permute-done((bf16[288,384]{1,0:T(8,128)(2,1)S(1)}, bf16[288,384]{1,0:T(8,128)(2,1)S(1)}, u32[]{:S(2)}, u32[]{:S(2)}) %collective-permute-start.4) | collective-permute-done | bytes 221216 | tf_op jit(solution)/shard_map/ppermute | solution.py:97
  40.2 1.2 %collective-permute-done.20 = bf16[128,384]{1,0:T(8,128)(2,1)S(1)} collective-permute-done((bf16[128,384]{1,0:T(8,128)(2,1)S(1)}, bf16[128,384]{1,0:T(8,128)(2,1)S(1)}, u32[]{:S(2)}, u32[]{:S(2)}) %collective-permute-start.20) | collective-permute-done | bytes 98336 | tf_op jit(solution)/shard_map/ppermute | solution.py:110
  41.5 0.3 convolution_add_fusion.1
  41.8 0.4 collective-permute-start.3
  42.2 0.4 collective-permute-done.22
  42.8 0.3 fusion.22
  43.2 0.8 %collective-permute-done.24 = bf16[128,384]{1,0:T(8,128)(2,1)S(1)} collective-permute-done((bf16[128,384]{1,0:T(8,128)(2,1)S(1)}, bf16[128,384]{1,0:T(8,128)(2,1)S(1)}, u32[]{:S(2)}, u32[]{:S(2)}) %collective-permute-start.24) | collective-permute-done | bytes 98336 | tf_op jit(solution)/shard_map/ppermute | solution.py:110
  44.0 0.3 fusion.26
  44.3 2.5 %collective-permute-start.28 = (bf16[96,256]{1,0:T(8,128)(2,1)S(1)}, bf16[96,256]{1,0:T(8,128)(2,1)S(1)}, u32[]{:S(2)}, u32[]{:S(2)}) collective-permute-start(bf16[96,256]{1,0:T(8,128)(2,1)S(1)} %get-tuple-element.29), channel_id=1, source_target_pairs={{0,24},{1,25},{2,26},{3,27},{4,29},{5,28},{6,31},{7,30},{8,16},{9,... | collective-permute-start | bytes 147464 | tf_op jit(solution)/shard_map/ppermute | solution.py:124
  46.9 0.4 fusion
  47.3 1.5 %collective-permute-start.10 = (bf16[256,384]{1,0:T(8,128)(2,1)S(1)}, bf16[256,384]{1,0:T(8,128)(2,1)S(1)}, u32[]{:S(2)}, u32[]{:S(2)}) collective-permute-start(bf16[256,384]{1,0:T(8,128)(2,1)S(1)} %collective-permute-done.9), channel_id=1, source_target_pairs={{0,4},{4,0},{8,12},{12,8},{16,20},{20,16},{24,28},{28,24},{1,5},{5... | collective-permute-start | bytes 589832 | tf_op jit(solution)/shard_map/ppermute | solution.py:110
  48.8 3.9 %collective-permute-done.11 = bf16[256,384]{1,0:T(8,128)(2,1)S(1)} collective-permute-done((bf16[256,384]{1,0:T(8,128)(2,1)S(1)}, bf16[256,384]{1,0:T(8,128)(2,1)S(1)}, u32[]{:S(2)}, u32[]{:S(2)}) %collective-permute-start.11) | collective-permute-done | bytes 196640 | tf_op jit(solution)/shard_map/ppermute | solution.py:91
  52.7 1.5 %collective-permute-start.27 = (bf16[96,256]{1,0:T(8,128)(2,1)S(1)}, bf16[96,256]{1,0:T(8,128)(2,1)S(1)}, u32[]{:S(2)}, u32[]{:S(2)}) collective-permute-start(bf16[96,256]{1,0:T(8,128)(2,1)S(1)} %get-tuple-element.30), channel_id=1, source_target_pairs={{0,16},{1,17},{2,18},{3,19},{4,21},{5,20},{6,23},{7,22},{8,24},{9,... | collective-permute-start | bytes 147464 | tf_op jit(solution)/shard_map/ppermute | solution.py:124
  54.2 1.4 %collective-permute-start.26 = (bf16[96,256]{1,0:T(8,128)(2,1)S(1)}, bf16[96,256]{1,0:T(8,128)(2,1)S(1)}, u32[]{:S(2)}, u32[]{:S(2)}) collective-permute-start(bf16[96,256]{1,0:T(8,128)(2,1)S(1)} %get-tuple-element.31), channel_id=1, source_target_pairs={{0,8},{1,9},{2,10},{3,11},{4,13},{5,12},{6,15},{7,14},{8,0},{9,1},... | collective-permute-start | bytes 147464 | tf_op jit(solution)/shard_map/ppermute | solution.py:124
  55.6 1.2 %collective-permute-done.27 = bf16[96,256]{1,0:T(8,128)(2,1)S(1)} collective-permute-done((bf16[96,256]{1,0:T(8,128)(2,1)S(1)}, bf16[96,256]{1,0:T(8,128)(2,1)S(1)}, u32[]{:S(2)}, u32[]{:S(2)}) %collective-permute-start.27) | collective-permute-done | bytes 49184 | tf_op jit(solution)/shard_map/ppermute | solution.py:124
  56.8 0.7 collective-permute-start.25
  57.5 1.3 %collective-permute-done.26 = bf16[96,256]{1,0:T(8,128)(2,1)S(1)} collective-permute-done((bf16[96,256]{1,0:T(8,128)(2,1)S(1)}, bf16[96,256]{1,0:T(8,128)(2,1)S(1)}, u32[]{:S(2)}, u32[]{:S(2)}) %collective-permute-start.26) | collective-permute-done | bytes 49184 | tf_op jit(solution)/shard_map/ppermute | solution.py:124
  58.8 0.4 convolution_add_fusion
  59.3 0.4 fusion.7
  59.8 0.4 fusion.11
  60.4 1.4 %collective-permute-start.16 = (bf16[96,512]{1,0:T(8,128)(2,1)S(1)}, bf16[96,512]{1,0:T(8,128)(2,1)S(1)}, u32[]{:S(2)}, u32[]{:S(2)}) collective-permute-start(bf16[96,512]{1,0:T(8,128)(2,1)S(1)} %get-tuple-element.12), channel_id=1, source_target_pairs={{0,24},{1,25},{2,26},{3,27},{4,29},{5,28},{6,31},{7,30},{8,16},{9,... | collective-permute-start | bytes 294920 | tf_op jit(solution)/shard_map/ppermute | solution.py:124
  61.8 4.0 %collective-permute-start.29 = (bf16[4,48,256]{2,1,0:T(8,128)(2,1)S(1)}, bf16[4,48,256]{2,1,0:T(8,128)(2,1)S(1)}, u32[]{:S(2)}, u32[]{:S(2)}) collective-permute-start(bf16[4,48,256]{2,1,0:T(8,128)(2,1)S(1)} %pad_maximum_fusion.5), channel_id=1, source_target_pairs={{0,4},{4,0},{8,12},{12,8},{16,20},{20,16},{24,28},{28,24},{1,5},{5... | collective-permute-start | bytes 294920 | tf_op jit(solution)/shard_map/ppermute | solution.py:128
  65.8 0.3 collective-permute-start.15
  66.1 0.5 collective-permute-start.14
  66.7 0.7 collective-permute-start.13
  67.4 4.1 %collective-permute-done.15 = bf16[96,512]{1,0:T(8,128)(2,1)S(1)} collective-permute-done((bf16[96,512]{1,0:T(8,128)(2,1)S(1)}, bf16[96,512]{1,0:T(8,128)(2,1)S(1)}, u32[]{:S(2)}, u32[]{:S(2)}) %collective-permute-start.15) | collective-permute-done | bytes 98336 | tf_op jit(solution)/shard_map/ppermute | solution.py:124
  71.5 0.3 collective-permute-done.14
  71.9 0.8 collective-permute-start.17
  72.6 1.3 %shard_map.28.refs_9_ = bf16[3,48,2048]{2,1,0:T(8,128)(2,1)} custom-call(s32[16]{0:T(128)S(1)} %stack.114.refs_0_, bf16[48,256]{1,0:T(8,128)(2,1)S(1)} %get-tuple-element.50.refs_1_, bf16[48,256]{1,0:T(8,128)(2,1)S(1)} %get-tuple-element.52.refs_2_, bf16[48,256]{1,0:T(8,128)(2,1)S(1)} %get-tuple-element.54.refs_3_, ...), custom_call_target="tpu_custom_call" | custom-call | tf_op jit(solution)/shard_map/pallas_call | solution.py:41
  74.0 1.4 %shard_map.29 = bf16[3,48,2048]{2,1,0:T(8,128)(2,1)} custom-call(s32[16]{0:T(128)S(1)} %stack.114.refs_0_, bf16[48,512]{1,0:T(8,128)(2,1)S(1)} %get-tuple-element.42.refs_1_, bf16[48,512]{1,0:T(8,128)(2,1)S(1)} %get-tuple-element.44.refs_2_, bf16[48,512]{1,0:T(8,128)(2,1)S(1)} %get-tuple-element.46.refs_3_, ...), custom_call_target="tpu_custom_call", output_to_operand_aliasing={{}: (9, {})} | custom-call | tf_op jit(solution)/shard_map/pallas_call | solution.py:41
  (57 shorter events, 1.7 us)
Async XLA Ops:
  1.3 38.7 %collective-permute-start.21 = (bf16[128,384]{1,0:T(8,128)(2,1)S(1)}, bf16[128,384]{1,0:T(8,128)(2,1)S(1)}, u32[]{:S(2)}, u32[]{:S(2)}) collective-permute-start(bf16[128,384]{1,0:T(8,128)(2,1)S(1)} %slice.148), channel_id=1, source_target_pairs={{0,1},{1,0},{2,3},{3,2},{4,5},{5,4},{6,7},{7,6},{8,9},{9,8},{10,11... | collective-permute-start | bytes 294920 | tf_op jit(solution)/shard_map/ppermute | solution.py:91
  4.4 31.0 %collective-permute-start.19 = (bf16[128,384]{1,0:T(8,128)(2,1)S(1)}, bf16[128,384]{1,0:T(8,128)(2,1)S(1)}, u32[]{:S(2)}, u32[]{:S(2)}) collective-permute-start(bf16[128,384]{1,0:T(8,128)(2,1)S(1)} %slice.148), channel_id=1, source_target_pairs={{0,3},{1,2},{2,1},{3,0},{4,7},{5,6},{6,5},{7,4},{8,11},{9,10},{10,... | collective-permute-start | bytes 294920 | tf_op jit(solution)/shard_map/ppermute | solution.py:91
  7.9 10.2 %collective-permute-start.2 = (bf16[96,384]{1,0:T(8,128)(2,1)S(1)}, bf16[96,384]{1,0:T(8,128)(2,1)S(1)}, u32[]{:S(2)}, u32[]{:S(2)}) collective-permute-start(bf16[96,384]{1,0:T(8,128)(2,1)S(1)} %get-tuple-element.7), channel_id=1, source_target_pairs={{0,3},{1,2},{2,1},{3,0},{4,7},{5,6},{6,5},{7,4},{8,11},{9,10},{10,... | collective-permute-start | bytes 221192 | tf_op jit(solution)/shard_map/ppermute | solution.py:82
  9.3 5.1 %collective-permute-start = (bf16[96,384]{1,0:T(8,128)(2,1)S(1)}, bf16[96,384]{1,0:T(8,128)(2,1)S(1)}, u32[]{:S(2)}, u32[]{:S(2)}) collective-permute-start(bf16[96,384]{1,0:T(8,128)(2,1)S(1)} %get-tuple-element.8), channel_id=1, source_target_pairs={{0,1},{1,0},{2,3},{3,2},{4,5},{5,4},{6,7},{7,6},{8,9},{9,8},{10,11... | collective-permute-start | bytes 221192 | tf_op jit(solution)/shard_map/ppermute | solution.py:82
  9.3 8.8 %collective-permute-start.1 = (bf16[96,384]{1,0:T(8,128)(2,1)S(1)}, bf16[96,384]{1,0:T(8,128)(2,1)S(1)}, u32[]{:S(2)}, u32[]{:S(2)}) collective-permute-start(bf16[96,384]{1,0:T(8,128)(2,1)S(1)} %get-tuple-element.9), channel_id=1, source_target_pairs={{0,2},{1,3},{2,0},{3,1},{4,6},{5,7},{6,4},{7,5},{8,10},{9,11},{10,... | collective-permute-start | bytes 221192 | tf_op jit(solution)/shard_map/ppermute | solution.py:82
  14.4 32.8 %collective-permute-start.9 = (bf16[256,384]{1,0:T(8,128)(2,1)S(1)}, bf16[256,384]{1,0:T(8,128)(2,1)S(1)}, u32[]{:S(2)}, u32[]{:S(2)}) collective-permute-start(bf16[256,384]{1,0:T(8,128)(2,1)S(1)} %slice.132), channel_id=1, source_target_pairs={{0,1},{1,0},{2,3},{3,2},{4,5},{5,4},{6,7},{7,6},{8,9},{9,8},{10,11... | collective-permute-start | bytes 589832 | tf_op jit(solution)/shard_map/ppermute | solution.py:91
  18.1 2.6 %collective-permute-start.18 = (bf16[128,384]{1,0:T(8,128)(2,1)S(1)}, bf16[128,384]{1,0:T(8,128)(2,1)S(1)}, u32[]{:S(2)}, u32[]{:S(2)}) collective-permute-start(bf16[128,384]{1,0:T(8,128)(2,1)S(1)} %slice.147), channel_id=1, source_target_pairs={{0,4},{4,0},{8,12},{12,8},{16,20},{20,16},{24,28},{28,24},{1,5},{5... | collective-permute-start | bytes 294920 | tf_op jit(solution)/shard_map/ppermute | solution.py:110
  18.1 8.8 %collective-permute-start.6 = (bf16[288,384]{1,0:T(8,128)(2,1)S(1)}, bf16[288,384]{1,0:T(8,128)(2,1)S(1)}, u32[]{:S(2)}, u32[]{:S(2)}) collective-permute-start(bf16[288,384]{1,0:T(8,128)(2,1)S(1)} %constant_dynamic-update-slice_fusion), channel_id=1, source_target_pairs={{0,24},{4,28},{8,16},{12,20},{16,8},{20,12},{24,0},{28,4},{1,25},{... | collective-permute-start | bytes 663560 | tf_op jit(solution)/shard_map/ppermute | solution.py:97
  20.7 28.0 %collective-permute-start.7 = (bf16[256,384]{1,0:T(8,128)(2,1)S(1)}, bf16[256,384]{1,0:T(8,128)(2,1)S(1)}, u32[]{:S(2)}, u32[]{:S(2)}) collective-permute-start(bf16[256,384]{1,0:T(8,128)(2,1)S(1)} %slice.132), channel_id=1, source_target_pairs={{0,3},{1,2},{2,1},{3,0},{4,7},{5,6},{6,5},{7,4},{8,11},{9,10},{10,... | collective-permute-start | bytes 589832 | tf_op jit(solution)/shard_map/ppermute | solution.py:91
  26.9 7.0 %collective-permute-start.5 = (bf16[288,384]{1,0:T(8,128)(2,1)S(1)}, bf16[288,384]{1,0:T(8,128)(2,1)S(1)}, u32[]{:S(2)}, u32[]{:S(2)}) collective-permute-start(bf16[288,384]{1,0:T(8,128)(2,1)S(1)} %constant_dynamic-update-slice_fusion), channel_id=1, source_target_pairs={{0,16},{4,20},{8,24},{12,28},{16,0},{20,4},{24,8},{28,12},{1,17},{... | collective-permute-start | bytes 663560 | tf_op jit(solution)/shard_map/ppermute | solution.py:97
  33.9 6.1 %collective-permute-start.4 = (bf16[288,384]{1,0:T(8,128)(2,1)S(1)}, bf16[288,384]{1,0:T(8,128)(2,1)S(1)}, u32[]{:S(2)}, u32[]{:S(2)}) collective-permute-start(bf16[288,384]{1,0:T(8,128)(2,1)S(1)} %constant_dynamic-update-slice_fusion), channel_id=1, source_target_pairs={{0,8},{4,12},{8,0},{12,4},{16,24},{20,28},{24,16},{28,20},{1,9},{5... | collective-permute-start | bytes 663560 | tf_op jit(solution)/shard_map/ppermute | solution.py:97
  35.4 6.4 %collective-permute-start.23 = (bf16[128,384]{1,0:T(8,128)(2,1)S(1)}, bf16[128,384]{1,0:T(8,128)(2,1)S(1)}, u32[]{:S(2)}, u32[]{:S(2)}) collective-permute-start(bf16[128,384]{1,0:T(8,128)(2,1)S(1)} %slice.147), channel_id=1, source_target_pairs={{0,2},{1,3},{2,0},{3,1},{4,6},{5,7},{6,4},{7,5},{8,10},{9,11},{10,... | collective-permute-start | bytes 294920 | tf_op jit(solution)/shard_map/ppermute | solution.py:91
  40.0 1.3 %collective-permute-start.20 = (bf16[128,384]{1,0:T(8,128)(2,1)S(1)}, bf16[128,384]{1,0:T(8,128)(2,1)S(1)}, u32[]{:S(2)}, u32[]{:S(2)}) collective-permute-start(bf16[128,384]{1,0:T(8,128)(2,1)S(1)} %collective-permute-done.19), channel_id=1, source_target_pairs={{0,4},{4,0},{8,12},{12,8},{16,20},{20,16},{24,28},{28,24},{1,5},{5... | collective-permute-start | bytes 294920 | tf_op jit(solution)/shard_map/ppermute | solution.py:110
  40.1 12.6 %collective-permute-start.11 = (bf16[256,384]{1,0:T(8,128)(2,1)S(1)}, bf16[256,384]{1,0:T(8,128)(2,1)S(1)}, u32[]{:S(2)}, u32[]{:S(2)}) collective-permute-start(bf16[256,384]{1,0:T(8,128)(2,1)S(1)} %slice.128), channel_id=1, source_target_pairs={{0,2},{1,3},{2,0},{3,1},{4,6},{5,7},{6,4},{7,5},{8,10},{9,11},{10,... | collective-permute-start | bytes 589832 | tf_op jit(solution)/shard_map/ppermute | solution.py:91
  41.3 1.3 %collective-permute-start.22 = (bf16[128,384]{1,0:T(8,128)(2,1)S(1)}, bf16[128,384]{1,0:T(8,128)(2,1)S(1)}, u32[]{:S(2)}, u32[]{:S(2)}) collective-permute-start(bf16[128,384]{1,0:T(8,128)(2,1)S(1)} %collective-permute-done.21), channel_id=1, source_target_pairs={{0,4},{4,0},{8,12},{12,8},{16,20},{20,16},{24,28},{28,24},{1,5},{5... | collective-permute-start | bytes 294920 | tf_op jit(solution)/shard_map/ppermute | solution.py:110
  41.8 5.0 %collective-permute-start.3 = (bf16[256,384]{1,0:T(8,128)(2,1)S(1)}, bf16[256,384]{1,0:T(8,128)(2,1)S(1)}, u32[]{:S(2)}, u32[]{:S(2)}) collective-permute-start(bf16[256,384]{1,0:T(8,128)(2,1)S(1)} %slice.128), channel_id=1, source_target_pairs={{0,4},{4,0},{8,12},{12,8},{16,20},{20,16},{24,28},{28,24},{1,5},{5... | collective-permute-start | bytes 589832 | tf_op jit(solution)/shard_map/ppermute | solution.py:110
  42.7 1.3 %collective-permute-start.24 = (bf16[128,384]{1,0:T(8,128)(2,1)S(1)}, bf16[128,384]{1,0:T(8,128)(2,1)S(1)}, u32[]{:S(2)}, u32[]{:S(2)}) collective-permute-start(bf16[128,384]{1,0:T(8,128)(2,1)S(1)} %collective-permute-done.23), channel_id=1, source_target_pairs={{0,4},{4,0},{8,12},{12,8},{16,20},{20,16},{24,28},{28,24},{1,5},{5... | collective-permute-start | bytes 294920 | tf_op jit(solution)/shard_map/ppermute | solution.py:110
  44.3 9.8 %collective-permute-start.28 = (bf16[96,256]{1,0:T(8,128)(2,1)S(1)}, bf16[96,256]{1,0:T(8,128)(2,1)S(1)}, u32[]{:S(2)}, u32[]{:S(2)}) collective-permute-start(bf16[96,256]{1,0:T(8,128)(2,1)S(1)} %get-tuple-element.29), channel_id=1, source_target_pairs={{0,24},{1,25},{2,26},{3,27},{4,29},{5,28},{6,31},{7,30},{8,16},{9,... | collective-permute-start | bytes 147464 | tf_op jit(solution)/shard_map/ppermute | solution.py:124
  47.3 12.0 %collective-permute-start.10 = (bf16[256,384]{1,0:T(8,128)(2,1)S(1)}, bf16[256,384]{1,0:T(8,128)(2,1)S(1)}, u32[]{:S(2)}, u32[]{:S(2)}) collective-permute-start(bf16[256,384]{1,0:T(8,128)(2,1)S(1)} %collective-permute-done.9), channel_id=1, source_target_pairs={{0,4},{4,0},{8,12},{12,8},{16,20},{20,16},{24,28},{28,24},{1,5},{5... | collective-permute-start | bytes 589832 | tf_op jit(solution)/shard_map/ppermute | solution.py:110
  48.7 10.1 %collective-permute-start.8 = (bf16[256,384]{1,0:T(8,128)(2,1)S(1)}, bf16[256,384]{1,0:T(8,128)(2,1)S(1)}, u32[]{:S(2)}, u32[]{:S(2)}) collective-permute-start(bf16[256,384]{1,0:T(8,128)(2,1)S(1)} %collective-permute-done.7), channel_id=1, source_target_pairs={{0,4},{4,0},{8,12},{12,8},{16,20},{20,16},{24,28},{28,24},{1,5},{5... | collective-permute-start | bytes 589832 | tf_op jit(solution)/shard_map/ppermute | solution.py:110
  52.7 7.1 %collective-permute-start.12 = (bf16[256,384]{1,0:T(8,128)(2,1)S(1)}, bf16[256,384]{1,0:T(8,128)(2,1)S(1)}, u32[]{:S(2)}, u32[]{:S(2)}) collective-permute-start(bf16[256,384]{1,0:T(8,128)(2,1)S(1)} %collective-permute-done.11), channel_id=1, source_target_pairs={{0,4},{4,0},{8,12},{12,8},{16,20},{20,16},{24,28},{28,24},{1,5},{5... | collective-permute-start | bytes 589832 | tf_op jit(solution)/shard_map/ppermute | solution.py:110
  52.7 4.1 %collective-permute-start.27 = (bf16[96,256]{1,0:T(8,128)(2,1)S(1)}, bf16[96,256]{1,0:T(8,128)(2,1)S(1)}, u32[]{:S(2)}, u32[]{:S(2)}) collective-permute-start(bf16[96,256]{1,0:T(8,128)(2,1)S(1)} %get-tuple-element.30), channel_id=1, source_target_pairs={{0,16},{1,17},{2,18},{3,19},{4,21},{5,20},{6,23},{7,22},{8,24},{9,... | collective-permute-start | bytes 147464 | tf_op jit(solution)/shard_map/ppermute | solution.py:124
  54.2 4.6 %collective-permute-start.26 = (bf16[96,256]{1,0:T(8,128)(2,1)S(1)}, bf16[96,256]{1,0:T(8,128)(2,1)S(1)}, u32[]{:S(2)}, u32[]{:S(2)}) collective-permute-start(bf16[96,256]{1,0:T(8,128)(2,1)S(1)} %get-tuple-element.31), channel_id=1, source_target_pairs={{0,8},{1,9},{2,10},{3,11},{4,13},{5,12},{6,15},{7,14},{8,0},{9,1},... | collective-permute-start | bytes 147464 | tf_op jit(solution)/shard_map/ppermute | solution.py:124
  56.8 2.0 %collective-permute-start.25 = (bf16[96,256]{1,0:T(8,128)(2,1)S(1)}, bf16[96,256]{1,0:T(8,128)(2,1)S(1)}, u32[]{:S(2)}, u32[]{:S(2)}) collective-permute-start(bf16[96,256]{1,0:T(8,128)(2,1)S(1)} %get-tuple-element.32), channel_id=1, source_target_pairs={{0,0},{1,1},{2,2},{3,3},{4,5},{5,4},{6,7},{7,6},{8,8},{9,9},{10,10... | collective-permute-start | bytes 147464 | tf_op jit(solution)/shard_map/ppermute | solution.py:124
  60.4 6.9 %collective-permute-start.16 = (bf16[96,512]{1,0:T(8,128)(2,1)S(1)}, bf16[96,512]{1,0:T(8,128)(2,1)S(1)}, u32[]{:S(2)}, u32[]{:S(2)}) collective-permute-start(bf16[96,512]{1,0:T(8,128)(2,1)S(1)} %get-tuple-element.12), channel_id=1, source_target_pairs={{0,24},{1,25},{2,26},{3,27},{4,29},{5,28},{6,31},{7,30},{8,16},{9,... | collective-permute-start | bytes 294920 | tf_op jit(solution)/shard_map/ppermute | solution.py:124
  61.8 10.8 %collective-permute-start.29 = (bf16[4,48,256]{2,1,0:T(8,128)(2,1)S(1)}, bf16[4,48,256]{2,1,0:T(8,128)(2,1)S(1)}, u32[]{:S(2)}, u32[]{:S(2)}) collective-permute-start(bf16[4,48,256]{2,1,0:T(8,128)(2,1)S(1)} %pad_maximum_fusion.5), channel_id=1, source_target_pairs={{0,4},{4,0},{8,12},{12,8},{16,20},{20,16},{24,28},{28,24},{1,5},{5... | collective-permute-start | bytes 294920 | tf_op jit(solution)/shard_map/ppermute | solution.py:128
  65.8 5.7 %collective-permute-start.15 = (bf16[96,512]{1,0:T(8,128)(2,1)S(1)}, bf16[96,512]{1,0:T(8,128)(2,1)S(1)}, u32[]{:S(2)}, u32[]{:S(2)}) collective-permute-start(bf16[96,512]{1,0:T(8,128)(2,1)S(1)} %get-tuple-element.13), channel_id=1, source_target_pairs={{0,16},{1,17},{2,18},{3,19},{4,21},{5,20},{6,23},{7,22},{8,24},{9,... | collective-permute-start | bytes 294920 | tf_op jit(solution)/shard_map/ppermute | solution.py:124
  66.1 5.7 %collective-permute-start.14 = (bf16[96,512]{1,0:T(8,128)(2,1)S(1)}, bf16[96,512]{1,0:T(8,128)(2,1)S(1)}, u32[]{:S(2)}, u32[]{:S(2)}) collective-permute-start(bf16[96,512]{1,0:T(8,128)(2,1)S(1)} %get-tuple-element.14), channel_id=1, source_target_pairs={{0,8},{1,9},{2,10},{3,11},{4,13},{5,12},{6,15},{7,14},{8,0},{9,1},... | collective-permute-start | bytes 294920 | tf_op jit(solution)/shard_map/ppermute | solution.py:124
  66.7 5.2 %collective-permute-start.13 = (bf16[96,512]{1,0:T(8,128)(2,1)S(1)}, bf16[96,512]{1,0:T(8,128)(2,1)S(1)}, u32[]{:S(2)}, u32[]{:S(2)}) collective-permute-start(bf16[96,512]{1,0:T(8,128)(2,1)S(1)} %get-tuple-element.15), channel_id=1, source_target_pairs={{0,0},{1,1},{2,2},{3,3},{4,5},{5,4},{6,7},{7,6},{8,8},{9,9},{10,10... | collective-permute-start | bytes 294920 | tf_op jit(solution)/shard_map/ppermute | solution.py:124
  71.9 2.0 %collective-permute-start.17 = (bf16[4,48,512]{2,1,0:T(8,128)(2,1)S(1)}, bf16[4,48,512]{2,1,0:T(8,128)(2,1)S(1)}, u32[]{:S(2)}, u32[]{:S(2)}) collective-permute-start(bf16[4,48,512]{2,1,0:T(8,128)(2,1)S(1)} %pad_maximum_fusion.4), channel_id=1, source_target_pairs={{0,4},{4,0},{8,12},{12,8},{16,20},{20,16},{24,28},{28,24},{1,5},{5... | collective-permute-start | bytes 589832 | tf_op jit(solution)/shard_map/ppermute | solution.py:128

commit v3 on v2

--- a/solution.py
+++ b/solution.py
@@ -1,3 +1,5 @@
+import functools
+
 import jax
 import jax.numpy as jnp
 from jax import lax
@@ -14,39 +16,22 @@
     return index ^ step if size & (size - 1) == 0 else (index - step + size) % size
 
 
-def assemble(first, place, *refs):
-    *parts, _, out, whole, sem = refs
-    comps, _, width = whole.shape
-    half = width // (2 * len(parts))
-    for number, part in enumerate(parts):
-        for other in range(2):
-            start = pl.multiple_of(place[2 * number + other] * half, half)
-            for comp in range(comps):
-                column = (other * comps + comp) * half
-                whole[comp, :, pl.ds(start, half)] = part[:, column : column + half]
-    copy = pltpu.make_async_copy(whole, out.at[pl.ds(first, comps)], sem)
-    copy.start()
-    copy.wait()
+def assemble(chunks, place, *refs):
+    *kept, fetched, out = refs
+    many = len(kept) // len(chunks)
+    half = out.shape[2] // (4 * many)
 
+    def put(spot, comp, values):
+        out[comp, :, pl.ds(pl.multiple_of(place[spot] * half, half), half)] = values
 
-def assemble_first(first, place, *refs):
-    assemble(first, place, *refs[:-3], None, *refs[-3:])
-
-
-def write_out(spots, parts, first, comps, shape, earlier):
-    rows = parts[0].shape[0]
-    smem, vmem, anywhere = (pl.BlockSpec(memory_space=m) for m in (pltpu.SMEM, pltpu.VMEM, pl.ANY))
-    given = [] if earlier is None else [earlier]
-    kernel = assemble if given else assemble_first
-    return pl.pallas_call(
-        lambda *refs: kernel(first, *refs),
-        out_shape=jax.ShapeDtypeStruct(shape, jnp.bfloat16),
-        in_specs=[smem] + [vmem] * len(parts) + [anywhere] * len(given),
-        out_specs=anywhere,
-        scratch_shapes=[pltpu.VMEM((comps, rows, shape[2]), jnp.bfloat16), pltpu.SemaphoreType.DMA],
-        input_output_aliases={1 + len(parts): 0} if given else {},
-        compiler_params=pltpu.CompilerParams(vmem_limit_bytes=8 << 20),
-    )(spots, *parts, *given)
+    for c, (first, end) in enumerate(chunks):
+        for number in range(many):
+            for other in range(2):
+                for comp in range(first, end):
+                    column = (other * (end - first) + comp - first) * half
+                    put(2 * number + other, comp, kept[c * many + number][:, column : column + half])
+                    column += 2 * first * half
+                    put(2 * (many + number) + other, comp, fetched[number, :, column : column + half])
 
 
 def direct(products, operator):
@@ -102,7 +87,7 @@
     for k in range(deep - 1):
         weights.append(jnp.concatenate([g[k * piece : k * piece + piece] for g in gathered]))
 
-    out = None
+    kept, passed = [], []
     for first, end, members in chunks:
         total = None
         for k in order:
@@ -115,7 +100,6 @@
             total = term if total is None else lax.optimization_barrier(total) + term
         result = total.astype(jnp.bfloat16).reshape(chips, piece, -1)
 
-        kept, passed, places = [], [], []
         for j in range(chips):
             pairs = []
             for i in range(wide):
@@ -124,16 +108,22 @@
             landed = lax.ppermute(result[j], ("gx", "gy"), pairs)
             kept.append(lax.dynamic_slice_in_dim(landed, core * rows, rows, 0))
             passed.append(lax.dynamic_slice_in_dim(landed, (1 - core) * rows, rows, 0))
-            places.append(hop(chip, j, chips))
-        fetched = lax.ppermute(jnp.stack(passed), "gx", swap)
-        spots = [
-            (place * 2 + (core ^ via ^ e)) * 2 + (q ^ core ^ via)
-            for via in range(2)
-            for place in places
-            for e in range(2)
-        ]
-        parts = kept + [fetched[i] for i in range(chips)]
-        out = write_out(jnp.stack(spots).astype(jnp.int32), parts, first, end - first, (comps, rows, wide * modes), out)
+    passed = [jnp.concatenate(passed[j::chips], axis=1) for j in range(chips)]
+    fetched = lax.ppermute(jnp.stack(passed), "gx", swap)
+    spots = [
+        (hop(chip, j, chips) * 2 + (core ^ via ^ e)) * 2 + (q ^ core ^ via)
+        for via in range(2)
+        for j in range(chips)
+        for e in range(2)
+    ]
+    smem, vmem = (pl.BlockSpec(memory_space=m) for m in (pltpu.SMEM, pltpu.VMEM))
+    out = pl.pallas_call(
+        functools.partial(assemble, [chunk[:2] for chunk in chunks]),
+        out_shape=jax.ShapeDtypeStruct((comps, rows, wide * modes), jnp.bfloat16),
+        in_specs=[smem] + [vmem] * (len(kept) + 1),
+        out_specs=vmem,
+        compiler_params=pltpu.CompilerParams(vmem_limit_bytes=8 << 20),
+    )(jnp.stack(spots).astype(jnp.int32), *kept, fetched)
     return out.transpose(1, 0, 2)
 
 

time: 75.6 us -> 82.8 us (1.095)
  waiting for transfers between devices: 29.6 us -> 35.8 us
  starting transfers between devices: 35.5 us -> 37.7 us
  Pallas kernels: 2.66 us -> 1.47 us
    ppermute x3, waiting for transfers between devices: 3.17 us -> 11 us  [paired(): shares[k] = lax.ppermute(pieces[k], 'gy', [(i, i ^ k) for i in range(deep)])]
    ppermute x2 -> x1, starting transfers between devices: 4.74 us -> 0.07 us  [paired(): fetched = lax.ppermute(jnp.stack(passed), 'gx', swap)]
    ppermute x3, waiting for transfers between devices: 13.2 us -> 8.75 us  [paired(): gathered.append(lax.ppermute(arrived, 'gx', pairs))]
    ppermute x8, starting transfers between devices: 2.29 us -> 5.18 us  [paired(): theirs = lax.ppermute(ours, 'gx', swap)]
    ppermute x8, starting transfers between devices: 8.94 us -> 10.8 us  [paired(): landed = lax.ppermute(result[j], ('gx', 'gy'), pairs)]
    ppermute x3, starting transfers between devices: 4.45 us -> 6.09 us  [paired(): shares[k] = lax.ppermute(pieces[k], 'gy', [(i, i ^ k) for i in range(deep)])]
    ppermute x2 -> x1, waiting for transfers between devices: 0.01 us -> 1.44 us  [paired(): fetched = lax.ppermute(jnp.stack(passed), 'gx', swap)]
    pallas_call x2 -> x1, Pallas kernels: 2.66 us -> 1.47 us  [paired(): pl.pallas_call(functools.partial(assemble, [chunk[:2] for chunk in chunks...]
  transfers between devices with their start and end apart: 30 -> 29, of which waited for: 13 -> 14; matrix products, arithmetic and copies ran while one was open for 7% -> 7% of each run, Pallas kernels for 2% -> 0%
where the time goes in v3:
time: 82.8 us; the launch traced here: 82.5 us
  starting transfers between devices  37.7 us (46%)
  waiting for transfers between devices  35.8 us (43%)
  local copies, waits for them, and re-layouts  3.92 us (5%)
  matrix products  2.72 us (3%)
  Pallas kernels  1.47 us (2%)
    ppermute x3, waiting for transfers between devices, paired(): shares[k] = lax.ppermute(pieces[k], 'gy', [(i, i ^ k) for i in range(deep)])  11 us
    ppermute x8, starting transfers between devices, paired(): landed = lax.ppermute(result[j], ('gx', 'gy'), pairs)  10.8 us
    ppermute x6, starting transfers between devices, paired(): lax.ppermute(halves[k % 2][a:b], 'gy', [(i, i ^ k) for i in range(deep)])  9.78 us
    ppermute x3, waiting for transfers between devices, paired(): gathered.append(lax.ppermute(arrived, 'gx', pairs))  8.75 us
    ppermute x8, waiting for transfers between devices, paired(): landed = lax.ppermute(result[j], ('gx', 'gy'), pairs)  7.71 us
    ppermute x3, starting transfers between devices, paired(): shares[k] = lax.ppermute(pieces[k], 'gy', [(i, i ^ k) for i in range(deep)])  6.09 us
    ppermute x3, starting transfers between devices, paired(): gathered.append(lax.ppermute(arrived, 'gx', pairs))  5.78 us
    ppermute x8, starting transfers between devices, paired(): theirs = lax.ppermute(ours, 'gx', swap)  5.18 us
  transfers between devices with their start and end apart: 29, of which 14 were waited for; matrix products, arithmetic and copies ran while one was open for 7% of the time, Pallas kernels for 0%

profile of v3, /device:TPU:0, one launch (start us, length us, event | category | flops | bytes accessed | tf_op | source)
XLA Modules:
  0.0 82.5 jit_solution(8570188568039697052)
XLA Ops:
  0.0 1.1 %constant_dynamic-slice_fusion.16 = (bf16[384,3,128]{2,0,1:T(8,128)(2,1)S(1)}, bf16[384,3,128]{2,0,1:T(8,128)(2,1)S(1)}) fusion(bf16[384,3,256]{2,0,1:T(8,128)(2,1)} %param.2, s32[]{:T(128)S(6)} %select_n.77, s32[]{:T(128)S(6)} %select_n.76), kind=kLoop, calls=%fused_computation.62 | loop fusion | bytes 1179656 | tf_op jit(solution)/shard_map/dynamic_slice | solution.py:70
  1.1 0.2 copy.6
  1.3 5.1 %collective-permute-start.7 = (bf16[128,384]{1,0:T(8,128)(2,1)S(1)}, bf16[128,384]{1,0:T(8,128)(2,1)S(1)}, u32[]{:S(2)}, u32[]{:S(2)}) collective-permute-start(bf16[128,384]{1,0:T(8,128)(2,1)S(1)} %slice.100), channel_id=1, source_target_pairs={{0,3},{1,2},{2,1},{3,0},{4,7},{5,6},{6,5},{7,4},{8,11},{9,10},{10,... | collective-permute-start | bytes 294920 | tf_op jit(solution)/shard_map/ppermute | solution.py:76
  6.5 0.2 copy.5
  6.8 0.7 collective-permute-start.11
  7.5 1.0 %constant_dynamic-slice_fusion.22 = (bf16[96,384]{1,0:T(8,128)(2,1)S(1)}, bf16[96,384]{1,0:T(8,128)(2,1)S(1)}, bf16[96,384]{1,0:T(8,128)(2,1)S(1)}) fusion(bf16[1536,384]{1,0:T(8,128)(2,1)} %param.3, s32[]{:T(128)S(6)} %select_n.71, s32[]{:T(128)S(6)} %select_n.69, s32[]{:T(128)S(6)} %select_n.70), kind=kLoop, calls=%fused_computation.68 | loop fusion | bytes 442380 | tf_op jit(solution)/shard_map/dynamic_slice | solution.py:63
  8.5 1.5 %collective-permute-start = (bf16[96,384]{1,0:T(8,128)(2,1)S(1)}, bf16[96,384]{1,0:T(8,128)(2,1)S(1)}, u32[]{:S(2)}, u32[]{:S(2)}) collective-permute-start(bf16[96,384]{1,0:T(8,128)(2,1)S(1)} %get-tuple-element.8), channel_id=1, source_target_pairs={{0,1},{1,0},{2,3},{3,2},{4,5},{5,4},{6,7},{7,6},{8,9},{9,8},{10,11... | collective-permute-start | bytes 221192 | tf_op jit(solution)/shard_map/ppermute | solution.py:67
  10.1 1.0 %constant_dynamic-slice_fusion.25 = bf16[384,384]{1,0:T(8,128)(2,1)S(1)} fusion(bf16[1536,384]{1,0:T(8,128)(2,1)} %param.3, s32[]{:T(128)S(6)} %select_n.68), kind=kLoop, calls=%fused_computation.71 | loop fusion | bytes 589828 | tf_op jit(solution)/shard_map/dynamic_slice | solution.py:83
  11.1 4.1 %collective-permute-done = bf16[96,384]{1,0:T(8,128)(2,1)S(1)} collective-permute-done((bf16[96,384]{1,0:T(8,128)(2,1)S(1)}, bf16[96,384]{1,0:T(8,128)(2,1)S(1)}, u32[]{:S(2)}, u32[]{:S(2)}) %collective-permute-start) | collective-permute-done | bytes 73760 | tf_op jit(solution)/shard_map/ppermute | solution.py:67
  15.2 1.3 %collective-permute-start.1 = (bf16[96,384]{1,0:T(8,128)(2,1)S(1)}, bf16[96,384]{1,0:T(8,128)(2,1)S(1)}, u32[]{:S(2)}, u32[]{:S(2)}) collective-permute-start(bf16[96,384]{1,0:T(8,128)(2,1)S(1)} %get-tuple-element.9), channel_id=1, source_target_pairs={{0,2},{1,3},{2,0},{3,1},{4,6},{5,7},{6,4},{7,5},{8,10},{9,11},{10,... | collective-permute-start | bytes 221192 | tf_op jit(solution)/shard_map/ppermute | solution.py:67
  16.5 3.9 %collective-permute-done.1 = bf16[96,384]{1,0:T(8,128)(2,1)S(1)} collective-permute-done((bf16[96,384]{1,0:T(8,128)(2,1)S(1)}, bf16[96,384]{1,0:T(8,128)(2,1)S(1)}, u32[]{:S(2)}, u32[]{:S(2)}) %collective-permute-start.1) | collective-permute-done | bytes 73760 | tf_op jit(solution)/shard_map/ppermute | solution.py:67
  20.4 3.2 %collective-permute-start.2 = (bf16[96,384]{1,0:T(8,128)(2,1)S(1)}, bf16[96,384]{1,0:T(8,128)(2,1)S(1)}, u32[]{:S(2)}, u32[]{:S(2)}) collective-permute-start(bf16[96,384]{1,0:T(8,128)(2,1)S(1)} %get-tuple-element.7), channel_id=1, source_target_pairs={{0,3},{1,2},{2,1},{3,0},{4,7},{5,6},{6,5},{7,4},{8,11},{9,10},{10,... | collective-permute-start | bytes 221192 | tf_op jit(solution)/shard_map/ppermute | solution.py:67
  23.7 3.0 %collective-permute-done.2 = bf16[96,384]{1,0:T(8,128)(2,1)S(1)} collective-permute-done((bf16[96,384]{1,0:T(8,128)(2,1)S(1)}, bf16[96,384]{1,0:T(8,128)(2,1)S(1)}, u32[]{:S(2)}, u32[]{:S(2)}) %collective-permute-start.2) | collective-permute-done | bytes 73760 | tf_op jit(solution)/shard_map/ppermute | solution.py:67
  26.7 2.6 %collective-permute-start.6 = (bf16[288,384]{1,0:T(8,128)(2,1)S(1)}, bf16[288,384]{1,0:T(8,128)(2,1)S(1)}, u32[]{:S(2)}, u32[]{:S(2)}) collective-permute-start(bf16[288,384]{1,0:T(8,128)(2,1)S(1)} %constant_dynamic-update-slice_fusion), channel_id=1, source_target_pairs={{0,24},{4,28},{8,16},{12,20},{16,8},{20,12},{24,0},{28,4},{1,25},{... | collective-permute-start | bytes 663560 | tf_op jit(solution)/shard_map/ppermute | solution.py:82
  29.4 3.2 %collective-permute-start.18 = (bf16[256,384]{1,0:T(8,128)(2,1)S(1)}, bf16[256,384]{1,0:T(8,128)(2,1)S(1)}, u32[]{:S(2)}, u32[]{:S(2)}) collective-permute-start(bf16[256,384]{1,0:T(8,128)(2,1)S(1)} %slice.112), channel_id=1, source_target_pairs={{0,3},{1,2},{2,1},{3,0},{4,7},{5,6},{6,5},{7,4},{8,11},{9,10},{10,... | collective-permute-start | bytes 589832 | tf_op jit(solution)/shard_map/ppermute | solution.py:76
  32.6 0.3 fusion.15
  32.9 0.8 collective-permute-done.6
  33.6 1.6 %collective-permute-start.5 = (bf16[288,384]{1,0:T(8,128)(2,1)S(1)}, bf16[288,384]{1,0:T(8,128)(2,1)S(1)}, u32[]{:S(2)}, u32[]{:S(2)}) collective-permute-start(bf16[288,384]{1,0:T(8,128)(2,1)S(1)} %constant_dynamic-update-slice_fusion), channel_id=1, source_target_pairs={{0,16},{4,20},{8,24},{12,28},{16,0},{20,4},{24,8},{28,12},{1,17},{... | collective-permute-start | bytes 663560 | tf_op jit(solution)/shard_map/ppermute | solution.py:82
  35.3 4.3 %collective-permute-done.5 = bf16[288,384]{1,0:T(8,128)(2,1)S(1)} collective-permute-done((bf16[288,384]{1,0:T(8,128)(2,1)S(1)}, bf16[288,384]{1,0:T(8,128)(2,1)S(1)}, u32[]{:S(2)}, u32[]{:S(2)}) %collective-permute-start.5) | collective-permute-done | bytes 221216 | tf_op jit(solution)/shard_map/ppermute | solution.py:82
  39.6 1.6 %collective-permute-start.4 = (bf16[288,384]{1,0:T(8,128)(2,1)S(1)}, bf16[288,384]{1,0:T(8,128)(2,1)S(1)}, u32[]{:S(2)}, u32[]{:S(2)}) collective-permute-start(bf16[288,384]{1,0:T(8,128)(2,1)S(1)} %constant_dynamic-update-slice_fusion), channel_id=1, source_target_pairs={{0,8},{4,12},{8,0},{12,4},{16,24},{20,28},{24,16},{28,20},{1,9},{5... | collective-permute-start | bytes 663560 | tf_op jit(solution)/shard_map/ppermute | solution.py:82
  41.2 0.7 collective-permute-start.20
  41.8 3.7 %collective-permute-done.4 = bf16[288,384]{1,0:T(8,128)(2,1)S(1)} collective-permute-done((bf16[288,384]{1,0:T(8,128)(2,1)S(1)}, bf16[288,384]{1,0:T(8,128)(2,1)S(1)}, u32[]{:S(2)}, u32[]{:S(2)}) %collective-permute-start.4) | collective-permute-done | bytes 221216 | tf_op jit(solution)/shard_map/ppermute | solution.py:82
  45.5 0.6 collective-permute-start.17
  46.1 0.7 collective-permute-done.8
  47.0 0.3 convolution_add_fusion.1
  47.3 0.8 collective-permute-done.10
  48.3 0.3 fusion.22
  48.6 0.8 collective-permute-done.12
  49.4 0.3 fusion.26
  49.8 0.7 collective-permute-start.13
  50.5 0.4 fusion
  50.9 4.1 %collective-permute-start.19 = (bf16[256,384]{1,0:T(8,128)(2,1)S(1)}, bf16[256,384]{1,0:T(8,128)(2,1)S(1)}, u32[]{:S(2)}, u32[]{:S(2)}) collective-permute-start(bf16[256,384]{1,0:T(8,128)(2,1)S(1)} %collective-permute-done.18), channel_id=1, source_target_pairs={{0,4},{4,0},{8,12},{12,8},{16,20},{20,16},{24,28},{28,24},{1,5},{5... | collective-permute-start | bytes 589832 | tf_op jit(solution)/shard_map/ppermute | solution.py:95
  55.1 4.6 %collective-permute-done.22 = bf16[256,384]{1,0:T(8,128)(2,1)S(1)} collective-permute-done((bf16[256,384]{1,0:T(8,128)(2,1)S(1)}, bf16[256,384]{1,0:T(8,128)(2,1)S(1)}, u32[]{:S(2)}, u32[]{:S(2)}) %collective-permute-start.22) | collective-permute-done | bytes 196640 | tf_op jit(solution)/shard_map/ppermute | solution.py:76
  59.7 1.6 %collective-permute-start.14 = (bf16[96,256]{1,0:T(8,128)(2,1)S(1)}, bf16[96,256]{1,0:T(8,128)(2,1)S(1)}, u32[]{:S(2)}, u32[]{:S(2)}) collective-permute-start(bf16[96,256]{1,0:T(8,128)(2,1)S(1)} %get-tuple-element.31), channel_id=1, source_target_pairs={{0,8},{1,9},{2,10},{3,11},{4,13},{5,12},{6,15},{7,14},{8,0},{9,1},... | collective-permute-start | bytes 147464 | tf_op jit(solution)/shard_map/ppermute | solution.py:108
  61.3 1.6 %collective-permute-start.15 = (bf16[96,256]{1,0:T(8,128)(2,1)S(1)}, bf16[96,256]{1,0:T(8,128)(2,1)S(1)}, u32[]{:S(2)}, u32[]{:S(2)}) collective-permute-start(bf16[96,256]{1,0:T(8,128)(2,1)S(1)} %get-tuple-element.30), channel_id=1, source_target_pairs={{0,16},{1,17},{2,18},{3,19},{4,21},{5,20},{6,23},{7,22},{8,24},{9,... | collective-permute-start | bytes 147464 | tf_op jit(solution)/shard_map/ppermute | solution.py:108
  62.9 0.9 %collective-permute-done.14 = bf16[96,256]{1,0:T(8,128)(2,1)S(1)} collective-permute-done((bf16[96,256]{1,0:T(8,128)(2,1)S(1)}, bf16[96,256]{1,0:T(8,128)(2,1)S(1)}, u32[]{:S(2)}, u32[]{:S(2)}) %collective-permute-start.14) | collective-permute-done | bytes 49184 | tf_op jit(solution)/shard_map/ppermute | solution.py:108
  63.8 2.6 %collective-permute-start.16 = (bf16[96,256]{1,0:T(8,128)(2,1)S(1)}, bf16[96,256]{1,0:T(8,128)(2,1)S(1)}, u32[]{:S(2)}, u32[]{:S(2)}) collective-permute-start(bf16[96,256]{1,0:T(8,128)(2,1)S(1)} %get-tuple-element.29), channel_id=1, source_target_pairs={{0,24},{1,25},{2,26},{3,27},{4,29},{5,28},{6,31},{7,30},{8,16},{9,... | collective-permute-start | bytes 147464 | tf_op jit(solution)/shard_map/ppermute | solution.py:108
  66.4 0.4 convolution_add_fusion
  66.9 0.4 fusion.7
  67.4 0.4 fusion.11
  68.1 0.6 collective-permute-start.26
  68.7 0.7 collective-permute-done.16
  69.3 0.7 collective-permute-start.24
  70.0 1.6 %collective-permute-start.25 = (bf16[96,512]{1,0:T(8,128)(2,1)S(1)}, bf16[96,512]{1,0:T(8,128)(2,1)S(1)}, u32[]{:S(2)}, u32[]{:S(2)}) collective-permute-start(bf16[96,512]{1,0:T(8,128)(2,1)S(1)} %get-tuple-element.14), channel_id=1, source_target_pairs={{0,8},{1,9},{2,10},{3,11},{4,13},{5,12},{6,15},{7,14},{8,0},{9,1},... | collective-permute-start | bytes 294920 | tf_op jit(solution)/shard_map/ppermute | solution.py:108
  71.6 1.5 %collective-permute-start.27 = (bf16[96,512]{1,0:T(8,128)(2,1)S(1)}, bf16[96,512]{1,0:T(8,128)(2,1)S(1)}, u32[]{:S(2)}, u32[]{:S(2)}) collective-permute-start(bf16[96,512]{1,0:T(8,128)(2,1)S(1)} %get-tuple-element.12), channel_id=1, source_target_pairs={{0,24},{1,25},{2,26},{3,27},{4,29},{5,28},{6,31},{7,30},{8,16},{9,... | collective-permute-start | bytes 294920 | tf_op jit(solution)/shard_map/ppermute | solution.py:108
  73.1 6.1 %collective-permute-done.27 = bf16[96,512]{1,0:T(8,128)(2,1)S(1)} collective-permute-done((bf16[96,512]{1,0:T(8,128)(2,1)S(1)}, bf16[96,512]{1,0:T(8,128)(2,1)S(1)}, u32[]{:S(2)}, u32[]{:S(2)}) %collective-permute-start.27) | collective-permute-done | bytes 98336 | tf_op jit(solution)/shard_map/ppermute | solution.py:108
  79.6 1.4 %collective-permute-done.28.refs_8_ = bf16[4,48,768]{2,1,0:T(8,128)(2,1)S(1)} collective-permute-done((bf16[4,48,768]{2,1,0:T(8,128)(2,1)S(1)}, bf16[4,48,768]{2,1,0:T(8,128)(2,1)S(1)}, u32[]{:S(2)}, u32[]{:S(2)}) %collective-permute-start.28) | collective-permute-done | bytes 294944 | tf_op jit(solution)/shard_map/ppermute | solution.py:112
  81.1 1.5 %shard_map.28 = bf16[3,48,2048]{2,1,0:T(8,128)(2,1)} custom-call(s32[16]{0:T(128)S(1)} %stack.82.place, bf16[48,256]{1,0:T(8,128)(2,1)S(1)} %get-tuple-element.42.refs_0_, bf16[48,256]{1,0:T(8,128)(2,1)S(1)} %get-tuple-element.44.refs_1_, bf16[48,256]{1,0:T(8,128)(2,1)S(1)} %get-tuple-element.46.refs_2_, bf16[48,256]{1,0:T(8,128)(2,1)S(1)} %get-tuple-element.48.refs_3_, ...), custom_call_target="tpu_custom_call" | custom-call | tf_op jit(solution)/shard_map/pallas_call | solution.py:120
  (53 shorter events, 1.6 us)
Async XLA Ops:
  1.3 39.8 %collective-permute-start.7 = (bf16[128,384]{1,0:T(8,128)(2,1)S(1)}, bf16[128,384]{1,0:T(8,128)(2,1)S(1)}, u32[]{:S(2)}, u32[]{:S(2)}) collective-permute-start(bf16[128,384]{1,0:T(8,128)(2,1)S(1)} %slice.100), channel_id=1, source_target_pairs={{0,3},{1,2},{2,1},{3,0},{4,7},{5,6},{6,5},{7,4},{8,11},{9,10},{10,... | collective-permute-start | bytes 294920 | tf_op jit(solution)/shard_map/ppermute | solution.py:76
  6.5 39.1 %collective-permute-start.9 = (bf16[128,384]{1,0:T(8,128)(2,1)S(1)}, bf16[128,384]{1,0:T(8,128)(2,1)S(1)}, u32[]{:S(2)}, u32[]{:S(2)}) collective-permute-start(bf16[128,384]{1,0:T(8,128)(2,1)S(1)} %slice.100), channel_id=1, source_target_pairs={{0,1},{1,0},{2,3},{3,2},{4,5},{5,4},{6,7},{7,6},{8,9},{9,8},{10,11... | collective-permute-start | bytes 294920 | tf_op jit(solution)/shard_map/ppermute | solution.py:76
  6.7 22.6 %collective-permute-start.3 = (bf16[128,384]{1,0:T(8,128)(2,1)S(1)}, bf16[128,384]{1,0:T(8,128)(2,1)S(1)}, u32[]{:S(2)}, u32[]{:S(2)}) collective-permute-start(bf16[128,384]{1,0:T(8,128)(2,1)S(1)} %slice.96), channel_id=1, source_target_pairs={{0,4},{4,0},{8,12},{12,8},{16,20},{20,16},{24,28},{28,24},{1,5},{5... | collective-permute-start | bytes 294920 | tf_op jit(solution)/shard_map/ppermute | solution.py:95
  6.8 40.5 %collective-permute-start.11 = (bf16[128,384]{1,0:T(8,128)(2,1)S(1)}, bf16[128,384]{1,0:T(8,128)(2,1)S(1)}, u32[]{:S(2)}, u32[]{:S(2)}) collective-permute-start(bf16[128,384]{1,0:T(8,128)(2,1)S(1)} %slice.96), channel_id=1, source_target_pairs={{0,2},{1,3},{2,0},{3,1},{4,6},{5,7},{6,4},{7,5},{8,10},{9,11},{10,... | collective-permute-start | bytes 294920 | tf_op jit(solution)/shard_map/ppermute | solution.py:76
  8.5 6.7 %collective-permute-start = (bf16[96,384]{1,0:T(8,128)(2,1)S(1)}, bf16[96,384]{1,0:T(8,128)(2,1)S(1)}, u32[]{:S(2)}, u32[]{:S(2)}) collective-permute-start(bf16[96,384]{1,0:T(8,128)(2,1)S(1)} %get-tuple-element.8), channel_id=1, source_target_pairs={{0,1},{1,0},{2,3},{3,2},{4,5},{5,4},{6,7},{7,6},{8,9},{9,8},{10,11... | collective-permute-start | bytes 221192 | tf_op jit(solution)/shard_map/ppermute | solution.py:67
  15.2 5.3 %collective-permute-start.1 = (bf16[96,384]{1,0:T(8,128)(2,1)S(1)}, bf16[96,384]{1,0:T(8,128)(2,1)S(1)}, u32[]{:S(2)}, u32[]{:S(2)}) collective-permute-start(bf16[96,384]{1,0:T(8,128)(2,1)S(1)} %get-tuple-element.9), channel_id=1, source_target_pairs={{0,2},{1,3},{2,0},{3,1},{4,6},{5,7},{6,4},{7,5},{8,10},{9,11},{10,... | collective-permute-start | bytes 221192 | tf_op jit(solution)/shard_map/ppermute | solution.py:67
  20.4 6.2 %collective-permute-start.2 = (bf16[96,384]{1,0:T(8,128)(2,1)S(1)}, bf16[96,384]{1,0:T(8,128)(2,1)S(1)}, u32[]{:S(2)}, u32[]{:S(2)}) collective-permute-start(bf16[96,384]{1,0:T(8,128)(2,1)S(1)} %get-tuple-element.7), channel_id=1, source_target_pairs={{0,3},{1,2},{2,1},{3,0},{4,7},{5,6},{6,5},{7,4},{8,11},{9,10},{10,... | collective-permute-start | bytes 221192 | tf_op jit(solution)/shard_map/ppermute | solution.py:67
  26.7 6.9 %collective-permute-start.6 = (bf16[288,384]{1,0:T(8,128)(2,1)S(1)}, bf16[288,384]{1,0:T(8,128)(2,1)S(1)}, u32[]{:S(2)}, u32[]{:S(2)}) collective-permute-start(bf16[288,384]{1,0:T(8,128)(2,1)S(1)} %constant_dynamic-update-slice_fusion), channel_id=1, source_target_pairs={{0,24},{4,28},{8,16},{12,20},{16,8},{20,12},{24,0},{28,4},{1,25},{... | collective-permute-start | bytes 663560 | tf_op jit(solution)/shard_map/ppermute | solution.py:82
  29.4 21.5 %collective-permute-start.18 = (bf16[256,384]{1,0:T(8,128)(2,1)S(1)}, bf16[256,384]{1,0:T(8,128)(2,1)S(1)}, u32[]{:S(2)}, u32[]{:S(2)}) collective-permute-start(bf16[256,384]{1,0:T(8,128)(2,1)S(1)} %slice.112), channel_id=1, source_target_pairs={{0,3},{1,2},{2,1},{3,0},{4,7},{5,6},{6,5},{7,4},{8,11},{9,10},{10,... | collective-permute-start | bytes 589832 | tf_op jit(solution)/shard_map/ppermute | solution.py:76
  33.6 5.9 %collective-permute-start.5 = (bf16[288,384]{1,0:T(8,128)(2,1)S(1)}, bf16[288,384]{1,0:T(8,128)(2,1)S(1)}, u32[]{:S(2)}, u32[]{:S(2)}) collective-permute-start(bf16[288,384]{1,0:T(8,128)(2,1)S(1)} %constant_dynamic-update-slice_fusion), channel_id=1, source_target_pairs={{0,16},{4,20},{8,24},{12,28},{16,0},{20,4},{24,8},{28,12},{1,17},{... | collective-permute-start | bytes 663560 | tf_op jit(solution)/shard_map/ppermute | solution.py:82
  39.6 5.9 %collective-permute-start.4 = (bf16[288,384]{1,0:T(8,128)(2,1)S(1)}, bf16[288,384]{1,0:T(8,128)(2,1)S(1)}, u32[]{:S(2)}, u32[]{:S(2)}) collective-permute-start(bf16[288,384]{1,0:T(8,128)(2,1)S(1)} %constant_dynamic-update-slice_fusion), channel_id=1, source_target_pairs={{0,8},{4,12},{8,0},{12,4},{16,24},{20,28},{24,16},{28,20},{1,9},{5... | collective-permute-start | bytes 663560 | tf_op jit(solution)/shard_map/ppermute | solution.py:82
  41.2 13.9 %collective-permute-start.20 = (bf16[256,384]{1,0:T(8,128)(2,1)S(1)}, bf16[256,384]{1,0:T(8,128)(2,1)S(1)}, u32[]{:S(2)}, u32[]{:S(2)}) collective-permute-start(bf16[256,384]{1,0:T(8,128)(2,1)S(1)} %slice.112), channel_id=1, source_target_pairs={{0,1},{1,0},{2,3},{3,2},{4,5},{5,4},{6,7},{7,6},{8,9},{9,8},{10,11... | collective-permute-start | bytes 589832 | tf_op jit(solution)/shard_map/ppermute | solution.py:76
  45.5 1.3 %collective-permute-start.8 = (bf16[128,384]{1,0:T(8,128)(2,1)S(1)}, bf16[128,384]{1,0:T(8,128)(2,1)S(1)}, u32[]{:S(2)}, u32[]{:S(2)}) collective-permute-start(bf16[128,384]{1,0:T(8,128)(2,1)S(1)} %collective-permute-done.7), channel_id=1, source_target_pairs={{0,4},{4,0},{8,12},{12,8},{16,20},{20,16},{24,28},{28,24},{1,5},{5... | collective-permute-start | bytes 294920 | tf_op jit(solution)/shard_map/ppermute | solution.py:95
  45.5 4.9 %collective-permute-start.17 = (bf16[256,384]{1,0:T(8,128)(2,1)S(1)}, bf16[256,384]{1,0:T(8,128)(2,1)S(1)}, u32[]{:S(2)}, u32[]{:S(2)}) collective-permute-start(bf16[256,384]{1,0:T(8,128)(2,1)S(1)} %slice.111), channel_id=1, source_target_pairs={{0,4},{4,0},{8,12},{12,8},{16,20},{20,16},{24,28},{28,24},{1,5},{5... | collective-permute-start | bytes 589832 | tf_op jit(solution)/shard_map/ppermute | solution.py:95
  46.8 1.3 %collective-permute-start.10 = (bf16[128,384]{1,0:T(8,128)(2,1)S(1)}, bf16[128,384]{1,0:T(8,128)(2,1)S(1)}, u32[]{:S(2)}, u32[]{:S(2)}) collective-permute-start(bf16[128,384]{1,0:T(8,128)(2,1)S(1)} %collective-permute-done.9), channel_id=1, source_target_pairs={{0,4},{4,0},{8,12},{12,8},{16,20},{20,16},{24,28},{28,24},{1,5},{5... | collective-permute-start | bytes 294920 | tf_op jit(solution)/shard_map/ppermute | solution.py:95
  47.3 12.4 %collective-permute-start.22 = (bf16[256,384]{1,0:T(8,128)(2,1)S(1)}, bf16[256,384]{1,0:T(8,128)(2,1)S(1)}, u32[]{:S(2)}, u32[]{:S(2)}) collective-permute-start(bf16[256,384]{1,0:T(8,128)(2,1)S(1)} %slice.111), channel_id=1, source_target_pairs={{0,2},{1,3},{2,0},{3,1},{4,6},{5,7},{6,4},{7,5},{8,10},{9,11},{10,... | collective-permute-start | bytes 589832 | tf_op jit(solution)/shard_map/ppermute | solution.py:76
  48.1 1.3 %collective-permute-start.12 = (bf16[128,384]{1,0:T(8,128)(2,1)S(1)}, bf16[128,384]{1,0:T(8,128)(2,1)S(1)}, u32[]{:S(2)}, u32[]{:S(2)}) collective-permute-start(bf16[128,384]{1,0:T(8,128)(2,1)S(1)} %collective-permute-done.11), channel_id=1, source_target_pairs={{0,4},{4,0},{8,12},{12,8},{16,20},{20,16},{24,28},{28,24},{1,5},{5... | collective-permute-start | bytes 294920 | tf_op jit(solution)/shard_map/ppermute | solution.py:95
  49.8 11.5 %collective-permute-start.13 = (bf16[96,256]{1,0:T(8,128)(2,1)S(1)}, bf16[96,256]{1,0:T(8,128)(2,1)S(1)}, u32[]{:S(2)}, u32[]{:S(2)}) collective-permute-start(bf16[96,256]{1,0:T(8,128)(2,1)S(1)} %get-tuple-element.32), channel_id=1, source_target_pairs={{0,0},{1,1},{2,2},{3,3},{4,5},{5,4},{6,7},{7,6},{8,8},{9,9},{10,10... | collective-permute-start | bytes 147464 | tf_op jit(solution)/shard_map/ppermute | solution.py:108
  50.9 15.6 %collective-permute-start.19 = (bf16[256,384]{1,0:T(8,128)(2,1)S(1)}, bf16[256,384]{1,0:T(8,128)(2,1)S(1)}, u32[]{:S(2)}, u32[]{:S(2)}) collective-permute-start(bf16[256,384]{1,0:T(8,128)(2,1)S(1)} %collective-permute-done.18), channel_id=1, source_target_pairs={{0,4},{4,0},{8,12},{12,8},{16,20},{20,16},{24,28},{28,24},{1,5},{5... | collective-permute-start | bytes 589832 | tf_op jit(solution)/shard_map/ppermute | solution.py:95
  55.0 11.8 %collective-permute-start.21 = (bf16[256,384]{1,0:T(8,128)(2,1)S(1)}, bf16[256,384]{1,0:T(8,128)(2,1)S(1)}, u32[]{:S(2)}, u32[]{:S(2)}) collective-permute-start(bf16[256,384]{1,0:T(8,128)(2,1)S(1)} %collective-permute-done.20), channel_id=1, source_target_pairs={{0,4},{4,0},{8,12},{12,8},{16,20},{20,16},{24,28},{28,24},{1,5},{5... | collective-permute-start | bytes 589832 | tf_op jit(solution)/shard_map/ppermute | solution.py:95
  59.7 7.7 %collective-permute-start.23 = (bf16[256,384]{1,0:T(8,128)(2,1)S(1)}, bf16[256,384]{1,0:T(8,128)(2,1)S(1)}, u32[]{:S(2)}, u32[]{:S(2)}) collective-permute-start(bf16[256,384]{1,0:T(8,128)(2,1)S(1)} %collective-permute-done.22), channel_id=1, source_target_pairs={{0,4},{4,0},{8,12},{12,8},{16,20},{20,16},{24,28},{28,24},{1,5},{5... | collective-permute-start | bytes 589832 | tf_op jit(solution)/shard_map/ppermute | solution.py:95
  59.7 4.1 %collective-permute-start.14 = (bf16[96,256]{1,0:T(8,128)(2,1)S(1)}, bf16[96,256]{1,0:T(8,128)(2,1)S(1)}, u32[]{:S(2)}, u32[]{:S(2)}) collective-permute-start(bf16[96,256]{1,0:T(8,128)(2,1)S(1)} %get-tuple-element.31), channel_id=1, source_target_pairs={{0,8},{1,9},{2,10},{3,11},{4,13},{5,12},{6,15},{7,14},{8,0},{9,1},... | collective-permute-start | bytes 147464 | tf_op jit(solution)/shard_map/ppermute | solution.py:108
  61.3 5.1 %collective-permute-start.15 = (bf16[96,256]{1,0:T(8,128)(2,1)S(1)}, bf16[96,256]{1,0:T(8,128)(2,1)S(1)}, u32[]{:S(2)}, u32[]{:S(2)}) collective-permute-start(bf16[96,256]{1,0:T(8,128)(2,1)S(1)} %get-tuple-element.30), channel_id=1, source_target_pairs={{0,16},{1,17},{2,18},{3,19},{4,21},{5,20},{6,23},{7,22},{8,24},{9,... | collective-permute-start | bytes 147464 | tf_op jit(solution)/shard_map/ppermute | solution.py:108
  63.8 5.5 %collective-permute-start.16 = (bf16[96,256]{1,0:T(8,128)(2,1)S(1)}, bf16[96,256]{1,0:T(8,128)(2,1)S(1)}, u32[]{:S(2)}, u32[]{:S(2)}) collective-permute-start(bf16[96,256]{1,0:T(8,128)(2,1)S(1)} %get-tuple-element.29), channel_id=1, source_target_pairs={{0,24},{1,25},{2,26},{3,27},{4,29},{5,28},{6,31},{7,30},{8,16},{9,... | collective-permute-start | bytes 147464 | tf_op jit(solution)/shard_map/ppermute | solution.py:108
  68.1 5.1 %collective-permute-start.26 = (bf16[96,512]{1,0:T(8,128)(2,1)S(1)}, bf16[96,512]{1,0:T(8,128)(2,1)S(1)}, u32[]{:S(2)}, u32[]{:S(2)}) collective-permute-start(bf16[96,512]{1,0:T(8,128)(2,1)S(1)} %get-tuple-element.13), channel_id=1, source_target_pairs={{0,16},{1,17},{2,18},{3,19},{4,21},{5,20},{6,23},{7,22},{8,24},{9,... | collective-permute-start | bytes 294920 | tf_op jit(solution)/shard_map/ppermute | solution.py:108
  69.3 10.0 %collective-permute-start.24 = (bf16[96,512]{1,0:T(8,128)(2,1)S(1)}, bf16[96,512]{1,0:T(8,128)(2,1)S(1)}, u32[]{:S(2)}, u32[]{:S(2)}) collective-permute-start(bf16[96,512]{1,0:T(8,128)(2,1)S(1)} %get-tuple-element.15), channel_id=1, source_target_pairs={{0,0},{1,1},{2,2},{3,3},{4,5},{5,4},{6,7},{7,6},{8,8},{9,9},{10,10... | collective-permute-start | bytes 294920 | tf_op jit(solution)/shard_map/ppermute | solution.py:108
  70.0 9.3 %collective-permute-start.25 = (bf16[96,512]{1,0:T(8,128)(2,1)S(1)}, bf16[96,512]{1,0:T(8,128)(2,1)S(1)}, u32[]{:S(2)}, u32[]{:S(2)}) collective-permute-start(bf16[96,512]{1,0:T(8,128)(2,1)S(1)} %get-tuple-element.14), channel_id=1, source_target_pairs={{0,8},{1,9},{2,10},{3,11},{4,13},{5,12},{6,15},{7,14},{8,0},{9,1},... | collective-permute-start | bytes 294920 | tf_op jit(solution)/shard_map/ppermute | solution.py:108
  71.6 7.6 %collective-permute-start.27 = (bf16[96,512]{1,0:T(8,128)(2,1)S(1)}, bf16[96,512]{1,0:T(8,128)(2,1)S(1)}, u32[]{:S(2)}, u32[]{:S(2)}) collective-permute-start(bf16[96,512]{1,0:T(8,128)(2,1)S(1)} %get-tuple-element.12), channel_id=1, source_target_pairs={{0,24},{1,25},{2,26},{3,27},{4,29},{5,28},{6,31},{7,30},{8,16},{9,... | collective-permute-start | bytes 294920 | tf_op jit(solution)/shard_map/ppermute | solution.py:108
  79.4 1.6 %collective-permute-start.28 = (bf16[4,48,768]{2,1,0:T(8,128)(2,1)S(1)}, bf16[4,48,768]{2,1,0:T(8,128)(2,1)S(1)}, u32[]{:S(2)}, u32[]{:S(2)}) collective-permute-start(bf16[4,48,768]{2,1,0:T(8,128)(2,1)S(1)} %pad_maximum_fusion.4), channel_id=1, source_target_pairs={{0,4},{4,0},{8,12},{12,8},{16,20},{20,16},{24,28},{28,24},{1,5},{5... | collective-permute-start | bytes 884744 | tf_op jit(solution)/shard_map/ppermute | solution.py:112

commit v4 on v3

--- a/solution.py
+++ b/solution.py
@@ -16,22 +16,34 @@
     return index ^ step if size & (size - 1) == 0 else (index - step + size) % size
 
 
-def assemble(chunks, place, *refs):
-    *kept, fetched, out = refs
+def assemble(chunks, *refs):
+    *kept, fetched, out, whole, sems = refs
     many = len(kept) // len(chunks)
-    half = out.shape[2] // (4 * many)
-
-    def put(spot, comp, values):
-        out[comp, :, pl.ds(pl.multiple_of(place[spot] * half, half), half)] = values
-
+    x, z = lax.axis_index("gx"), lax.axis_index("gy")
+    chip, core, q = lax.div(x, 2), lax.rem(x, 2), lax.rem(z, 2)
+    place = [
+        (hop(chip, j, many) * 2 + (core ^ via ^ e)) * 2 + (q ^ core ^ via)
+        for via in range(2)
+        for j in range(many)
+        for e in range(2)
+    ]
+    half = whole.shape[2] // (4 * many)
+    copies = []
     for c, (first, end) in enumerate(chunks):
-        for number in range(many):
-            for other in range(2):
-                for comp in range(first, end):
+        for comp in range(first, end):
+            for number in range(many):
+                for other in range(2):
                     column = (other * (end - first) + comp - first) * half
-                    put(2 * number + other, comp, kept[c * many + number][:, column : column + half])
-                    column += 2 * first * half
-                    put(2 * (many + number) + other, comp, fetched[number, :, column : column + half])
+                    beside = column + 2 * first * half
+                    for spot, values in (
+                        (2 * number + other, kept[c * many + number][:, column : column + half]),
+                        (2 * (many + number) + other, fetched[number, :, beside : beside + half]),
+                    ):
+                        whole[comp, :, pl.ds(pl.multiple_of(place[spot] * half, half), half)] = values
+            copies.append(pltpu.make_async_copy(whole.at[comp], out.at[comp], sems.at[comp]))
+            copies[-1].start()
+    for copy in copies:
+        copy.wait()
 
 
 def direct(products, operator):
@@ -110,20 +122,18 @@
             passed.append(lax.dynamic_slice_in_dim(landed, (1 - core) * rows, rows, 0))
     passed = [jnp.concatenate(passed[j::chips], axis=1) for j in range(chips)]
     fetched = lax.ppermute(jnp.stack(passed), "gx", swap)
-    spots = [
-        (hop(chip, j, chips) * 2 + (core ^ via ^ e)) * 2 + (q ^ core ^ via)
-        for via in range(2)
-        for j in range(chips)
-        for e in range(2)
-    ]
-    smem, vmem = (pl.BlockSpec(memory_space=m) for m in (pltpu.SMEM, pltpu.VMEM))
+    vmem = pl.BlockSpec(memory_space=pltpu.VMEM)
     out = pl.pallas_call(
         functools.partial(assemble, [chunk[:2] for chunk in chunks]),
         out_shape=jax.ShapeDtypeStruct((comps, rows, wide * modes), jnp.bfloat16),
-        in_specs=[smem] + [vmem] * (len(kept) + 1),
-        out_specs=vmem,
+        in_specs=[vmem] * (len(kept) + 1),
+        out_specs=pl.BlockSpec(memory_space=pl.ANY),
+        scratch_shapes=[
+            pltpu.VMEM((comps, rows, wide * modes), jnp.bfloat16),
+            pltpu.SemaphoreType.DMA((comps,)),
+        ],
         compiler_params=pltpu.CompilerParams(vmem_limit_bytes=8 << 20),
-    )(jnp.stack(spots).astype(jnp.int32), *kept, fetched)
+    )(*kept, fetched)
     return out.transpose(1, 0, 2)
 
 

time: 82.8 us -> 82.2 us (level)
  no operation moved by 1% of the time
where the time goes in v4:
time: 82.2 us; the launch traced here: 81.9 us
  starting transfers between devices  37.7 us (46%)
  waiting for transfers between devices  35.9 us (44%)
  local copies, waits for them, and re-layouts  3.83 us (5%)
  matrix products  2.74 us (3%)
  Pallas kernels  0.88 us (1%)
    ppermute x3, waiting for transfers between devices, paired(): shares[k] = lax.ppermute(pieces[k], 'gy', [(i, i ^ k) for i in range(deep)])  11 us
    ppermute x8, starting transfers between devices, paired(): landed = lax.ppermute(result[j], ('gx', 'gy'), pairs)  10.8 us
    ppermute x6, starting transfers between devices, paired(): lax.ppermute(halves[k % 2][a:b], 'gy', [(i, i ^ k) for i in range(deep)])  9.78 us
    ppermute x3, waiting for transfers between devices, paired(): gathered.append(lax.ppermute(arrived, 'gx', pairs))  8.75 us
    ppermute x8, waiting for transfers between devices, paired(): landed = lax.ppermute(result[j], ('gx', 'gy'), pairs)  7.71 us
    ppermute x3, starting transfers between devices, paired(): shares[k] = lax.ppermute(pieces[k], 'gy', [(i, i ^ k) for i in range(deep)])  6.08 us
    ppermute x3, starting transfers between devices, paired(): gathered.append(lax.ppermute(arrived, 'gx', pairs))  5.78 us
    ppermute x8, starting transfers between devices, paired(): theirs = lax.ppermute(ours, 'gx', swap)  5.2 us
  transfers between devices with their start and end apart: 29, of which 14 were waited for; matrix products, arithmetic and copies ran while one was open for 7% of the time, Pallas kernels for 0%

profile of v4, /device:TPU:0, one launch (start us, length us, event | category | flops | bytes accessed | tf_op | source)
XLA Modules:
  0.0 81.9 jit_solution(5763376281959074838)
XLA Ops:
  0.0 1.1 %constant_dynamic-slice_fusion.16 = (bf16[384,3,128]{2,0,1:T(8,128)(2,1)S(1)}, bf16[384,3,128]{2,0,1:T(8,128)(2,1)S(1)}) fusion(bf16[384,3,256]{2,0,1:T(8,128)(2,1)} %param.2, s32[]{:T(128)S(6)} %select_n.77, s32[]{:T(128)S(6)} %select_n.76), kind=kLoop, calls=%fused_computation.62 | loop fusion | bytes 1179656 | tf_op jit(solution)/shard_map/dynamic_slice | solution.py:82
  1.1 0.2 copy.6
  1.3 5.1 %collective-permute-start.7 = (bf16[128,384]{1,0:T(8,128)(2,1)S(1)}, bf16[128,384]{1,0:T(8,128)(2,1)S(1)}, u32[]{:S(2)}, u32[]{:S(2)}) collective-permute-start(bf16[128,384]{1,0:T(8,128)(2,1)S(1)} %slice.100), channel_id=1, source_target_pairs={{0,3},{1,2},{2,1},{3,0},{4,7},{5,6},{6,5},{7,4},{8,11},{9,10},{10,... | collective-permute-start | bytes 294920 | tf_op jit(solution)/shard_map/ppermute | solution.py:88
  6.5 0.2 copy.5
  6.8 0.7 collective-permute-start.11
  7.5 1.0 %constant_dynamic-slice_fusion.22 = (bf16[96,384]{1,0:T(8,128)(2,1)S(1)}, bf16[96,384]{1,0:T(8,128)(2,1)S(1)}, bf16[96,384]{1,0:T(8,128)(2,1)S(1)}) fusion(bf16[1536,384]{1,0:T(8,128)(2,1)} %param.3, s32[]{:T(128)S(6)} %select_n.70, s32[]{:T(128)S(6)} %select_n.68, s32[]{:T(128)S(6)} %select_n.69), kind=kLoop, calls=%fused_computation.68 | loop fusion | bytes 442380 | tf_op jit(solution)/shard_map/dynamic_slice | solution.py:75
  8.5 1.5 %collective-permute-start = (bf16[96,384]{1,0:T(8,128)(2,1)S(1)}, bf16[96,384]{1,0:T(8,128)(2,1)S(1)}, u32[]{:S(2)}, u32[]{:S(2)}) collective-permute-start(bf16[96,384]{1,0:T(8,128)(2,1)S(1)} %get-tuple-element.8), channel_id=1, source_target_pairs={{0,1},{1,0},{2,3},{3,2},{4,5},{5,4},{6,7},{7,6},{8,9},{9,8},{10,11... | collective-permute-start | bytes 221192 | tf_op jit(solution)/shard_map/ppermute | solution.py:79
  10.1 1.0 %constant_dynamic-slice_fusion.25 = bf16[384,384]{1,0:T(8,128)(2,1)S(1)} fusion(bf16[1536,384]{1,0:T(8,128)(2,1)} %param.3, s32[]{:T(128)S(6)} %select_n.66), kind=kLoop, calls=%fused_computation.71 | loop fusion | bytes 589828 | tf_op jit(solution)/shard_map/dynamic_slice | solution.py:95
  11.1 4.1 %collective-permute-done = bf16[96,384]{1,0:T(8,128)(2,1)S(1)} collective-permute-done((bf16[96,384]{1,0:T(8,128)(2,1)S(1)}, bf16[96,384]{1,0:T(8,128)(2,1)S(1)}, u32[]{:S(2)}, u32[]{:S(2)}) %collective-permute-start) | collective-permute-done | bytes 73760 | tf_op jit(solution)/shard_map/ppermute | solution.py:79
  15.2 1.3 %collective-permute-start.1 = (bf16[96,384]{1,0:T(8,128)(2,1)S(1)}, bf16[96,384]{1,0:T(8,128)(2,1)S(1)}, u32[]{:S(2)}, u32[]{:S(2)}) collective-permute-start(bf16[96,384]{1,0:T(8,128)(2,1)S(1)} %get-tuple-element.9), channel_id=1, source_target_pairs={{0,2},{1,3},{2,0},{3,1},{4,6},{5,7},{6,4},{7,5},{8,10},{9,11},{10,... | collective-permute-start | bytes 221192 | tf_op jit(solution)/shard_map/ppermute | solution.py:79
  16.5 3.9 %collective-permute-done.1 = bf16[96,384]{1,0:T(8,128)(2,1)S(1)} collective-permute-done((bf16[96,384]{1,0:T(8,128)(2,1)S(1)}, bf16[96,384]{1,0:T(8,128)(2,1)S(1)}, u32[]{:S(2)}, u32[]{:S(2)}) %collective-permute-start.1) | collective-permute-done | bytes 73760 | tf_op jit(solution)/shard_map/ppermute | solution.py:79
  20.4 3.2 %collective-permute-start.2 = (bf16[96,384]{1,0:T(8,128)(2,1)S(1)}, bf16[96,384]{1,0:T(8,128)(2,1)S(1)}, u32[]{:S(2)}, u32[]{:S(2)}) collective-permute-start(bf16[96,384]{1,0:T(8,128)(2,1)S(1)} %get-tuple-element.7), channel_id=1, source_target_pairs={{0,3},{1,2},{2,1},{3,0},{4,7},{5,6},{6,5},{7,4},{8,11},{9,10},{10,... | collective-permute-start | bytes 221192 | tf_op jit(solution)/shard_map/ppermute | solution.py:79
  23.7 3.0 %collective-permute-done.2 = bf16[96,384]{1,0:T(8,128)(2,1)S(1)} collective-permute-done((bf16[96,384]{1,0:T(8,128)(2,1)S(1)}, bf16[96,384]{1,0:T(8,128)(2,1)S(1)}, u32[]{:S(2)}, u32[]{:S(2)}) %collective-permute-start.2) | collective-permute-done | bytes 73760 | tf_op jit(solution)/shard_map/ppermute | solution.py:79
  26.7 2.6 %collective-permute-start.6 = (bf16[288,384]{1,0:T(8,128)(2,1)S(1)}, bf16[288,384]{1,0:T(8,128)(2,1)S(1)}, u32[]{:S(2)}, u32[]{:S(2)}) collective-permute-start(bf16[288,384]{1,0:T(8,128)(2,1)S(1)} %constant_dynamic-update-slice_fusion), channel_id=1, source_target_pairs={{0,24},{4,28},{8,16},{12,20},{16,8},{20,12},{24,0},{28,4},{1,25},{... | collective-permute-start | bytes 663560 | tf_op jit(solution)/shard_map/ppermute | solution.py:94
  29.4 3.2 %collective-permute-start.18 = (bf16[256,384]{1,0:T(8,128)(2,1)S(1)}, bf16[256,384]{1,0:T(8,128)(2,1)S(1)}, u32[]{:S(2)}, u32[]{:S(2)}) collective-permute-start(bf16[256,384]{1,0:T(8,128)(2,1)S(1)} %slice.112), channel_id=1, source_target_pairs={{0,3},{1,2},{2,1},{3,0},{4,7},{5,6},{6,5},{7,4},{8,11},{9,10},{10,... | collective-permute-start | bytes 589832 | tf_op jit(solution)/shard_map/ppermute | solution.py:88
  32.6 0.3 fusion.15
  32.9 0.8 collective-permute-done.6
  33.6 1.6 %collective-permute-start.5 = (bf16[288,384]{1,0:T(8,128)(2,1)S(1)}, bf16[288,384]{1,0:T(8,128)(2,1)S(1)}, u32[]{:S(2)}, u32[]{:S(2)}) collective-permute-start(bf16[288,384]{1,0:T(8,128)(2,1)S(1)} %constant_dynamic-update-slice_fusion), channel_id=1, source_target_pairs={{0,16},{4,20},{8,24},{12,28},{16,0},{20,4},{24,8},{28,12},{1,17},{... | collective-permute-start | bytes 663560 | tf_op jit(solution)/shard_map/ppermute | solution.py:94
  35.3 4.3 %collective-permute-done.5 = bf16[288,384]{1,0:T(8,128)(2,1)S(1)} collective-permute-done((bf16[288,384]{1,0:T(8,128)(2,1)S(1)}, bf16[288,384]{1,0:T(8,128)(2,1)S(1)}, u32[]{:S(2)}, u32[]{:S(2)}) %collective-permute-start.5) | collective-permute-done | bytes 221216 | tf_op jit(solution)/shard_map/ppermute | solution.py:94
  39.6 1.6 %collective-permute-start.4 = (bf16[288,384]{1,0:T(8,128)(2,1)S(1)}, bf16[288,384]{1,0:T(8,128)(2,1)S(1)}, u32[]{:S(2)}, u32[]{:S(2)}) collective-permute-start(bf16[288,384]{1,0:T(8,128)(2,1)S(1)} %constant_dynamic-update-slice_fusion), channel_id=1, source_target_pairs={{0,8},{4,12},{8,0},{12,4},{16,24},{20,28},{24,16},{28,20},{1,9},{5... | collective-permute-start | bytes 663560 | tf_op jit(solution)/shard_map/ppermute | solution.py:94
  41.2 0.7 collective-permute-start.20
  41.8 3.7 %collective-permute-done.4 = bf16[288,384]{1,0:T(8,128)(2,1)S(1)} collective-permute-done((bf16[288,384]{1,0:T(8,128)(2,1)S(1)}, bf16[288,384]{1,0:T(8,128)(2,1)S(1)}, u32[]{:S(2)}, u32[]{:S(2)}) %collective-permute-start.4) | collective-permute-done | bytes 221216 | tf_op jit(solution)/shard_map/ppermute | solution.py:94
  45.5 0.6 collective-permute-start.17
  46.1 0.7 collective-permute-done.8
  47.0 0.3 convolution_add_fusion.1
  47.3 0.8 collective-permute-done.10
  48.3 0.3 fusion.22
  48.6 0.8 collective-permute-done.12
  49.4 0.3 fusion.26
  49.8 0.7 collective-permute-start.13
  50.5 0.4 fusion
  50.9 4.2 %collective-permute-start.19 = (bf16[256,384]{1,0:T(8,128)(2,1)S(1)}, bf16[256,384]{1,0:T(8,128)(2,1)S(1)}, u32[]{:S(2)}, u32[]{:S(2)}) collective-permute-start(bf16[256,384]{1,0:T(8,128)(2,1)S(1)} %collective-permute-done.18), channel_id=1, source_target_pairs={{0,4},{4,0},{8,12},{12,8},{16,20},{20,16},{24,28},{28,24},{1,5},{5... | collective-permute-start | bytes 589832 | tf_op jit(solution)/shard_map/ppermute | solution.py:107
  55.1 4.6 %collective-permute-done.22 = bf16[256,384]{1,0:T(8,128)(2,1)S(1)} collective-permute-done((bf16[256,384]{1,0:T(8,128)(2,1)S(1)}, bf16[256,384]{1,0:T(8,128)(2,1)S(1)}, u32[]{:S(2)}, u32[]{:S(2)}) %collective-permute-start.22) | collective-permute-done | bytes 196640 | tf_op jit(solution)/shard_map/ppermute | solution.py:88
  59.7 1.6 %collective-permute-start.14 = (bf16[96,256]{1,0:T(8,128)(2,1)S(1)}, bf16[96,256]{1,0:T(8,128)(2,1)S(1)}, u32[]{:S(2)}, u32[]{:S(2)}) collective-permute-start(bf16[96,256]{1,0:T(8,128)(2,1)S(1)} %get-tuple-element.31), channel_id=1, source_target_pairs={{0,8},{1,9},{2,10},{3,11},{4,13},{5,12},{6,15},{7,14},{8,0},{9,1},... | collective-permute-start | bytes 147464 | tf_op jit(solution)/shard_map/ppermute | solution.py:120
  61.3 1.6 %collective-permute-start.15 = (bf16[96,256]{1,0:T(8,128)(2,1)S(1)}, bf16[96,256]{1,0:T(8,128)(2,1)S(1)}, u32[]{:S(2)}, u32[]{:S(2)}) collective-permute-start(bf16[96,256]{1,0:T(8,128)(2,1)S(1)} %get-tuple-element.30), channel_id=1, source_target_pairs={{0,16},{1,17},{2,18},{3,19},{4,21},{5,20},{6,23},{7,22},{8,24},{9,... | collective-permute-start | bytes 147464 | tf_op jit(solution)/shard_map/ppermute | solution.py:120
  62.9 0.9 %collective-permute-done.14 = bf16[96,256]{1,0:T(8,128)(2,1)S(1)} collective-permute-done((bf16[96,256]{1,0:T(8,128)(2,1)S(1)}, bf16[96,256]{1,0:T(8,128)(2,1)S(1)}, u32[]{:S(2)}, u32[]{:S(2)}) %collective-permute-start.14) | collective-permute-done | bytes 49184 | tf_op jit(solution)/shard_map/ppermute | solution.py:120
  63.8 2.6 %collective-permute-start.16 = (bf16[96,256]{1,0:T(8,128)(2,1)S(1)}, bf16[96,256]{1,0:T(8,128)(2,1)S(1)}, u32[]{:S(2)}, u32[]{:S(2)}) collective-permute-start(bf16[96,256]{1,0:T(8,128)(2,1)S(1)} %get-tuple-element.29), channel_id=1, source_target_pairs={{0,24},{1,25},{2,26},{3,27},{4,29},{5,28},{6,31},{7,30},{8,16},{9,... | collective-permute-start | bytes 147464 | tf_op jit(solution)/shard_map/ppermute | solution.py:120
  66.4 0.4 convolution_add_fusion
  66.9 0.4 fusion.7
  67.4 0.4 fusion.11
  68.1 0.6 collective-permute-start.26
  68.6 0.7 collective-permute-done.16
  69.3 0.7 collective-permute-start.24
  70.0 1.6 %collective-permute-start.25 = (bf16[96,512]{1,0:T(8,128)(2,1)S(1)}, bf16[96,512]{1,0:T(8,128)(2,1)S(1)}, u32[]{:S(2)}, u32[]{:S(2)}) collective-permute-start(bf16[96,512]{1,0:T(8,128)(2,1)S(1)} %get-tuple-element.14), channel_id=1, source_target_pairs={{0,8},{1,9},{2,10},{3,11},{4,13},{5,12},{6,15},{7,14},{8,0},{9,1},... | collective-permute-start | bytes 294920 | tf_op jit(solution)/shard_map/ppermute | solution.py:120
  71.6 1.5 %collective-permute-start.27 = (bf16[96,512]{1,0:T(8,128)(2,1)S(1)}, bf16[96,512]{1,0:T(8,128)(2,1)S(1)}, u32[]{:S(2)}, u32[]{:S(2)}) collective-permute-start(bf16[96,512]{1,0:T(8,128)(2,1)S(1)} %get-tuple-element.12), channel_id=1, source_target_pairs={{0,24},{1,25},{2,26},{3,27},{4,29},{5,28},{6,31},{7,30},{8,16},{9,... | collective-permute-start | bytes 294920 | tf_op jit(solution)/shard_map/ppermute | solution.py:120
  73.1 6.1 %collective-permute-done.27 = bf16[96,512]{1,0:T(8,128)(2,1)S(1)} collective-permute-done((bf16[96,512]{1,0:T(8,128)(2,1)S(1)}, bf16[96,512]{1,0:T(8,128)(2,1)S(1)}, u32[]{:S(2)}, u32[]{:S(2)}) %collective-permute-start.27) | collective-permute-done | bytes 98336 | tf_op jit(solution)/shard_map/ppermute | solution.py:120
  79.5 1.6 %collective-permute-done.28.refs_8_ = bf16[4,48,768]{2,1,0:T(8,128)(2,1)S(1)} collective-permute-done((bf16[4,48,768]{2,1,0:T(8,128)(2,1)S(1)}, bf16[4,48,768]{2,1,0:T(8,128)(2,1)S(1)}, u32[]{:S(2)}, u32[]{:S(2)}) %collective-permute-start.28) | collective-permute-done | bytes 294944 | tf_op jit(solution)/shard_map/ppermute | solution.py:124
  81.1 0.9 %shard_map.28 = bf16[3,48,2048]{2,1,0:T(8,128)(2,1)} custom-call(bf16[48,256]{1,0:T(8,128)(2,1)S(1)} %get-tuple-element.42.refs_0_, bf16[48,256]{1,0:T(8,128)(2,1)S(1)} %get-tuple-element.44.refs_1_, bf16[48,256]{1,0:T(8,128)(2,1)S(1)} %get-tuple-element.46.refs_2_, bf16[48,256]{1,0:T(8,128)(2,1)S(1)} %get-tuple-element.48.refs_3_, ...), custom_call_target="tpu_custom_call" | custom-call | tf_op jit(solution)/shard_map/pallas_call | solution.py:126
  (52 shorter events, 1.5 us)
Async XLA Ops:
  1.3 39.8 %collective-permute-start.7 = (bf16[128,384]{1,0:T(8,128)(2,1)S(1)}, bf16[128,384]{1,0:T(8,128)(2,1)S(1)}, u32[]{:S(2)}, u32[]{:S(2)}) collective-permute-start(bf16[128,384]{1,0:T(8,128)(2,1)S(1)} %slice.100), channel_id=1, source_target_pairs={{0,3},{1,2},{2,1},{3,0},{4,7},{5,6},{6,5},{7,4},{8,11},{9,10},{10,... | collective-permute-start | bytes 294920 | tf_op jit(solution)/shard_map/ppermute | solution.py:88
  6.5 39.1 %collective-permute-start.9 = (bf16[128,384]{1,0:T(8,128)(2,1)S(1)}, bf16[128,384]{1,0:T(8,128)(2,1)S(1)}, u32[]{:S(2)}, u32[]{:S(2)}) collective-permute-start(bf16[128,384]{1,0:T(8,128)(2,1)S(1)} %slice.100), channel_id=1, source_target_pairs={{0,1},{1,0},{2,3},{3,2},{4,5},{5,4},{6,7},{7,6},{8,9},{9,8},{10,11... | collective-permute-start | bytes 294920 | tf_op jit(solution)/shard_map/ppermute | solution.py:88
  6.7 22.6 %collective-permute-start.3 = (bf16[128,384]{1,0:T(8,128)(2,1)S(1)}, bf16[128,384]{1,0:T(8,128)(2,1)S(1)}, u32[]{:S(2)}, u32[]{:S(2)}) collective-permute-start(bf16[128,384]{1,0:T(8,128)(2,1)S(1)} %slice.96), channel_id=1, source_target_pairs={{0,4},{4,0},{8,12},{12,8},{16,20},{20,16},{24,28},{28,24},{1,5},{5... | collective-permute-start | bytes 294920 | tf_op jit(solution)/shard_map/ppermute | solution.py:107
  6.8 40.5 %collective-permute-start.11 = (bf16[128,384]{1,0:T(8,128)(2,1)S(1)}, bf16[128,384]{1,0:T(8,128)(2,1)S(1)}, u32[]{:S(2)}, u32[]{:S(2)}) collective-permute-start(bf16[128,384]{1,0:T(8,128)(2,1)S(1)} %slice.96), channel_id=1, source_target_pairs={{0,2},{1,3},{2,0},{3,1},{4,6},{5,7},{6,4},{7,5},{8,10},{9,11},{10,... | collective-permute-start | bytes 294920 | tf_op jit(solution)/shard_map/ppermute | solution.py:88
  8.5 6.7 %collective-permute-start = (bf16[96,384]{1,0:T(8,128)(2,1)S(1)}, bf16[96,384]{1,0:T(8,128)(2,1)S(1)}, u32[]{:S(2)}, u32[]{:S(2)}) collective-permute-start(bf16[96,384]{1,0:T(8,128)(2,1)S(1)} %get-tuple-element.8), channel_id=1, source_target_pairs={{0,1},{1,0},{2,3},{3,2},{4,5},{5,4},{6,7},{7,6},{8,9},{9,8},{10,11... | collective-permute-start | bytes 221192 | tf_op jit(solution)/shard_map/ppermute | solution.py:79
  15.2 5.3 %collective-permute-start.1 = (bf16[96,384]{1,0:T(8,128)(2,1)S(1)}, bf16[96,384]{1,0:T(8,128)(2,1)S(1)}, u32[]{:S(2)}, u32[]{:S(2)}) collective-permute-start(bf16[96,384]{1,0:T(8,128)(2,1)S(1)} %get-tuple-element.9), channel_id=1, source_target_pairs={{0,2},{1,3},{2,0},{3,1},{4,6},{5,7},{6,4},{7,5},{8,10},{9,11},{10,... | collective-permute-start | bytes 221192 | tf_op jit(solution)/shard_map/ppermute | solution.py:79
  20.4 6.2 %collective-permute-start.2 = (bf16[96,384]{1,0:T(8,128)(2,1)S(1)}, bf16[96,384]{1,0:T(8,128)(2,1)S(1)}, u32[]{:S(2)}, u32[]{:S(2)}) collective-permute-start(bf16[96,384]{1,0:T(8,128)(2,1)S(1)} %get-tuple-element.7), channel_id=1, source_target_pairs={{0,3},{1,2},{2,1},{3,0},{4,7},{5,6},{6,5},{7,4},{8,11},{9,10},{10,... | collective-permute-start | bytes 221192 | tf_op jit(solution)/shard_map/ppermute | solution.py:79
  26.7 6.9 %collective-permute-start.6 = (bf16[288,384]{1,0:T(8,128)(2,1)S(1)}, bf16[288,384]{1,0:T(8,128)(2,1)S(1)}, u32[]{:S(2)}, u32[]{:S(2)}) collective-permute-start(bf16[288,384]{1,0:T(8,128)(2,1)S(1)} %constant_dynamic-update-slice_fusion), channel_id=1, source_target_pairs={{0,24},{4,28},{8,16},{12,20},{16,8},{20,12},{24,0},{28,4},{1,25},{... | collective-permute-start | bytes 663560 | tf_op jit(solution)/shard_map/ppermute | solution.py:94
  29.4 21.5 %collective-permute-start.18 = (bf16[256,384]{1,0:T(8,128)(2,1)S(1)}, bf16[256,384]{1,0:T(8,128)(2,1)S(1)}, u32[]{:S(2)}, u32[]{:S(2)}) collective-permute-start(bf16[256,384]{1,0:T(8,128)(2,1)S(1)} %slice.112), channel_id=1, source_target_pairs={{0,3},{1,2},{2,1},{3,0},{4,7},{5,6},{6,5},{7,4},{8,11},{9,10},{10,... | collective-permute-start | bytes 589832 | tf_op jit(solution)/shard_map/ppermute | solution.py:88
  33.6 5.9 %collective-permute-start.5 = (bf16[288,384]{1,0:T(8,128)(2,1)S(1)}, bf16[288,384]{1,0:T(8,128)(2,1)S(1)}, u32[]{:S(2)}, u32[]{:S(2)}) collective-permute-start(bf16[288,384]{1,0:T(8,128)(2,1)S(1)} %constant_dynamic-update-slice_fusion), channel_id=1, source_target_pairs={{0,16},{4,20},{8,24},{12,28},{16,0},{20,4},{24,8},{28,12},{1,17},{... | collective-permute-start | bytes 663560 | tf_op jit(solution)/shard_map/ppermute | solution.py:94
  39.6 5.9 %collective-permute-start.4 = (bf16[288,384]{1,0:T(8,128)(2,1)S(1)}, bf16[288,384]{1,0:T(8,128)(2,1)S(1)}, u32[]{:S(2)}, u32[]{:S(2)}) collective-permute-start(bf16[288,384]{1,0:T(8,128)(2,1)S(1)} %constant_dynamic-update-slice_fusion), channel_id=1, source_target_pairs={{0,8},{4,12},{8,0},{12,4},{16,24},{20,28},{24,16},{28,20},{1,9},{5... | collective-permute-start | bytes 663560 | tf_op jit(solution)/shard_map/ppermute | solution.py:94
  41.2 13.9 %collective-permute-start.20 = (bf16[256,384]{1,0:T(8,128)(2,1)S(1)}, bf16[256,384]{1,0:T(8,128)(2,1)S(1)}, u32[]{:S(2)}, u32[]{:S(2)}) collective-permute-start(bf16[256,384]{1,0:T(8,128)(2,1)S(1)} %slice.112), channel_id=1, source_target_pairs={{0,1},{1,0},{2,3},{3,2},{4,5},{5,4},{6,7},{7,6},{8,9},{9,8},{10,11... | collective-permute-start | bytes 589832 | tf_op jit(solution)/shard_map/ppermute | solution.py:88
  45.5 1.3 %collective-permute-start.8 = (bf16[128,384]{1,0:T(8,128)(2,1)S(1)}, bf16[128,384]{1,0:T(8,128)(2,1)S(1)}, u32[]{:S(2)}, u32[]{:S(2)}) collective-permute-start(bf16[128,384]{1,0:T(8,128)(2,1)S(1)} %collective-permute-done.7), channel_id=1, source_target_pairs={{0,4},{4,0},{8,12},{12,8},{16,20},{20,16},{24,28},{28,24},{1,5},{5... | collective-permute-start | bytes 294920 | tf_op jit(solution)/shard_map/ppermute | solution.py:107
  45.5 4.9 %collective-permute-start.17 = (bf16[256,384]{1,0:T(8,128)(2,1)S(1)}, bf16[256,384]{1,0:T(8,128)(2,1)S(1)}, u32[]{:S(2)}, u32[]{:S(2)}) collective-permute-start(bf16[256,384]{1,0:T(8,128)(2,1)S(1)} %slice.111), channel_id=1, source_target_pairs={{0,4},{4,0},{8,12},{12,8},{16,20},{20,16},{24,28},{28,24},{1,5},{5... | collective-permute-start | bytes 589832 | tf_op jit(solution)/shard_map/ppermute | solution.py:107
  46.8 1.3 %collective-permute-start.10 = (bf16[128,384]{1,0:T(8,128)(2,1)S(1)}, bf16[128,384]{1,0:T(8,128)(2,1)S(1)}, u32[]{:S(2)}, u32[]{:S(2)}) collective-permute-start(bf16[128,384]{1,0:T(8,128)(2,1)S(1)} %collective-permute-done.9), channel_id=1, source_target_pairs={{0,4},{4,0},{8,12},{12,8},{16,20},{20,16},{24,28},{28,24},{1,5},{5... | collective-permute-start | bytes 294920 | tf_op jit(solution)/shard_map/ppermute | solution.py:107
  47.3 12.4 %collective-permute-start.22 = (bf16[256,384]{1,0:T(8,128)(2,1)S(1)}, bf16[256,384]{1,0:T(8,128)(2,1)S(1)}, u32[]{:S(2)}, u32[]{:S(2)}) collective-permute-start(bf16[256,384]{1,0:T(8,128)(2,1)S(1)} %slice.111), channel_id=1, source_target_pairs={{0,2},{1,3},{2,0},{3,1},{4,6},{5,7},{6,4},{7,5},{8,10},{9,11},{10,... | collective-permute-start | bytes 589832 | tf_op jit(solution)/shard_map/ppermute | solution.py:88
  48.1 1.3 %collective-permute-start.12 = (bf16[128,384]{1,0:T(8,128)(2,1)S(1)}, bf16[128,384]{1,0:T(8,128)(2,1)S(1)}, u32[]{:S(2)}, u32[]{:S(2)}) collective-permute-start(bf16[128,384]{1,0:T(8,128)(2,1)S(1)} %collective-permute-done.11), channel_id=1, source_target_pairs={{0,4},{4,0},{8,12},{12,8},{16,20},{20,16},{24,28},{28,24},{1,5},{5... | collective-permute-start | bytes 294920 | tf_op jit(solution)/shard_map/ppermute | solution.py:107
  49.8 11.5 %collective-permute-start.13 = (bf16[96,256]{1,0:T(8,128)(2,1)S(1)}, bf16[96,256]{1,0:T(8,128)(2,1)S(1)}, u32[]{:S(2)}, u32[]{:S(2)}) collective-permute-start(bf16[96,256]{1,0:T(8,128)(2,1)S(1)} %get-tuple-element.32), channel_id=1, source_target_pairs={{0,0},{1,1},{2,2},{3,3},{4,5},{5,4},{6,7},{7,6},{8,8},{9,9},{10,10... | collective-permute-start | bytes 147464 | tf_op jit(solution)/shard_map/ppermute | solution.py:120
  50.9 15.6 %collective-permute-start.19 = (bf16[256,384]{1,0:T(8,128)(2,1)S(1)}, bf16[256,384]{1,0:T(8,128)(2,1)S(1)}, u32[]{:S(2)}, u32[]{:S(2)}) collective-permute-start(bf16[256,384]{1,0:T(8,128)(2,1)S(1)} %collective-permute-done.18), channel_id=1, source_target_pairs={{0,4},{4,0},{8,12},{12,8},{16,20},{20,16},{24,28},{28,24},{1,5},{5... | collective-permute-start | bytes 589832 | tf_op jit(solution)/shard_map/ppermute | solution.py:107
  55.0 11.8 %collective-permute-start.21 = (bf16[256,384]{1,0:T(8,128)(2,1)S(1)}, bf16[256,384]{1,0:T(8,128)(2,1)S(1)}, u32[]{:S(2)}, u32[]{:S(2)}) collective-permute-start(bf16[256,384]{1,0:T(8,128)(2,1)S(1)} %collective-permute-done.20), channel_id=1, source_target_pairs={{0,4},{4,0},{8,12},{12,8},{16,20},{20,16},{24,28},{28,24},{1,5},{5... | collective-permute-start | bytes 589832 | tf_op jit(solution)/shard_map/ppermute | solution.py:107
  59.7 7.7 %collective-permute-start.23 = (bf16[256,384]{1,0:T(8,128)(2,1)S(1)}, bf16[256,384]{1,0:T(8,128)(2,1)S(1)}, u32[]{:S(2)}, u32[]{:S(2)}) collective-permute-start(bf16[256,384]{1,0:T(8,128)(2,1)S(1)} %collective-permute-done.22), channel_id=1, source_target_pairs={{0,4},{4,0},{8,12},{12,8},{16,20},{20,16},{24,28},{28,24},{1,5},{5... | collective-permute-start | bytes 589832 | tf_op jit(solution)/shard_map/ppermute | solution.py:107
  59.7 4.1 %collective-permute-start.14 = (bf16[96,256]{1,0:T(8,128)(2,1)S(1)}, bf16[96,256]{1,0:T(8,128)(2,1)S(1)}, u32[]{:S(2)}, u32[]{:S(2)}) collective-permute-start(bf16[96,256]{1,0:T(8,128)(2,1)S(1)} %get-tuple-element.31), channel_id=1, source_target_pairs={{0,8},{1,9},{2,10},{3,11},{4,13},{5,12},{6,15},{7,14},{8,0},{9,1},... | collective-permute-start | bytes 147464 | tf_op jit(solution)/shard_map/ppermute | solution.py:120
  61.3 5.1 %collective-permute-start.15 = (bf16[96,256]{1,0:T(8,128)(2,1)S(1)}, bf16[96,256]{1,0:T(8,128)(2,1)S(1)}, u32[]{:S(2)}, u32[]{:S(2)}) collective-permute-start(bf16[96,256]{1,0:T(8,128)(2,1)S(1)} %get-tuple-element.30), channel_id=1, source_target_pairs={{0,16},{1,17},{2,18},{3,19},{4,21},{5,20},{6,23},{7,22},{8,24},{9,... | collective-permute-start | bytes 147464 | tf_op jit(solution)/shard_map/ppermute | solution.py:120
  63.8 5.5 %collective-permute-start.16 = (bf16[96,256]{1,0:T(8,128)(2,1)S(1)}, bf16[96,256]{1,0:T(8,128)(2,1)S(1)}, u32[]{:S(2)}, u32[]{:S(2)}) collective-permute-start(bf16[96,256]{1,0:T(8,128)(2,1)S(1)} %get-tuple-element.29), channel_id=1, source_target_pairs={{0,24},{1,25},{2,26},{3,27},{4,29},{5,28},{6,31},{7,30},{8,16},{9,... | collective-permute-start | bytes 147464 | tf_op jit(solution)/shard_map/ppermute | solution.py:120
  68.1 5.1 %collective-permute-start.26 = (bf16[96,512]{1,0:T(8,128)(2,1)S(1)}, bf16[96,512]{1,0:T(8,128)(2,1)S(1)}, u32[]{:S(2)}, u32[]{:S(2)}) collective-permute-start(bf16[96,512]{1,0:T(8,128)(2,1)S(1)} %get-tuple-element.13), channel_id=1, source_target_pairs={{0,16},{1,17},{2,18},{3,19},{4,21},{5,20},{6,23},{7,22},{8,24},{9,... | collective-permute-start | bytes 294920 | tf_op jit(solution)/shard_map/ppermute | solution.py:120
  69.3 9.9 %collective-permute-start.24 = (bf16[96,512]{1,0:T(8,128)(2,1)S(1)}, bf16[96,512]{1,0:T(8,128)(2,1)S(1)}, u32[]{:S(2)}, u32[]{:S(2)}) collective-permute-start(bf16[96,512]{1,0:T(8,128)(2,1)S(1)} %get-tuple-element.15), channel_id=1, source_target_pairs={{0,0},{1,1},{2,2},{3,3},{4,5},{5,4},{6,7},{7,6},{8,8},{9,9},{10,10... | collective-permute-start | bytes 294920 | tf_op jit(solution)/shard_map/ppermute | solution.py:120
  70.0 9.3 %collective-permute-start.25 = (bf16[96,512]{1,0:T(8,128)(2,1)S(1)}, bf16[96,512]{1,0:T(8,128)(2,1)S(1)}, u32[]{:S(2)}, u32[]{:S(2)}) collective-permute-start(bf16[96,512]{1,0:T(8,128)(2,1)S(1)} %get-tuple-element.14), channel_id=1, source_target_pairs={{0,8},{1,9},{2,10},{3,11},{4,13},{5,12},{6,15},{7,14},{8,0},{9,1},... | collective-permute-start | bytes 294920 | tf_op jit(solution)/shard_map/ppermute | solution.py:120
  71.6 7.6 %collective-permute-start.27 = (bf16[96,512]{1,0:T(8,128)(2,1)S(1)}, bf16[96,512]{1,0:T(8,128)(2,1)S(1)}, u32[]{:S(2)}, u32[]{:S(2)}) collective-permute-start(bf16[96,512]{1,0:T(8,128)(2,1)S(1)} %get-tuple-element.12), channel_id=1, source_target_pairs={{0,24},{1,25},{2,26},{3,27},{4,29},{5,28},{6,31},{7,30},{8,16},{9,... | collective-permute-start | bytes 294920 | tf_op jit(solution)/shard_map/ppermute | solution.py:120
  79.4 1.6 %collective-permute-start.28 = (bf16[4,48,768]{2,1,0:T(8,128)(2,1)S(1)}, bf16[4,48,768]{2,1,0:T(8,128)(2,1)S(1)}, u32[]{:S(2)}, u32[]{:S(2)}) collective-permute-start(bf16[4,48,768]{2,1,0:T(8,128)(2,1)S(1)} %pad_maximum_fusion.4), channel_id=1, source_target_pairs={{0,4},{4,0},{8,12},{12,8},{16,20},{20,16},{24,28},{28,24},{1,5},{5... | collective-permute-start | bytes 884744 | tf_op jit(solution)/shard_map/ppermute | solution.py:124

commit v5 on v4

--- a/solution.py
+++ b/solution.py
@@ -59,6 +59,12 @@
     return [0] + [k for k in list(range(deep - 1, 2, -1)) + [1, 2] if k < deep]
 
 
+def swap_waves(deep, chunk):
+    own, *ks = arrival_order(deep)
+    waves = [[own], ks] if chunk == 0 else [[own]] + [[k] for k in ks]
+    return [wave for wave in waves if wave]
+
+
 def paired(wide, deep, products, operator):
     points, comps, modes = products.shape
     chips, half = wide // 2, modes // 2
@@ -100,12 +106,16 @@
         weights.append(jnp.concatenate([g[k * piece : k * piece + piece] for g in gathered]))
 
     kept, passed = [], []
-    for first, end, members in chunks:
+    for c, (first, end, members) in enumerate(chunks):
         total = None
+        ours = {k: jnp.concatenate([mine[g][k] for g in members]) for k in order}
+        theirs = {}
+        for wave in swap_waves(deep, c):
+            swapped = lax.ppermute(jnp.concatenate([ours[k] for k in wave]), "gx", swap)
+            for k, part in zip(wave, jnp.split(swapped, len(wave))):
+                theirs[k] = part
         for k in order:
-            ours = jnp.concatenate([mine[g][k] for g in members])
-            theirs = lax.ppermute(ours, "gx", swap)
-            both = jnp.concatenate([ours, theirs])
+            both = jnp.concatenate([ours[k], theirs[k]])
             term = lax.dot_general(
                 weights[k], both, (((1,), (1,)), ((), ())), preferred_element_type=jnp.float32
             )

time: 82.2 us -> 69.9 us (0.85)
  waiting for transfers between devices: 35.9 us -> 28 us
  starting transfers between devices: 37.7 us -> 33.2 us
    ppermute x3, waiting for transfers between devices: 8.75 us -> 4.34 us  [paired(): gathered.append(lax.ppermute(arrived, 'gx', pairs))]
    ppermute x8 -> x6, starting transfers between devices: 5.2 us -> 1.19 us  [paired(): swapped = lax.ppermute(jnp.concatenate([ours[k] for k in wave]), 'gx', swap)]
    ppermute x1, starting transfers between devices: 0.07 us -> 3.89 us  [paired(): fetched = lax.ppermute(jnp.stack(passed), 'gx', swap)]
    ppermute x8, waiting for transfers between devices: 7.71 us -> 4.92 us  [paired(): landed = lax.ppermute(result[j], ('gx', 'gy'), pairs)]
    ppermute x3, waiting for transfers between devices: 11 us -> 13.4 us  [paired(): shares[k] = lax.ppermute(pieces[k], 'gy', [(i, i ^ k) for i in range(deep)])]
    ppermute x8 -> x6, waiting for transfers between devices: 2.25 us -> 0.02 us  [paired(): swapped = lax.ppermute(jnp.concatenate([ours[k] for k in wave]), 'gx', swap)]
    ppermute x8, starting transfers between devices: 10.8 us -> 8.62 us  [paired(): landed = lax.ppermute(result[j], ('gx', 'gy'), pairs)]
    ppermute x3, starting transfers between devices: 6.08 us -> 4.73 us  [paired(): shares[k] = lax.ppermute(pieces[k], 'gy', [(i, i ^ k) for i in range(deep)])]
  transfers between devices with their start and end apart: 29 -> 27, of which waited for: 14 -> 9; matrix products, arithmetic and copies ran while one was open for 7% -> 8% of each run, Pallas kernels for 0% -> 0%
where the time goes in v5:
time: 69.9 us; the launch traced here: 69.6 us
  starting transfers between devices  33.2 us (47%)
  waiting for transfers between devices  28 us (40%)
  local copies, waits for them, and re-layouts  3.87 us (6%)
  matrix products  2.73 us (4%)
  Pallas kernels  0.88 us (1%)
    ppermute x3, waiting for transfers between devices, paired(): shares[k] = lax.ppermute(pieces[k], 'gy', [(i, i ^ k) for i in range(deep)])  13.4 us
    ppermute x6, starting transfers between devices, paired(): lax.ppermute(halves[k % 2][a:b], 'gy', [(i, i ^ k) for i in range(deep)])  9.8 us
    ppermute x8, starting transfers between devices, paired(): landed = lax.ppermute(result[j], ('gx', 'gy'), pairs)  8.62 us
    ppermute x3, starting transfers between devices, paired(): gathered.append(lax.ppermute(arrived, 'gx', pairs))  4.94 us
    ppermute x8, waiting for transfers between devices, paired(): landed = lax.ppermute(result[j], ('gx', 'gy'), pairs)  4.92 us
    ppermute x3, starting transfers between devices, paired(): shares[k] = lax.ppermute(pieces[k], 'gy', [(i, i ^ k) for i in range(deep)])  4.73 us
    ppermute x3, waiting for transfers between devices, paired(): gathered.append(lax.ppermute(arrived, 'gx', pairs))  4.34 us
    ppermute x6, waiting for transfers between devices, paired(): lax.ppermute(halves[k % 2][a:b], 'gy', [(i, i ^ k) for i in range(deep)])  4.11 us
  transfers between devices with their start and end apart: 27, of which 9 were waited for; matrix products, arithmetic and copies ran while one was open for 8% of the time, Pallas kernels for 0%

profile of v5, /device:TPU:0, one launch (start us, length us, event | category | flops | bytes accessed | tf_op | source)
XLA Modules:
  0.0 69.6 jit_solution(1437695694853329853)
XLA Ops:
  0.0 1.1 %constant_dynamic-slice_fusion.16 = (bf16[384,3,128]{2,0,1:T(8,128)(2,1)S(1)}, bf16[384,3,128]{2,0,1:T(8,128)(2,1)S(1)}) fusion(bf16[384,3,256]{2,0,1:T(8,128)(2,1)} %param.2, s32[]{:T(128)S(6)} %select_n.77, s32[]{:T(128)S(6)} %select_n.76), kind=kLoop, calls=%fused_computation.63 | loop fusion | bytes 1179656 | tf_op jit(solution)/shard_map/dynamic_slice | solution.py:88
  1.1 0.2 copy.5
  1.3 0.6 collective-permute-start.3
  1.9 3.7 %collective-permute-start.9 = (bf16[128,384]{1,0:T(8,128)(2,1)S(1)}, bf16[128,384]{1,0:T(8,128)(2,1)S(1)}, u32[]{:S(2)}, u32[]{:S(2)}) collective-permute-start(bf16[128,384]{1,0:T(8,128)(2,1)S(1)} %slice.96), channel_id=1, source_target_pairs={{0,2},{1,3},{2,0},{3,1},{4,6},{5,7},{6,4},{7,5},{8,10},{9,11},{10,... | collective-permute-start | bytes 294920 | tf_op jit(solution)/shard_map/ppermute | solution.py:94
  5.5 0.2 copy.6
  5.8 1.6 %collective-permute-start.8 = (bf16[128,384]{1,0:T(8,128)(2,1)S(1)}, bf16[128,384]{1,0:T(8,128)(2,1)S(1)}, u32[]{:S(2)}, u32[]{:S(2)}) collective-permute-start(bf16[128,384]{1,0:T(8,128)(2,1)S(1)} %slice.100), channel_id=1, source_target_pairs={{0,1},{1,0},{2,3},{3,2},{4,5},{5,4},{6,7},{7,6},{8,9},{9,8},{10,11... | collective-permute-start | bytes 294920 | tf_op jit(solution)/shard_map/ppermute | solution.py:94
  7.4 1.0 %constant_dynamic-slice_fusion.22 = (bf16[96,384]{1,0:T(8,128)(2,1)S(1)}, bf16[96,384]{1,0:T(8,128)(2,1)S(1)}, bf16[96,384]{1,0:T(8,128)(2,1)S(1)}) fusion(bf16[1536,384]{1,0:T(8,128)(2,1)} %param.3, s32[]{:T(128)S(6)} %select_n.70, s32[]{:T(128)S(6)} %select_n.68, s32[]{:T(128)S(6)} %select_n.69), kind=kLoop, calls=%fused_computation.69 | loop fusion | bytes 442380 | tf_op jit(solution)/shard_map/dynamic_slice | solution.py:81
  8.4 1.0 %collective-permute-start = (bf16[96,384]{1,0:T(8,128)(2,1)S(1)}, bf16[96,384]{1,0:T(8,128)(2,1)S(1)}, u32[]{:S(2)}, u32[]{:S(2)}) collective-permute-start(bf16[96,384]{1,0:T(8,128)(2,1)S(1)} %get-tuple-element.8), channel_id=1, source_target_pairs={{0,1},{1,0},{2,3},{3,2},{4,5},{5,4},{6,7},{7,6},{8,9},{9,8},{10,11... | collective-permute-start | bytes 221192 | tf_op jit(solution)/shard_map/ppermute | solution.py:85
  9.5 1.0 %constant_dynamic-slice_fusion.25 = bf16[384,384]{1,0:T(8,128)(2,1)S(1)} fusion(bf16[1536,384]{1,0:T(8,128)(2,1)} %param.3, s32[]{:T(128)S(6)} %select_n.66), kind=kLoop, calls=%fused_computation.72 | loop fusion | bytes 589828 | tf_op jit(solution)/shard_map/dynamic_slice | solution.py:101
  10.5 4.9 %collective-permute-done = bf16[96,384]{1,0:T(8,128)(2,1)S(1)} collective-permute-done((bf16[96,384]{1,0:T(8,128)(2,1)S(1)}, bf16[96,384]{1,0:T(8,128)(2,1)S(1)}, u32[]{:S(2)}, u32[]{:S(2)}) %collective-permute-start) | collective-permute-done | bytes 73760 | tf_op jit(solution)/shard_map/ppermute | solution.py:85
  15.3 1.1 %collective-permute-start.1 = (bf16[96,384]{1,0:T(8,128)(2,1)S(1)}, bf16[96,384]{1,0:T(8,128)(2,1)S(1)}, u32[]{:S(2)}, u32[]{:S(2)}) collective-permute-start(bf16[96,384]{1,0:T(8,128)(2,1)S(1)} %get-tuple-element.9), channel_id=1, source_target_pairs={{0,2},{1,3},{2,0},{3,1},{4,6},{5,7},{6,4},{7,5},{8,10},{9,11},{10,... | collective-permute-start | bytes 221192 | tf_op jit(solution)/shard_map/ppermute | solution.py:85
  16.5 5.0 %collective-permute-done.1 = bf16[96,384]{1,0:T(8,128)(2,1)S(1)} collective-permute-done((bf16[96,384]{1,0:T(8,128)(2,1)S(1)}, bf16[96,384]{1,0:T(8,128)(2,1)S(1)}, u32[]{:S(2)}, u32[]{:S(2)}) %collective-permute-start.1) | collective-permute-done | bytes 73760 | tf_op jit(solution)/shard_map/ppermute | solution.py:85
  21.5 2.6 %collective-permute-start.2 = (bf16[96,384]{1,0:T(8,128)(2,1)S(1)}, bf16[96,384]{1,0:T(8,128)(2,1)S(1)}, u32[]{:S(2)}, u32[]{:S(2)}) collective-permute-start(bf16[96,384]{1,0:T(8,128)(2,1)S(1)} %get-tuple-element.7), channel_id=1, source_target_pairs={{0,3},{1,2},{2,1},{3,0},{4,7},{5,6},{6,5},{7,4},{8,11},{9,10},{10,... | collective-permute-start | bytes 221192 | tf_op jit(solution)/shard_map/ppermute | solution.py:85
  24.2 3.5 %collective-permute-done.2 = bf16[96,384]{1,0:T(8,128)(2,1)S(1)} collective-permute-done((bf16[96,384]{1,0:T(8,128)(2,1)S(1)}, bf16[96,384]{1,0:T(8,128)(2,1)S(1)}, u32[]{:S(2)}, u32[]{:S(2)}) %collective-permute-start.2) | collective-permute-done | bytes 73760 | tf_op jit(solution)/shard_map/ppermute | solution.py:85
  27.7 2.7 %collective-permute-start.16 = (bf16[256,384]{1,0:T(8,128)(2,1)S(1)}, bf16[256,384]{1,0:T(8,128)(2,1)S(1)}, u32[]{:S(2)}, u32[]{:S(2)}) collective-permute-start(bf16[256,384]{1,0:T(8,128)(2,1)S(1)} %slice.112), channel_id=1, source_target_pairs={{0,3},{1,2},{2,1},{3,0},{4,7},{5,6},{6,5},{7,4},{8,11},{9,10},{10,... | collective-permute-start | bytes 589832 | tf_op jit(solution)/shard_map/ppermute | solution.py:94
  30.4 0.3 fusion.15
  30.8 0.1 collective-permute-start.18
  30.8 1.7 %collective-permute-start.20 = (bf16[256,384]{1,0:T(8,128)(2,1)S(1)}, bf16[256,384]{1,0:T(8,128)(2,1)S(1)}, u32[]{:S(2)}, u32[]{:S(2)}) collective-permute-start(bf16[256,384]{1,0:T(8,128)(2,1)S(1)} %slice.111), channel_id=1, source_target_pairs={{0,2},{1,3},{2,0},{3,1},{4,6},{5,7},{6,4},{7,5},{8,10},{9,11},{10,... | collective-permute-start | bytes 589832 | tf_op jit(solution)/shard_map/ppermute | solution.py:94
  32.6 2.7 %collective-permute-start.6 = (bf16[288,384]{1,0:T(8,128)(2,1)S(1)}, bf16[288,384]{1,0:T(8,128)(2,1)S(1)}, u32[]{:S(2)}, u32[]{:S(2)}) collective-permute-start(bf16[288,384]{1,0:T(8,128)(2,1)S(1)} %constant_dynamic-update-slice_fusion), channel_id=1, source_target_pairs={{0,24},{4,28},{8,16},{12,20},{16,8},{20,12},{24,0},{28,4},{1,25},{... | collective-permute-start | bytes 663560 | tf_op jit(solution)/shard_map/ppermute | solution.py:100
  35.3 0.6 collective-permute-start.5
  35.9 0.4 fusion
  36.3 4.3 %collective-permute-done.6 = bf16[288,384]{1,0:T(8,128)(2,1)S(1)} collective-permute-done((bf16[288,384]{1,0:T(8,128)(2,1)S(1)}, bf16[288,384]{1,0:T(8,128)(2,1)S(1)}, u32[]{:S(2)}, u32[]{:S(2)}) %collective-permute-start.6) | collective-permute-done | bytes 221216 | tf_op jit(solution)/shard_map/ppermute | solution.py:100
  40.6 1.7 %collective-permute-start.4 = (bf16[288,384]{1,0:T(8,128)(2,1)S(1)}, bf16[288,384]{1,0:T(8,128)(2,1)S(1)}, u32[]{:S(2)}, u32[]{:S(2)}) collective-permute-start(bf16[288,384]{1,0:T(8,128)(2,1)S(1)} %constant_dynamic-update-slice_fusion), channel_id=1, source_target_pairs={{0,8},{4,12},{8,0},{12,4},{16,24},{20,28},{24,16},{28,20},{1,9},{5... | collective-permute-start | bytes 663560 | tf_op jit(solution)/shard_map/ppermute | solution.py:100
  42.3 0.1 collective-permute-start.10
  42.4 2.0 %collective-permute-done.18 = bf16[256,384]{1,0:T(8,128)(2,1)S(1)} collective-permute-done((bf16[256,384]{1,0:T(8,128)(2,1)S(1)}, bf16[256,384]{1,0:T(8,128)(2,1)S(1)}, u32[]{:S(2)}, u32[]{:S(2)}) %collective-permute-start.18) | collective-permute-done | bytes 196640 | tf_op jit(solution)/shard_map/ppermute | solution.py:94
  44.5 2.1 %collective-permute-done.20 = bf16[256,384]{1,0:T(8,128)(2,1)S(1)} collective-permute-done((bf16[256,384]{1,0:T(8,128)(2,1)S(1)}, bf16[256,384]{1,0:T(8,128)(2,1)S(1)}, u32[]{:S(2)}, u32[]{:S(2)}) %collective-permute-start.20) | collective-permute-done | bytes 196640 | tf_op jit(solution)/shard_map/ppermute | solution.py:94
  46.6 0.5 collective-permute-start.21
  47.2 0.3 fusion.19
  47.5 0.3 fusion.23
  47.9 0.3 fusion.27
  48.3 0.7 collective-permute-start.11
  48.9 1.5 %collective-permute-start.12 = (bf16[96,256]{1,0:T(8,128)(2,1)S(1)}, bf16[96,256]{1,0:T(8,128)(2,1)S(1)}, u32[]{:S(2)}, u32[]{:S(2)}) collective-permute-start(bf16[96,256]{1,0:T(8,128)(2,1)S(1)} %get-tuple-element.34), channel_id=1, source_target_pairs={{0,8},{1,9},{2,10},{3,11},{4,13},{5,12},{6,15},{7,14},{8,0},{9,1},... | collective-permute-start | bytes 147464 | tf_op jit(solution)/shard_map/ppermute | solution.py:130
  50.4 1.5 %collective-permute-start.13 = (bf16[96,256]{1,0:T(8,128)(2,1)S(1)}, bf16[96,256]{1,0:T(8,128)(2,1)S(1)}, u32[]{:S(2)}, u32[]{:S(2)}) collective-permute-start(bf16[96,256]{1,0:T(8,128)(2,1)S(1)} %get-tuple-element.33), channel_id=1, source_target_pairs={{0,16},{1,17},{2,18},{3,19},{4,21},{5,20},{6,23},{7,22},{8,24},{9,... | collective-permute-start | bytes 147464 | tf_op jit(solution)/shard_map/ppermute | solution.py:130
  51.9 0.4 convolution_add_fusion
  52.4 0.6 collective-permute-start.14
  53.0 0.4 fusion.7
  53.4 0.1 add.105
  53.6 0.4 fusion.11
  54.0 0.2 add_convert_fusion
  54.2 0.7 collective-permute-start.22
  54.9 1.5 %collective-permute-start.23 = (bf16[96,512]{1,0:T(8,128)(2,1)S(1)}, bf16[96,512]{1,0:T(8,128)(2,1)S(1)}, u32[]{:S(2)}, u32[]{:S(2)}) collective-permute-start(bf16[96,512]{1,0:T(8,128)(2,1)S(1)} %get-tuple-element.14), channel_id=1, source_target_pairs={{0,8},{1,9},{2,10},{3,11},{4,13},{5,12},{6,15},{7,14},{8,0},{9,1},... | collective-permute-start | bytes 294920 | tf_op jit(solution)/shard_map/ppermute | solution.py:130
  56.3 1.6 %collective-permute-start.24 = (bf16[96,512]{1,0:T(8,128)(2,1)S(1)}, bf16[96,512]{1,0:T(8,128)(2,1)S(1)}, u32[]{:S(2)}, u32[]{:S(2)}) collective-permute-start(bf16[96,512]{1,0:T(8,128)(2,1)S(1)} %get-tuple-element.13), channel_id=1, source_target_pairs={{0,16},{1,17},{2,18},{3,19},{4,21},{5,20},{6,23},{7,22},{8,24},{9,... | collective-permute-start | bytes 294920 | tf_op jit(solution)/shard_map/ppermute | solution.py:130
  57.9 0.6 collective-permute-start.25
  58.6 2.4 %collective-permute-done.24 = bf16[96,512]{1,0:T(8,128)(2,1)S(1)} collective-permute-done((bf16[96,512]{1,0:T(8,128)(2,1)S(1)}, bf16[96,512]{1,0:T(8,128)(2,1)S(1)}, u32[]{:S(2)}, u32[]{:S(2)}) %collective-permute-start.24) | collective-permute-done | bytes 98336 | tf_op jit(solution)/shard_map/ppermute | solution.py:130
  61.0 2.5 %collective-permute-done.25 = bf16[96,512]{1,0:T(8,128)(2,1)S(1)} collective-permute-done((bf16[96,512]{1,0:T(8,128)(2,1)S(1)}, bf16[96,512]{1,0:T(8,128)(2,1)S(1)}, u32[]{:S(2)}, u32[]{:S(2)}) %collective-permute-start.25) | collective-permute-done | bytes 98336 | tf_op jit(solution)/shard_map/ppermute | solution.py:130
  63.7 3.9 %collective-permute-start.26 = (bf16[4,48,768]{2,1,0:T(8,128)(2,1)S(1)}, bf16[4,48,768]{2,1,0:T(8,128)(2,1)S(1)}, u32[]{:S(2)}, u32[]{:S(2)}) collective-permute-start(bf16[4,48,768]{2,1,0:T(8,128)(2,1)S(1)} %pad_maximum_fusion.5), channel_id=1, source_target_pairs={{0,4},{4,0},{8,12},{12,8},{16,20},{20,16},{24,28},{28,24},{1,5},{5... | collective-permute-start | bytes 884744 | tf_op jit(solution)/shard_map/ppermute | solution.py:134
  67.6 1.2 %collective-permute-done.26.refs_8_ = bf16[4,48,768]{2,1,0:T(8,128)(2,1)S(1)} collective-permute-done((bf16[4,48,768]{2,1,0:T(8,128)(2,1)S(1)}, bf16[4,48,768]{2,1,0:T(8,128)(2,1)S(1)}, u32[]{:S(2)}, u32[]{:S(2)}) %collective-permute-start.26) | collective-permute-done | bytes 294944 | tf_op jit(solution)/shard_map/ppermute | solution.py:134
  68.8 0.9 %shard_map.28 = bf16[3,48,2048]{2,1,0:T(8,128)(2,1)} custom-call(bf16[48,256]{1,0:T(8,128)(2,1)S(1)} %get-tuple-element.45.refs_0_, bf16[48,256]{1,0:T(8,128)(2,1)S(1)} %get-tuple-element.47.refs_1_, bf16[48,256]{1,0:T(8,128)(2,1)S(1)} %get-tuple-element.49.refs_2_, bf16[48,256]{1,0:T(8,128)(2,1)S(1)} %get-tuple-element.51.refs_3_, ...), custom_call_target="tpu_custom_call" | custom-call | tf_op jit(solution)/shard_map/pallas_call | solution.py:136
  (51 shorter events, 0.7 us)
Async XLA Ops:
  1.3 26.4 %collective-permute-start.3 = (bf16[128,384]{1,0:T(8,128)(2,1)S(1)}, bf16[128,384]{1,0:T(8,128)(2,1)S(1)}, u32[]{:S(2)}, u32[]{:S(2)}) collective-permute-start(bf16[128,384]{1,0:T(8,128)(2,1)S(1)} %slice.96), channel_id=1, source_target_pairs={{0,4},{4,0},{8,12},{12,8},{16,20},{20,16},{24,28},{28,24},{1,5},{5... | collective-permute-start | bytes 294920 | tf_op jit(solution)/shard_map/ppermute | solution.py:114
  1.9 28.9 %collective-permute-start.9 = (bf16[128,384]{1,0:T(8,128)(2,1)S(1)}, bf16[128,384]{1,0:T(8,128)(2,1)S(1)}, u32[]{:S(2)}, u32[]{:S(2)}) collective-permute-start(bf16[128,384]{1,0:T(8,128)(2,1)S(1)} %slice.96), channel_id=1, source_target_pairs={{0,2},{1,3},{2,0},{3,1},{4,6},{5,7},{6,4},{7,5},{8,10},{9,11},{10,... | collective-permute-start | bytes 294920 | tf_op jit(solution)/shard_map/ppermute | solution.py:94
  5.8 25.1 %collective-permute-start.8 = (bf16[128,384]{1,0:T(8,128)(2,1)S(1)}, bf16[128,384]{1,0:T(8,128)(2,1)S(1)}, u32[]{:S(2)}, u32[]{:S(2)}) collective-permute-start(bf16[128,384]{1,0:T(8,128)(2,1)S(1)} %slice.100), channel_id=1, source_target_pairs={{0,1},{1,0},{2,3},{3,2},{4,5},{5,4},{6,7},{7,6},{8,9},{9,8},{10,11... | collective-permute-start | bytes 294920 | tf_op jit(solution)/shard_map/ppermute | solution.py:94
  7.4 25.1 %collective-permute-start.7 = (bf16[128,384]{1,0:T(8,128)(2,1)S(1)}, bf16[128,384]{1,0:T(8,128)(2,1)S(1)}, u32[]{:S(2)}, u32[]{:S(2)}) collective-permute-start(bf16[128,384]{1,0:T(8,128)(2,1)S(1)} %slice.100), channel_id=1, source_target_pairs={{0,3},{1,2},{2,1},{3,0},{4,7},{5,6},{6,5},{7,4},{8,11},{9,10},{10,... | collective-permute-start | bytes 294920 | tf_op jit(solution)/shard_map/ppermute | solution.py:94
  8.4 6.9 %collective-permute-start = (bf16[96,384]{1,0:T(8,128)(2,1)S(1)}, bf16[96,384]{1,0:T(8,128)(2,1)S(1)}, u32[]{:S(2)}, u32[]{:S(2)}) collective-permute-start(bf16[96,384]{1,0:T(8,128)(2,1)S(1)} %get-tuple-element.8), channel_id=1, source_target_pairs={{0,1},{1,0},{2,3},{3,2},{4,5},{5,4},{6,7},{7,6},{8,9},{9,8},{10,11... | collective-permute-start | bytes 221192 | tf_op jit(solution)/shard_map/ppermute | solution.py:85
  15.3 6.2 %collective-permute-start.1 = (bf16[96,384]{1,0:T(8,128)(2,1)S(1)}, bf16[96,384]{1,0:T(8,128)(2,1)S(1)}, u32[]{:S(2)}, u32[]{:S(2)}) collective-permute-start(bf16[96,384]{1,0:T(8,128)(2,1)S(1)} %get-tuple-element.9), channel_id=1, source_target_pairs={{0,2},{1,3},{2,0},{3,1},{4,6},{5,7},{6,4},{7,5},{8,10},{9,11},{10,... | collective-permute-start | bytes 221192 | tf_op jit(solution)/shard_map/ppermute | solution.py:85
  21.5 6.2 %collective-permute-start.2 = (bf16[96,384]{1,0:T(8,128)(2,1)S(1)}, bf16[96,384]{1,0:T(8,128)(2,1)S(1)}, u32[]{:S(2)}, u32[]{:S(2)}) collective-permute-start(bf16[96,384]{1,0:T(8,128)(2,1)S(1)} %get-tuple-element.7), channel_id=1, source_target_pairs={{0,3},{1,2},{2,1},{3,0},{4,7},{5,6},{6,5},{7,4},{8,11},{9,10},{10,... | collective-permute-start | bytes 221192 | tf_op jit(solution)/shard_map/ppermute | solution.py:85
  27.7 7.6 %collective-permute-start.15 = (bf16[256,384]{1,0:T(8,128)(2,1)S(1)}, bf16[256,384]{1,0:T(8,128)(2,1)S(1)}, u32[]{:S(2)}, u32[]{:S(2)}) collective-permute-start(bf16[256,384]{1,0:T(8,128)(2,1)S(1)} %slice.111), channel_id=1, source_target_pairs={{0,4},{4,0},{8,12},{12,8},{16,20},{20,16},{24,28},{28,24},{1,5},{5... | collective-permute-start | bytes 589832 | tf_op jit(solution)/shard_map/ppermute | solution.py:114
  27.7 14.6 %collective-permute-start.16 = (bf16[256,384]{1,0:T(8,128)(2,1)S(1)}, bf16[256,384]{1,0:T(8,128)(2,1)S(1)}, u32[]{:S(2)}, u32[]{:S(2)}) collective-permute-start(bf16[256,384]{1,0:T(8,128)(2,1)S(1)} %slice.112), channel_id=1, source_target_pairs={{0,3},{1,2},{2,1},{3,0},{4,7},{5,6},{6,5},{7,4},{8,11},{9,10},{10,... | collective-permute-start | bytes 589832 | tf_op jit(solution)/shard_map/ppermute | solution.py:94
  30.8 13.7 %collective-permute-start.18 = (bf16[256,384]{1,0:T(8,128)(2,1)S(1)}, bf16[256,384]{1,0:T(8,128)(2,1)S(1)}, u32[]{:S(2)}, u32[]{:S(2)}) collective-permute-start(bf16[256,384]{1,0:T(8,128)(2,1)S(1)} %slice.112), channel_id=1, source_target_pairs={{0,1},{1,0},{2,3},{3,2},{4,5},{5,4},{6,7},{7,6},{8,9},{9,8},{10,11... | collective-permute-start | bytes 589832 | tf_op jit(solution)/shard_map/ppermute | solution.py:94
  30.8 15.7 %collective-permute-start.20 = (bf16[256,384]{1,0:T(8,128)(2,1)S(1)}, bf16[256,384]{1,0:T(8,128)(2,1)S(1)}, u32[]{:S(2)}, u32[]{:S(2)}) collective-permute-start(bf16[256,384]{1,0:T(8,128)(2,1)S(1)} %slice.111), channel_id=1, source_target_pairs={{0,2},{1,3},{2,0},{3,1},{4,6},{5,7},{6,4},{7,5},{8,10},{9,11},{10,... | collective-permute-start | bytes 589832 | tf_op jit(solution)/shard_map/ppermute | solution.py:94
  32.6 8.0 %collective-permute-start.6 = (bf16[288,384]{1,0:T(8,128)(2,1)S(1)}, bf16[288,384]{1,0:T(8,128)(2,1)S(1)}, u32[]{:S(2)}, u32[]{:S(2)}) collective-permute-start(bf16[288,384]{1,0:T(8,128)(2,1)S(1)} %constant_dynamic-update-slice_fusion), channel_id=1, source_target_pairs={{0,24},{4,28},{8,16},{12,20},{16,8},{20,12},{24,0},{28,4},{1,25},{... | collective-permute-start | bytes 663560 | tf_op jit(solution)/shard_map/ppermute | solution.py:100
  35.3 11.3 %collective-permute-start.5 = (bf16[288,384]{1,0:T(8,128)(2,1)S(1)}, bf16[288,384]{1,0:T(8,128)(2,1)S(1)}, u32[]{:S(2)}, u32[]{:S(2)}) collective-permute-start(bf16[288,384]{1,0:T(8,128)(2,1)S(1)} %constant_dynamic-update-slice_fusion), channel_id=1, source_target_pairs={{0,16},{4,20},{8,24},{12,28},{16,0},{20,4},{24,8},{28,12},{1,17},{... | collective-permute-start | bytes 663560 | tf_op jit(solution)/shard_map/ppermute | solution.py:100
  40.6 6.5 %collective-permute-start.4 = (bf16[288,384]{1,0:T(8,128)(2,1)S(1)}, bf16[288,384]{1,0:T(8,128)(2,1)S(1)}, u32[]{:S(2)}, u32[]{:S(2)}) collective-permute-start(bf16[288,384]{1,0:T(8,128)(2,1)S(1)} %constant_dynamic-update-slice_fusion), channel_id=1, source_target_pairs={{0,8},{4,12},{8,0},{12,4},{16,24},{20,28},{24,16},{28,20},{1,9},{5... | collective-permute-start | bytes 663560 | tf_op jit(solution)/shard_map/ppermute | solution.py:100
  42.3 4.8 %collective-permute-start.10 = (bf16[384,384]{1,0:T(8,128)(2,1)S(1)}, bf16[384,384]{1,0:T(8,128)(2,1)S(1)}, u32[]{:S(2)}, u32[]{:S(2)}) collective-permute-start(bf16[384,384]{1,0:T(8,128)(2,1)S(1)} %pad_maximum_fusion.2), channel_id=1, source_target_pairs={{0,4},{4,0},{8,12},{12,8},{16,20},{20,16},{24,28},{28,24},{1,5},{5... | collective-permute-start | bytes 884744 | tf_op jit(solution)/shard_map/ppermute | solution.py:114
  44.4 6.0 %collective-permute-start.17 = (bf16[256,384]{1,0:T(8,128)(2,1)S(1)}, bf16[256,384]{1,0:T(8,128)(2,1)S(1)}, u32[]{:S(2)}, u32[]{:S(2)}) collective-permute-start(bf16[256,384]{1,0:T(8,128)(2,1)S(1)} %collective-permute-done.16), channel_id=1, source_target_pairs={{0,4},{4,0},{8,12},{12,8},{16,20},{20,16},{24,28},{28,24},{1,5},{5... | collective-permute-start | bytes 589832 | tf_op jit(solution)/shard_map/ppermute | solution.py:114
  46.5 5.8 %collective-permute-start.19 = (bf16[256,384]{1,0:T(8,128)(2,1)S(1)}, bf16[256,384]{1,0:T(8,128)(2,1)S(1)}, u32[]{:S(2)}, u32[]{:S(2)}) collective-permute-start(bf16[256,384]{1,0:T(8,128)(2,1)S(1)} %collective-permute-done.18), channel_id=1, source_target_pairs={{0,4},{4,0},{8,12},{12,8},{16,20},{20,16},{24,28},{28,24},{1,5},{5... | collective-permute-start | bytes 589832 | tf_op jit(solution)/shard_map/ppermute | solution.py:114
  46.6 7.0 %collective-permute-start.21 = (bf16[256,384]{1,0:T(8,128)(2,1)S(1)}, bf16[256,384]{1,0:T(8,128)(2,1)S(1)}, u32[]{:S(2)}, u32[]{:S(2)}) collective-permute-start(bf16[256,384]{1,0:T(8,128)(2,1)S(1)} %collective-permute-done.20), channel_id=1, source_target_pairs={{0,4},{4,0},{8,12},{12,8},{16,20},{20,16},{24,28},{28,24},{1,5},{5... | collective-permute-start | bytes 589832 | tf_op jit(solution)/shard_map/ppermute | solution.py:114
  48.3 6.6 %collective-permute-start.11 = (bf16[96,256]{1,0:T(8,128)(2,1)S(1)}, bf16[96,256]{1,0:T(8,128)(2,1)S(1)}, u32[]{:S(2)}, u32[]{:S(2)}) collective-permute-start(bf16[96,256]{1,0:T(8,128)(2,1)S(1)} %get-tuple-element.35), channel_id=1, source_target_pairs={{0,0},{1,1},{2,2},{3,3},{4,5},{5,4},{6,7},{7,6},{8,8},{9,9},{10,10... | collective-permute-start | bytes 147464 | tf_op jit(solution)/shard_map/ppermute | solution.py:130
  48.9 7.4 %collective-permute-start.12 = (bf16[96,256]{1,0:T(8,128)(2,1)S(1)}, bf16[96,256]{1,0:T(8,128)(2,1)S(1)}, u32[]{:S(2)}, u32[]{:S(2)}) collective-permute-start(bf16[96,256]{1,0:T(8,128)(2,1)S(1)} %get-tuple-element.34), channel_id=1, source_target_pairs={{0,8},{1,9},{2,10},{3,11},{4,13},{5,12},{6,15},{7,14},{8,0},{9,1},... | collective-permute-start | bytes 147464 | tf_op jit(solution)/shard_map/ppermute | solution.py:130
  50.4 7.5 %collective-permute-start.13 = (bf16[96,256]{1,0:T(8,128)(2,1)S(1)}, bf16[96,256]{1,0:T(8,128)(2,1)S(1)}, u32[]{:S(2)}, u32[]{:S(2)}) collective-permute-start(bf16[96,256]{1,0:T(8,128)(2,1)S(1)} %get-tuple-element.33), channel_id=1, source_target_pairs={{0,16},{1,17},{2,18},{3,19},{4,21},{5,20},{6,23},{7,22},{8,24},{9,... | collective-permute-start | bytes 147464 | tf_op jit(solution)/shard_map/ppermute | solution.py:130
  52.4 6.2 %collective-permute-start.14 = (bf16[96,256]{1,0:T(8,128)(2,1)S(1)}, bf16[96,256]{1,0:T(8,128)(2,1)S(1)}, u32[]{:S(2)}, u32[]{:S(2)}) collective-permute-start(bf16[96,256]{1,0:T(8,128)(2,1)S(1)} %get-tuple-element.32), channel_id=1, source_target_pairs={{0,24},{1,25},{2,26},{3,27},{4,29},{5,28},{6,31},{7,30},{8,16},{9,... | collective-permute-start | bytes 147464 | tf_op jit(solution)/shard_map/ppermute | solution.py:130
  54.2 9.4 %collective-permute-start.22 = (bf16[96,512]{1,0:T(8,128)(2,1)S(1)}, bf16[96,512]{1,0:T(8,128)(2,1)S(1)}, u32[]{:S(2)}, u32[]{:S(2)}) collective-permute-start(bf16[96,512]{1,0:T(8,128)(2,1)S(1)} %get-tuple-element.15), channel_id=1, source_target_pairs={{0,0},{1,1},{2,2},{3,3},{4,5},{5,4},{6,7},{7,6},{8,8},{9,9},{10,10... | collective-permute-start | bytes 294920 | tf_op jit(solution)/shard_map/ppermute | solution.py:130
  54.9 8.7 %collective-permute-start.23 = (bf16[96,512]{1,0:T(8,128)(2,1)S(1)}, bf16[96,512]{1,0:T(8,128)(2,1)S(1)}, u32[]{:S(2)}, u32[]{:S(2)}) collective-permute-start(bf16[96,512]{1,0:T(8,128)(2,1)S(1)} %get-tuple-element.14), channel_id=1, source_target_pairs={{0,8},{1,9},{2,10},{3,11},{4,13},{5,12},{6,15},{7,14},{8,0},{9,1},... | collective-permute-start | bytes 294920 | tf_op jit(solution)/shard_map/ppermute | solution.py:130
  56.3 4.7 %collective-permute-start.24 = (bf16[96,512]{1,0:T(8,128)(2,1)S(1)}, bf16[96,512]{1,0:T(8,128)(2,1)S(1)}, u32[]{:S(2)}, u32[]{:S(2)}) collective-permute-start(bf16[96,512]{1,0:T(8,128)(2,1)S(1)} %get-tuple-element.13), channel_id=1, source_target_pairs={{0,16},{1,17},{2,18},{3,19},{4,21},{5,20},{6,23},{7,22},{8,24},{9,... | collective-permute-start | bytes 294920 | tf_op jit(solution)/shard_map/ppermute | solution.py:130
  57.9 5.6 %collective-permute-start.25 = (bf16[96,512]{1,0:T(8,128)(2,1)S(1)}, bf16[96,512]{1,0:T(8,128)(2,1)S(1)}, u32[]{:S(2)}, u32[]{:S(2)}) collective-permute-start(bf16[96,512]{1,0:T(8,128)(2,1)S(1)} %get-tuple-element.12), channel_id=1, source_target_pairs={{0,24},{1,25},{2,26},{3,27},{4,29},{5,28},{6,31},{7,30},{8,16},{9,... | collective-permute-start | bytes 294920 | tf_op jit(solution)/shard_map/ppermute | solution.py:130
  63.7 5.1 %collective-permute-start.26 = (bf16[4,48,768]{2,1,0:T(8,128)(2,1)S(1)}, bf16[4,48,768]{2,1,0:T(8,128)(2,1)S(1)}, u32[]{:S(2)}, u32[]{:S(2)}) collective-permute-start(bf16[4,48,768]{2,1,0:T(8,128)(2,1)S(1)} %pad_maximum_fusion.5), channel_id=1, source_target_pairs={{0,4},{4,0},{8,12},{12,8},{16,20},{20,16},{24,28},{28,24},{1,5},{5... | collective-permute-start | bytes 884744 | tf_op jit(solution)/shard_map/ppermute | solution.py:134
